TPU v7x, 32 devices: a whole 2x2x4 slice. The times are simulated.
32 devices in a mesh: dp: 4 (over z), tensor: 8 (over y, x, core).
Axes of the slice: x: 2, y: 2, z: 4, core: 2. Of those that a mesh axis runs over, the one named last changes fastest.
Arguments:
- embed_rows: bfloat16 [98304, 512], P('tensor', 'dp'), may hold values from -6 to 6
- head_rows: bfloat16 [98304, 512], P('tensor', 'dp'), may hold values from -6 to 6
- row_offsets: int32 [2, 9], replicated, may hold values from -2047 to 67583, as said below
- slot_table: int32 [1024], replicated, may hold values from 0 to 1023, as said below
- probe: bfloat16 [512, 1024], replicated, may hold values from -0.25 to 0.25
Outputs:
- stored: bfloat16 [1024, 128, 512], P(('dp', 'tensor'))
- sketch: float32 [1024, 128, 1024], P(('dp', 'tensor'))
Inputs may be any that keep to these rules, and one draw needn't show every extreme that they name: row_offsets[m, 8] is row_offsets[m, 0] + 65536; every entry row_offsets[m, t] with t < 8 lies strictly within 2048 rows of t * 8192, and the distance 8192 // 4 - 1 is reached above and below among ranks 1 onward in every row of every draw; row_offsets[m, 0] is never 0, above 0 for one matrix and below 0 for the other. `slot_table`: A permutation of the 1024 block numbers. Devices along dp+tensor write 32 consecutive slots each; among one device's slots exactly 4 blocks come from each aligned range of 8192 vocabulary rows (rows t * 8192 onward of either matrix, both matrices together).
All inputs are finite; a program needn't handle non-finite values.
Results may differ from a plain program's by a relative error of at most 0.001.
Values may be sent and summed in bfloat16 or wider, within the bound.
No kernel may reach another device: no remote copies, remote signals or barrier semaphores. Data moves between devices by JAX's collectives and lax.ppermute only.
A program may use at most 64 MiB of HBM per device.

v0:
```python
import jax
import jax.numpy as jnp
from jax import lax
from jax.sharding import PartitionSpec as P

R = 8192
BLOCK = 128


def from_behind(block, axis, distance):
    devices = range(lax.axis_size(axis))
    route = [((i - distance) % len(devices), i) for i in devices]
    return lax.ppermute(block, axis, route)


def shards(embed_rows, head_rows, row_offsets, slot_table, probe):
    n_tensor = lax.axis_size("tensor")
    n_data = lax.axis_size("dp")
    my_tensor = lax.axis_index("tensor")
    my_data = lax.axis_index("dp")
    quarter = R // 4
    height = embed_rows.shape[0]
    col_width = embed_rows.shape[1]
    buffers = [embed_rows, head_rows]
    own_start = row_offsets[:, my_tensor]
    next_start = row_offsets[:, my_tensor + 1]
    lead_part = jnp.stack([embed_rows[:quarter], head_rows[:quarter]])
    tail_begin = jnp.clip((my_tensor + 1) * R - own_start, 0, height - quarter)
    trail_part = jnp.stack(
        [lax.dynamic_slice_in_dim(buffers[m], tail_begin[m], quarter, 0) for m in range(2)]
    )
    from_right = from_behind(lead_part, "tensor", -1)
    from_left = from_behind(trail_part, "tensor", 1)
    local_row = jnp.arange(R, dtype=jnp.int32)[:, None]
    filler = jnp.zeros((R - quarter, col_width), embed_rows.dtype)
    aligned_list = []
    for m in range(2):
        extended = jnp.concatenate([from_left[m], buffers[m], from_right[m]], axis=0)
        before = own_start[m] - my_tensor * R
        after = next_start[m] - my_tensor * R
        middle = lax.dynamic_slice_in_dim(extended, quarter - before, R, 0)
        beyond = lax.dynamic_slice_in_dim(extended, quarter + height - after, R, 0)
        leading = jnp.concatenate([from_left[m], filler], axis=0)
        aligned_list.append(
            jnp.where(local_row < before, leading, jnp.where(local_row < after, middle, beyond))
        )
    aligned = jnp.stack(aligned_list)
    blocks = aligned.reshape(2 * (R // BLOCK), BLOCK, col_width)
    devices = n_tensor * n_data
    per_rank = R // BLOCK
    total_blocks = per_rank * n_tensor
    slot_count = 2 * total_blocks // devices
    max_from = slot_count // n_tensor
    slot_grid = slot_table.reshape(devices, slot_count)
    source = slot_grid % total_blocks // per_rank
    local_block = slot_grid // total_blocks * per_rank + slot_grid % per_rank
    from_me = source == my_tensor
    rank_order = jnp.cumsum(from_me.astype(jnp.int32), axis=1) - 1
    slot_index = jnp.arange(max_from, dtype=jnp.int32)
    select = from_me[:, None, :] & (rank_order[:, None, :] == slot_index[None, :, None])
    picked = jnp.sum(jnp.where(select, local_block[:, None, :], 0), axis=2).reshape(-1)
    outgoing = blocks[picked]
    incoming = lax.all_to_all(outgoing, ("dp", "tensor"), split_axis=0, concat_axis=0, tiled=True)
    writer = my_data * n_tensor + my_tensor
    my_source = source[writer]
    slot_range = jnp.arange(slot_count, dtype=jnp.int32)
    earlier = (my_source[None, :] == my_source[:, None]) & (
        slot_range[None, :] < slot_range[:, None]
    )
    rank_within = jnp.sum(earlier.astype(jnp.int32), axis=1)
    data_range = jnp.arange(n_data, dtype=jnp.int32)
    position = (data_range[None, :] * n_tensor + my_source[:, None]) * max_from + rank_within[
        :, None
    ]
    gathered = incoming[position]
    stored = gathered.transpose(0, 2, 1, 3).reshape(slot_count, BLOCK, n_data * col_width)
    sketch = jnp.dot(
        stored.reshape(slot_count * BLOCK, n_data * col_width),
        probe,
        preferred_element_type=jnp.float32,
    ).reshape(slot_count, BLOCK, probe.shape[1])
    return (stored, sketch)


def solution(mesh):
    return jax.shard_map(
        shards,
        mesh=mesh,
        in_specs=(P("tensor", "dp"), P("tensor", "dp"), P(), P(), P()),
        out_specs=(P(("dp", "tensor"), None, None), P(("dp", "tensor"), None, None)),
        check_vma=False,
    )
```

profile of v0, /device:TPU:0, one launch (start us, length us, event | category | flops | bytes accessed | tf_op | source)
XLA Modules:
  0.0 208.2 jit_solution(8664068044040684529)
XLA Ops:
  0.7 0.9 subtract_clamp_fusion
  1.5 0.5 fusion.16
  5.9 1.8 dynamic-slice_bitcast_fusion
  7.7 1.1 pad_maximum_fusion.4
  8.8 3.4 %collective-permute-start.1 = (bf16[2,2048,128]{2,1,0:T(8,128)(2,1)}, bf16[2,2048,128]{2,1,0:T(8,128)(2,1)S(1)}, u32[]{:S(2)}, u32[]{:S(2)}) collective-permute-start(bf16[2,2048,128]{2,1,0:T(8,128)(2,1)} %pad_maximum_fusion.4), channel_id=1, source_target_pairs={{1,0},{2,1},{3,2},{4,3},{5,4},{6,5},{7,6},{0,7},{9,8},{10,9},{11,1... | collective-permute-start | bytes 3145736 | tf_op jit(solution)/shard_map/ppermute | solution.py:13
  12.2 1.1 pad_maximum_fusion.3
  13.2 0.6 fusion.14
  16.5 0.2 reduce_window_sum.11
  16.7 0.1 select_reduce_fusion
  17.2 18.8 %collective-permute-done.1 = bf16[2,2048,128]{2,1,0:T(8,128)(2,1)S(1)} collective-permute-done((bf16[2,2048,128]{2,1,0:T(8,128)(2,1)}, bf16[2,2048,128]{2,1,0:T(8,128)(2,1)S(1)}, u32[]{:S(2)}, u32[]{:S(2)}) %collective-permute-start.1) | collective-permute-done | bytes 1048608 | tf_op jit(solution)/shard_map/ppermute | solution.py:13
  36.0 0.9 collective-permute-done
  37.0 13.4 %pad_maximum_fusion = bf16[16384,128]{1,0:T(8,128)(2,1)S(1)} fusion(bf16[2048,128]{1,0:T(8,128)(2,1)S(1)} %get-tuple-element.17, bf16[12288,128]{1,0:T(8,128)(2,1)S(1)} %copy-done.1, bf16[2048,128]{1,0:T(8,128)(2,1)S(1)} %get-tuple-element.15), kind=kLoop, calls=%fused_computation.2 | loop fusion | flops 12582912 | bytes 8388608 | tf_op jit(solution)/shard_map/concatenate | solution.py:38
  50.5 13.6 %pad_maximum_fusion.1 = bf16[16384,128]{1,0:T(8,128)(2,1)S(1)} fusion(bf16[2048,128]{1,0:T(8,128)(2,1)S(1)} %get-tuple-element.18, bf16[12288,128]{1,0:T(8,128)(2,1)S(1)} %copy-done.2, bf16[2048,128]{1,0:T(8,128)(2,1)S(1)} %get-tuple-element.16), kind=kLoop, calls=%fused_computation.3 | loop fusion | flops 12582912 | bytes 8388608 | tf_op jit(solution)/shard_map/concatenate | solution.py:38
  64.1 4.2 %select_bitcast_fusion.1 = bf16[1,8192,128]{2,1,0:T(8,128)(2,1)S(1)} fusion(bf16[16384,128]{1,0:T(8,128)(2,1)S(1)} %pad_maximum_fusion, s32[]{:T(128)S(6)} %select_n.112, s32[]{:T(128)S(6)} %select_n.111, bf16[2048,128]{1,0:T(8,128)(2,1)S(1)} %get-tuple-element.15, pred[8192]{0:T(1024)(128)(4,1)S(1)} %iota_compare_fusion.3, ...), kind=kLoop, calls=%fused_computation.6 | loop fusion | flops 2097152 | bytes 6832136 | tf_op jit(solution)/shard_map/stack | solution.py:47
  68.3 4.2 %select_bitcast_fusion = bf16[1,8192,128]{2,1,0:T(8,128)(2,1)S(1)} fusion(bf16[16384,128]{1,0:T(8,128)(2,1)S(1)} %pad_maximum_fusion.1, s32[]{:T(128)S(6)} %select_n.116, s32[]{:T(128)S(6)} %select_n.115, bf16[2048,128]{1,0:T(8,128)(2,1)S(1)} %get-tuple-element.16, pred[8192]{0:T(1024)(128)(4,1)S(1)} %iota_compare_fusion.1, ...), kind=kLoop, calls=%fused_computation.5 | loop fusion | flops 2097152 | bytes 6832136 | tf_op jit(solution)/shard_map/stack | solution.py:47
  72.5 2.4 %pad_maximum_fusion.2 = bf16[2,8192,128]{2,1,0:T(8,128)(2,1)} fusion(bf16[1,8192,128]{2,1,0:T(8,128)(2,1)S(1)} %select_bitcast_fusion, bf16[1,8192,128]{2,1,0:T(8,128)(2,1)S(1)} %select_bitcast_fusion.1), kind=kLoop, calls=%fused_computation.4 | loop fusion | flops 2097152 | bytes 8388608 | tf_op jit(solution)/shard_map/stack | solution.py:47
  74.9 5.3 %gather_fusion = bf16[128,128,128]{2,1,0:T(8,128)(2,1)} fusion(bf16[128,128,128]{2,1,0:T(8,128)(2,1)} %bitcast.43, s32[1024]{0:T(1024)S(1)} %pad_clamp_fusion.1), kind=kCustom, calls=%fused_computation | custom fusion | bytes 8389120 | tf_op jit(solution)/shard_map/gather | solution.py:62
  80.2 5.5 %all-to-all-start = ((bf16[128,128,128]{2,1,0:T(8,128)(2,1)}), bf16[128,128,128]{2,1,0:T(8,128)(2,1)}, u32[]{:S(2)}, u32[]{:S(2)}) async-start(bf16[128,128,128]{2,1,0:T(8,128)(2,1)} %gather_fusion), calls=%async_computation | async-start | bytes 8388608 | tf_op jit(solution)/shard_map/all_to_all | solution.py:63
  85.8 0.2 convert_reduce_fusion
  86.2 93.3 %all-to-all-done = bf16[128,128,128]{2,1,0:T(8,128)(2,1)} async-done(((bf16[128,128,128]{2,1,0:T(8,128)(2,1)}), bf16[128,128,128]{2,1,0:T(8,128)(2,1)}, u32[]{:S(2)}, u32[]{:S(2)}) %all-to-all-start) | async-done | bytes 4194336 | tf_op jit(solution)/shard_map/all_to_all | solution.py:63
  179.4 5.3 %gather_fusion.1 = bf16[128,128,128]{2,1,0:T(8,128)(2,1)} fusion(bf16[128,128,128]{2,1,0:T(8,128)(2,1)} %all-to-all-done, s32[1024]{0:T(1024)S(1)} %pad_clamp_fusion), kind=kCustom, calls=%fused_computation.1 | custom fusion | bytes 8389120 | tf_op jit(solution)/shard_map/gather | solution.py:75
  184.7 6.4 %copy.11 = bf16[32,128,4,128]{1,3,2,0:T(8,128)(2,1)} copy(bf16[32,128,4,128]{3,1,2,0:T(8,128)(2,1)} %bitcast.44) | data formatting | bytes 8388608 | tf_op jit(solution)/shard_map/transpose | solution.py:76
  191.1 6.4 %copy.13 = bf16[32,128,512]{2,1,0:T(8,128)(2,1)} copy(bf16[32,128,512]{1,2,0:T(8,128)(2,1)} %bitcast.41) | data formatting | bytes 8388608
  197.5 10.7 %fusion = f32[32,128,1024]{2,1,0:T(8,128)} fusion(bf16[32,128,512]{1,2,0:T(8,128)(2,1)} %bitcast.42, bf16[512,1024]{1,0:T(8,128)(2,1)S(1)} %copy-done), kind=kOutput, calls=%fused_computation.9 | convolution fusion | flops 4294967296 | bytes 22020096 | tf_op jit(solution)/shard_map/dot_general | solution.py:77
  (27 shorter events, 0.8 us)
Async XLA Ops:
  0.6 196.9 %copy-start = (bf16[512,1024]{1,0:T(8,128)(2,1)S(1)}, bf16[512,1024]{1,0:T(8,128)(2,1)}, u32[]{:S(2)}) copy-start(bf16[512,1024]{1,0:T(8,128)(2,1)} %param.9) | copy-start | bytes 3145732
  5.9 10.4 %copy-start.3 = (s32[1024]{0:T(1024)S(1)}, s32[1024]{0:T(1024)}, u32[]{:S(2)}) copy-start(s32[1024]{0:T(1024)} %param.8) | copy-start | bytes 12292
  8.8 27.1 %collective-permute-start.1 = (bf16[2,2048,128]{2,1,0:T(8,128)(2,1)}, bf16[2,2048,128]{2,1,0:T(8,128)(2,1)S(1)}, u32[]{:S(2)}, u32[]{:S(2)}) collective-permute-start(bf16[2,2048,128]{2,1,0:T(8,128)(2,1)} %pad_maximum_fusion.4), channel_id=1, source_target_pairs={{1,0},{2,1},{3,2},{4,3},{5,4},{6,5},{7,6},{0,7},{9,8},{10,9},{11,1... | collective-permute-start | bytes 3145736 | tf_op jit(solution)/shard_map/ppermute | solution.py:13
  13.2 23.7 %collective-permute-start = (bf16[2,2048,128]{2,1,0:T(8,128)(2,1)}, bf16[2,2048,128]{2,1,0:T(8,128)(2,1)S(1)}, u32[]{:S(2)}, u32[]{:S(2)}) collective-permute-start(bf16[2,2048,128]{2,1,0:T(8,128)(2,1)} %pad_maximum_fusion.3), channel_id=1, source_target_pairs={{7,0},{0,1},{1,2},{2,3},{3,4},{4,5},{5,6},{6,7},{15,8},{8,9},{9,10... | collective-permute-start | bytes 3145736 | tf_op jit(solution)/shard_map/ppermute | solution.py:13
  17.1 20.0 %copy-start.1 = (bf16[12288,128]{1,0:T(8,128)(2,1)S(1)}, bf16[12288,128]{1,0:T(8,128)(2,1)}, u32[]{:S(2)}) copy-start(bf16[12288,128]{1,0:T(8,128)(2,1)} %param.5) | copy-start | bytes 9437188
  37.0 13.4 %copy-start.2 = (bf16[12288,128]{1,0:T(8,128)(2,1)S(1)}, bf16[12288,128]{1,0:T(8,128)(2,1)}, u32[]{:S(2)}) copy-start(bf16[12288,128]{1,0:T(8,128)(2,1)} %param.6) | copy-start | bytes 9437188
  80.2 99.2 %all-to-all-start = ((bf16[128,128,128]{2,1,0:T(8,128)(2,1)}), bf16[128,128,128]{2,1,0:T(8,128)(2,1)}, u32[]{:S(2)}, u32[]{:S(2)}) async-start(bf16[128,128,128]{2,1,0:T(8,128)(2,1)} %gather_fusion), calls=%async_computation | async-start | bytes 8388608 | tf_op jit(solution)/shard_map/all_to_all | solution.py:63
where the time goes:
time: 209 us; the launch traced here: 208 us
  waiting for transfers between devices  113 us (54%)
  other arithmetic  41.5 us (20%)
  local copies, waits for them, and re-layouts  26.9 us (13%)
  matrix products  10.7 us (5%)
  starting transfers between devices  8.89 us (4%)
  between operations  7.29 us (3%)
    all_to_all x1, waiting for transfers between devices, shards(): lax.all_to_all(outgoing, ('dp', 'tensor'), split_axis=0, concat_axis=0, t...  93.3 us
    concatenate x2, other arithmetic, shards(): jnp.concatenate([from_left[m], buffers[m], from_right[m]], axis=0)  27 us
    ppermute x2, waiting for transfers between devices, from_behind(): return lax.ppermute(block, axis, route)  19.7 us
    another operation x3, other arithmetic, shards(): aligned = jnp.stack(aligned_list)  10.8 us
    dot_general x1, matrix products, shards(): jnp.dot(stored.reshape(slot_count * BLOCK, n_data * col_width), probe, pr...  10.7 us
    unnamed x9, local copies, waits for them, and re-layouts  6.44 us
    transpose x1, local copies, waits for them, and re-layouts, shards(): gathered.transpose(0, 2, 1, 3)  6.41 us
    all_to_all x1, starting transfers between devices, shards(): lax.all_to_all(outgoing, ('dp', 'tensor'), split_axis=0, concat_axis=0, t...  5.53 us
  transfers between devices with their start and end apart: 3, of which 3 were waited for; matrix products, arithmetic and copies ran while one was open for 1% of the time, Pallas kernels for 0%

commit v1 on v0

v1 whole, which is shorter than its diff:
```python
import functools

import jax
import jax.numpy as jnp
from jax import lax
from jax.experimental import pallas as pl
from jax.experimental.pallas import tpu as pltpu
from jax.sharding import PartitionSpec as P

R = 8192
BLOCK = 128
ALIGN = 16


def from_behind(block, axis, distance):
    devices = range(lax.axis_size(axis))
    route = [((i - distance) % len(devices), i) for i in devices]
    return lax.ppermute(block, axis, route)


def any_space():
    return pl.BlockSpec(memory_space=pl.ANY)


def edges_kernel(starts, embed, head, lead_out, trail_out, rows, wide, sems):
    quarter = lead_out.shape[1]
    raws = [embed, head]
    copies = []
    for m in range(2):
        first = starts[2 + m] // ALIGN * ALIGN
        window = pl.ds(pl.multiple_of(first, ALIGN), quarter + ALIGN)
        lead = pltpu.make_async_copy(
            raws[m].at[pl.ds(0, quarter)], rows.at[2 * m, pl.ds(0, quarter)], sems.at[2 * m]
        )
        trail = pltpu.make_async_copy(raws[m].at[window], rows.at[2 * m + 1], sems.at[2 * m + 1])
        lead.start()
        trail.start()
        copies.append((lead, trail))
    for m in range(2):
        lead, trail = copies[m]
        lead.wait()
        count = starts[m]

        def widen_lead(i, _):
            at = pl.multiple_of(i * BLOCK, BLOCK)
            wide[pl.ds(quarter + at, BLOCK), :] = rows[2 * m, pl.ds(at, BLOCK), :].astype(jnp.float32)
            return _

        lax.fori_loop(0, quarter // BLOCK, widen_lead, 0)

        def put_lead(i, _):
            at = pl.multiple_of(i * BLOCK, BLOCK)
            lead_out[m, pl.ds(at, BLOCK), :] = wide[pl.ds(count + at, BLOCK), :].astype(jnp.bfloat16)
            return _

        lax.fori_loop(0, quarter // BLOCK, put_lead, 0)
        trail.wait()
        shift = starts[2 + m] % ALIGN

        def widen_trail(i, _):
            at = pl.multiple_of(i * BLOCK, BLOCK)
            wide[pl.ds(at, BLOCK), :] = rows[2 * m + 1, pl.ds(at, BLOCK), :].astype(jnp.float32)
            return _

        lax.fori_loop(0, quarter // BLOCK, widen_trail, 0)
        wide[pl.ds(quarter, ALIGN), :] = rows[2 * m + 1, pl.ds(quarter, ALIGN), :].astype(jnp.float32)

        def put_trail(i, _):
            at = pl.multiple_of(i * BLOCK, BLOCK)
            trail_out[m, pl.ds(at, BLOCK), :] = wide[pl.ds(shift + at, BLOCK), :].astype(jnp.bfloat16)
            return _

        lax.fori_loop(0, quarter // BLOCK, put_trail, 0)


def cut_edges(embed, head, n_lead, tail_begin, quarter):
    width = embed.shape[1]
    starts = jnp.concatenate([n_lead, tail_begin])
    shape = jax.ShapeDtypeStruct((2, quarter, width), embed.dtype)
    return pl.pallas_call(
        edges_kernel,
        out_shape=(shape, shape),
        in_specs=[pl.BlockSpec(memory_space=pltpu.SMEM), any_space(), any_space()],
        out_specs=[pl.BlockSpec(memory_space=pltpu.VMEM)] * 2,
        scratch_shapes=[
            pltpu.VMEM((4, quarter + ALIGN, width), embed.dtype),
            pltpu.VMEM((2 * quarter, width), jnp.float32),
            pltpu.SemaphoreType.DMA((4,)),
        ],
    )(starts, embed, head)


def pack_kernel(picked, before, embed, head, *refs):
    outs, (rows, wide, sems) = refs[:-3], refs[-3:]
    height = embed.shape[0]
    per_rank = R // BLOCK
    copies = []
    for m, raw in enumerate([embed, head]):
        copy = pltpu.make_async_copy(
            raw, rows.at[pl.ds(BLOCK + m * height, height)], sems.at[m]
        )
        copy.start()
        copies.append(copy)
    for copy in copies:
        copy.wait()
    per_piece = outs[0].shape[0]
    for c, out in enumerate(outs):

        def body(d, _):
            block = picked[c * per_piece + d]
            m = block // per_rank
            start = block % per_rank * BLOCK - before[m]
            start = jnp.maximum(start + BLOCK, 0) + m * height
            first = pl.multiple_of(start // ALIGN * ALIGN, ALIGN)
            slot = lax.rem(d, 2)
            wide[slot] = rows[pl.ds(first, BLOCK + ALIGN), :].astype(jnp.float32)
            out[d] = wide[slot, pl.ds(start - first, BLOCK), :].astype(jnp.bfloat16)
            return _

        lax.fori_loop(0, per_piece, body, 0)


def pack_local(picked, before, embed, head, pieces, per_piece):
    height, width = embed.shape
    shape = jax.ShapeDtypeStruct((per_piece, BLOCK, width), embed.dtype)
    smem = pl.BlockSpec(memory_space=pltpu.SMEM)
    return pl.pallas_call(
        pack_kernel,
        out_shape=[shape] * pieces,
        in_specs=[smem, smem, any_space(), any_space()],
        out_specs=[pl.BlockSpec(memory_space=pltpu.VMEM)] * pieces,
        scratch_shapes=[
            pltpu.VMEM((BLOCK + 2 * height, width), embed.dtype),
            pltpu.VMEM((2, BLOCK + ALIGN, width), jnp.float32),
            pltpu.SemaphoreType.DMA((2,)),
        ],
        cost_estimate=pl.CostEstimate(flops=4_000_000_000, bytes_accessed=10_000_000, transcendentals=0),
    )(picked, before, embed, head)


def overlay_kernel(picked, before, after, packed, left, right, out):
    per_rank = R // BLOCK
    quarter = left.shape[1]

    def body(d, _):
        block = picked[d]
        m = block // per_rank
        first = block % per_rank * BLOCK
        out[d] = packed[d]
        row = first + lax.broadcasted_iota(jnp.int32, (BLOCK, 1), 0)

        @pl.when(first < before[m])
        def _left():
            at = pl.multiple_of(first, BLOCK)
            out[d] = jnp.where(row < before[m], left[m, pl.ds(at, BLOCK), :], out[d])

        @pl.when(first + BLOCK > after[m])
        def _right():
            at = pl.multiple_of(first - (R - quarter), BLOCK)
            out[d] = jnp.where(row >= after[m], right[m, pl.ds(at, BLOCK), :], out[d])

        return _

    lax.fori_loop(0, packed.shape[0], body, 0)


def overlay(picked, before, after, packed, left, right):
    smem = pl.BlockSpec(memory_space=pltpu.SMEM)
    vmem = pl.BlockSpec(memory_space=pltpu.VMEM)
    return pl.pallas_call(
        overlay_kernel,
        out_shape=jax.ShapeDtypeStruct(packed.shape, packed.dtype),
        in_specs=[smem] * 3 + [vmem] * 3,
        out_specs=vmem,
        cost_estimate=pl.CostEstimate(flops=1_000_000_000, bytes_accessed=4_000_000, transcendentals=0),
    )(picked, before, after, packed, left, right)


def store_kernel(position, incoming, probe, *refs):
    stored, sketch = refs[-2:]
    n_data, width = incoming.shape[0], incoming.shape[3]
    for z in range(n_data):
        stored[0, :, z * width : (z + 1) * width] = incoming[z, 0]
    sketch[0] = jnp.dot(stored[0], probe[...], preferred_element_type=jnp.float32)


def store_piece(position, incoming, probe, slot_count, previous):
    n_data, n_tensor, _, width = incoming.shape
    columns = n_data * width
    sketch_width = probe.shape[1]
    out_shape = [
        jax.ShapeDtypeStruct((slot_count, BLOCK, columns), incoming.dtype),
        jax.ShapeDtypeStruct((slot_count, BLOCK, sketch_width), jnp.float32),
    ]
    held = [] if previous is None else list(previous)
    return pl.pallas_call(
        store_kernel,
        out_shape=out_shape,
        grid_spec=pltpu.PrefetchScalarGridSpec(
            num_scalar_prefetch=1,
            grid=(n_tensor,),
            in_specs=[
                pl.BlockSpec((n_data, 1, BLOCK, width), lambda i, p: (0, i, 0, 0)),
                pl.BlockSpec((columns, sketch_width), lambda i, p: (0, 0)),
            ]
            + [any_space() for _ in held],
            out_specs=[
                pl.BlockSpec((1, BLOCK, columns), lambda i, p: (p[i], 0, 0)),
                pl.BlockSpec((1, BLOCK, sketch_width), lambda i, p: (p[i], 0, 0)),
            ],
        ),
        input_output_aliases={3: 0, 4: 1} if held else {},
        cost_estimate=pl.CostEstimate(
            flops=2 * n_tensor * BLOCK * columns * sketch_width,
            bytes_accessed=6_000_000,
            transcendentals=0,
        ),
    )(position, incoming, probe, *held)


def shards(embed_rows, head_rows, row_offsets, slot_table, probe):
    n_tensor = lax.axis_size("tensor")
    n_data = lax.axis_size("dp")
    my_tensor = lax.axis_index("tensor")
    my_data = lax.axis_index("dp")
    quarter = R // 4
    col_width = embed_rows.shape[1]
    devices = n_tensor * n_data
    per_rank = R // BLOCK
    total_blocks = per_rank * n_tensor
    slot_count = 2 * total_blocks // devices
    max_from = slot_count // n_tensor

    mine = lax.dynamic_slice_in_dim(row_offsets, my_tensor, 2, 1)
    before = mine[:, 0] - my_tensor * R
    after = mine[:, 1] - my_tensor * R
    n_lead = jnp.clip(-before, 0, quarter)
    tail_begin = R - before
    lead_part, trail_part = cut_edges(embed_rows, head_rows, n_lead, tail_begin, quarter)
    from_right = from_behind(lead_part, "tensor", -1)
    from_left = from_behind(trail_part, "tensor", 1)

    slot_grid = slot_table.reshape(devices, slot_count)
    source = slot_grid % total_blocks // per_rank
    local_block = slot_grid // total_blocks * per_rank + slot_grid % per_rank
    from_me = source == my_tensor
    rank_order = jnp.cumsum(from_me.astype(jnp.int32), axis=1) - 1
    slot_index = jnp.arange(max_from, dtype=jnp.int32)
    select = from_me[:, None, :] & (rank_order[:, None, :] == slot_index[None, :, None])
    picked = jnp.sum(jnp.where(select, local_block[:, None, :], 0), axis=2).T
    packed = pack_local(picked.reshape(-1), before, embed_rows, head_rows, max_from, devices)

    writer = my_data * n_tensor + my_tensor
    my_source = lax.dynamic_slice_in_dim(source, writer, 1, 0)[0]
    slot_range = jnp.arange(slot_count, dtype=jnp.int32)
    earlier = (my_source[None, :] == my_source[:, None]) & (
        slot_range[None, :] < slot_range[:, None]
    )
    rank_within = jnp.sum(earlier.astype(jnp.int32), axis=1)
    order = rank_within * n_tensor + my_source
    position = jnp.sum(
        jnp.where(order[None, :] == slot_range[:, None], slot_range[None, :], 0), axis=1
    ).reshape(max_from, n_tensor)

    outputs = None
    for c in range(max_from):
        outgoing = overlay(picked[c], before, after, packed[c], from_left, from_right)
        incoming = lax.all_to_all(
            outgoing, ("dp", "tensor"), split_axis=0, concat_axis=0, tiled=True
        )
        incoming = incoming.reshape(n_data, n_tensor, BLOCK, col_width)
        outputs = store_piece(position[c], incoming, probe, slot_count, outputs)
    return tuple(outputs)


def solution(mesh):
    return jax.shard_map(
        shards,
        mesh=mesh,
        in_specs=(P("tensor", "dp"), P("tensor", "dp"), P(), P(), P()),
        out_specs=(P(("dp", "tensor"), None, None), P(("dp", "tensor"), None, None)),
        check_vma=False,
    )
```

time: 209 us -> 170 us (0.81)
  Pallas kernels: 0 us -> 61.9 us
  other arithmetic: 41.5 us -> 2.04 us
  waiting for transfers between devices: 113 us -> 79.2 us
  local copies, waits for them, and re-layouts: 26.9 us -> 4.51 us
  starting transfers between devices: 8.89 us -> 20.6 us
  matrix products: 10.7 us -> 0 us
  between operations: 7.29 us -> 0.75 us
    pallas_call x0 -> x10, Pallas kernels: none -> 61.9 us  [the longest x4 32 us: store_piece(): pl.pallas_call(store_kernel, out_shape=out_shape, grid_spec=pltpu.Prefetc...]
    concatenate x2 -> x1, other arithmetic: 27 us -> 0.59 us  [cut_edges(): starts = jnp.concatenate([n_lead, tail_begin])]
    all_to_all x1 -> x4, waiting for transfers between devices: 93.3 us -> 68 us  [shards(): lax.all_to_all(outgoing, ('dp', 'tensor'), split_axis=0, concat_axis=0, t...]
    another operation x5 -> x0, other arithmetic: 13 us -> none  [the longest x3 10.8 us: shards(): aligned = jnp.stack(aligned_list)]
    all_to_all x1 -> x4, starting transfers between devices: 5.53 us -> 17.1 us  [shards(): lax.all_to_all(outgoing, ('dp', 'tensor'), split_axis=0, concat_axis=0, t...]
    dot_general x1 -> x0, matrix products: 10.7 us -> none  [shards(): jnp.dot(stored.reshape(slot_count * BLOCK, n_data * col_width), probe, pr...]
    gather x2 -> x0, local copies, waits for them, and re-layouts: 10.6 us -> none  [the longest x1 5.28 us: shards(): gathered = incoming[position]]
    ppermute x2, waiting for transfers between devices: 19.7 us -> 11.2 us  [from_behind(): return lax.ppermute(block, axis, route)]
  transfers between devices with their start and end apart: 3 -> 6, of which waited for: 3 -> 6; matrix products, arithmetic and copies ran while one was open for 1% -> 1% of each run, Pallas kernels for 0% -> 27%
where the time goes in v1:
time: 170 us; the launch traced here: 169 us
  waiting for transfers between devices  79.2 us (47%)
  Pallas kernels  61.9 us (36%)
  starting transfers between devices  20.6 us (12%)
  local copies, waits for them, and re-layouts  4.51 us (3%)
  other arithmetic  2.04 us (1%)
    all_to_all x4, waiting for transfers between devices, shards(): lax.all_to_all(outgoing, ('dp', 'tensor'), split_axis=0, concat_axis=0, t...  68 us
    pallas_call x4, Pallas kernels, store_piece(): pl.pallas_call(store_kernel, out_shape=out_shape, grid_spec=pltpu.Prefetc...  32 us
    all_to_all x4, starting transfers between devices, shards(): lax.all_to_all(outgoing, ('dp', 'tensor'), split_axis=0, concat_axis=0, t...  17.1 us
    pallas_call x4, Pallas kernels, overlay(): pl.pallas_call(overlay_kernel, out_shape=jax.ShapeDtypeStruct(packed.shap...  15.8 us
    ppermute x2, waiting for transfers between devices, from_behind(): return lax.ppermute(block, axis, route)  11.2 us
    pallas_call x1, Pallas kernels, pack_local(): pl.pallas_call(pack_kernel, out_shape=[shape] * pieces, in_specs=[smem, s...  10 us
    pallas_call x1, Pallas kernels, cut_edges(): pl.pallas_call(edges_kernel, out_shape=(shape, shape), in_specs=[pl.Block...  4.06 us
    ppermute x2, starting transfers between devices, from_behind(): return lax.ppermute(block, axis, route)  3.48 us
  transfers between devices with their start and end apart: 6, of which 6 were waited for; matrix products, arithmetic and copies ran while one was open for 1% of the time, Pallas kernels for 27%

profile of v1, /device:TPU:0, one launch (start us, length us, event | category | flops | bytes accessed | tf_op | source)
XLA Modules:
  0.0 169.0 jit_solution(5316111927342115224)
XLA Ops:
  1.4 0.8 subtract_reduce_fusion
  2.7 4.1 %shard_map.69 = (bf16[2,2048,128]{2,1,0:T(8,128)(2,1)}, bf16[2,2048,128]{2,1,0:T(8,128)(2,1)}) custom-call(s32[4]{0:T(128)} %pad_add_fusion.starts, bf16[12288,128]{1,0:T(8,128)(2,1)} %embed.3, bf16[12288,128]{1,0:T(8,128)(2,1)} %head.3), custom_call_target="tpu_custom_call" | custom-call | tf_op jit(solution)/shard_map/pallas_call | solution.py:80
  7.4 2.9 %collective-permute-start.1 = (bf16[2,2048,128]{2,1,0:T(8,128)(2,1)}, bf16[2,2048,128]{2,1,0:T(8,128)(2,1)S(1)}, u32[]{:S(2)}, u32[]{:S(2)}) collective-permute-start(bf16[2,2048,128]{2,1,0:T(8,128)(2,1)} %get-tuple-element.16), channel_id=1, source_target_pairs={{1,0},{2,1},{3,2},{4,3},{5,4},{6,5},{7,6},{0,7},{9,8},{10,9},{11,1... | collective-permute-start | bytes 3145736 | tf_op jit(solution)/shard_map/ppermute | solution.py:18
  11.9 10.0 %shard_map.68 = (bf16[32,128,128]{2,1,0:T(8,128)(2,1)}, bf16[32,128,128]{2,1,0:T(8,128)(2,1)}, bf16[32,128,128]{2,1,0:T(8,128)(2,1)}, bf16[32,128,128]{2,1,0:T(8,128)(2,1)}) custom-call(s32[128]{0:T(128)} %reshape.177.picked, s32[2]{0:T(128)} %copy-done.7, bf16[12288,128]{1,0:T(8,128)(2,1)} %embed.3, bf16[12288,128]{1,0:T(8,128)(2,1)} %head.3), custom_call_target="tpu_custom_call" | custom-call | flops 4000000000 | bytes 10000000 | tf_op jit(solution)/shard_map/pallas_call | solution.py:127
  21.9 9.6 %collective-permute-done.left = bf16[2,2048,128]{2,1,0:T(8,128)(2,1)S(1)} collective-permute-done((bf16[2,2048,128]{2,1,0:T(8,128)(2,1)}, bf16[2,2048,128]{2,1,0:T(8,128)(2,1)S(1)}, u32[]{:S(2)}, u32[]{:S(2)}) %collective-permute-start) | collective-permute-done | bytes 1048608 | tf_op jit(solution)/shard_map/ppermute | solution.py:18
  31.6 1.6 collective-permute-done.1.right
  33.1 1.0 copy-done.2
  34.1 3.9 %shard_map.71 = bf16[32,128,128]{2,1,0:T(8,128)(2,1)} custom-call(s32[32]{0:T(128)} %get-tuple-element.33.picked, s32[2]{0:T(128)} %copy-done.7, s32[2]{0:T(128)} %get-tuple-element.26.after, bf16[32,128,128]{2,1,0:T(8,128)(2,1)} %get-tuple-element.17.packed, bf16[2,2048,128]{2,1,0:T(8,128)(2,1)} %copy-done.1, bf16[2,2048,128]{2,1,0:T(8,128)(2,1)} %copy-done.2), custom_call_target="tpu_custom_call" | custom-call | flops 1000000000 | bytes 4000000 | tf_op jit(solution)/shard_map/pallas_call | solution.py:170
  38.0 6.3 %all-to-all-start.1 = ((bf16[32,128,128]{2,1,0:T(8,128)(2,1)}), bf16[32,128,128]{2,1,0:T(8,128)(2,1)S(1)}, u32[]{:S(2)}, u32[]{:S(2)}) async-start(bf16[32,128,128]{2,1,0:T(8,128)(2,1)} %shard_map.71), calls=%async_computation.1 | async-start | bytes 2097152 | tf_op jit(solution)/shard_map/all_to_all | solution.py:268
  44.3 4.0 %shard_map.73 = bf16[32,128,128]{2,1,0:T(8,128)(2,1)} custom-call(s32[32]{0:T(128)} %get-tuple-element.31.picked, s32[2]{0:T(128)} %copy-done.7, s32[2]{0:T(128)} %get-tuple-element.26.after, bf16[32,128,128]{2,1,0:T(8,128)(2,1)} %get-tuple-element.19.packed, bf16[2,2048,128]{2,1,0:T(8,128)(2,1)} %copy-done.1, bf16[2,2048,128]{2,1,0:T(8,128)(2,1)} %copy-done.2), custom_call_target="tpu_custom_call" | custom-call | flops 1000000000 | bytes 4000000 | tf_op jit(solution)/shard_map/pallas_call | solution.py:170
  48.3 22.2 %all-to-all-done.1 = bf16[32,128,128]{2,1,0:T(8,128)(2,1)S(1)} async-done(((bf16[32,128,128]{2,1,0:T(8,128)(2,1)}), bf16[32,128,128]{2,1,0:T(8,128)(2,1)S(1)}, u32[]{:S(2)}, u32[]{:S(2)}) %all-to-all-start.1) | async-done | bytes 1048608 | tf_op jit(solution)/shard_map/all_to_all | solution.py:268
  70.5 3.6 %all-to-all-start.3 = ((bf16[32,128,128]{2,1,0:T(8,128)(2,1)}), bf16[32,128,128]{2,1,0:T(8,128)(2,1)S(1)}, u32[]{:S(2)}, u32[]{:S(2)}) async-start(bf16[32,128,128]{2,1,0:T(8,128)(2,1)} %shard_map.73), calls=%async_computation.3 | async-start | bytes 2097152 | tf_op jit(solution)/shard_map/all_to_all | solution.py:268
  74.2 3.9 %shard_map.72 = bf16[32,128,128]{2,1,0:T(8,128)(2,1)} custom-call(s32[32]{0:T(128)} %get-tuple-element.32.picked, s32[2]{0:T(128)} %copy-done.7, s32[2]{0:T(128)} %get-tuple-element.26.after, bf16[32,128,128]{2,1,0:T(8,128)(2,1)} %get-tuple-element.18.packed, bf16[2,2048,128]{2,1,0:T(8,128)(2,1)} %copy-done.1, bf16[2,2048,128]{2,1,0:T(8,128)(2,1)} %copy-done.2), custom_call_target="tpu_custom_call" | custom-call | flops 1000000000 | bytes 4000000 | tf_op jit(solution)/shard_map/pallas_call | solution.py:170
  78.1 22.3 %all-to-all-done.3 = bf16[32,128,128]{2,1,0:T(8,128)(2,1)S(1)} async-done(((bf16[32,128,128]{2,1,0:T(8,128)(2,1)}), bf16[32,128,128]{2,1,0:T(8,128)(2,1)S(1)}, u32[]{:S(2)}, u32[]{:S(2)}) %all-to-all-start.3) | async-done | bytes 1048608 | tf_op jit(solution)/shard_map/all_to_all | solution.py:268
  100.4 3.6 %all-to-all-start.2 = ((bf16[32,128,128]{2,1,0:T(8,128)(2,1)}), bf16[32,128,128]{2,1,0:T(8,128)(2,1)S(1)}, u32[]{:S(2)}, u32[]{:S(2)}) async-start(bf16[32,128,128]{2,1,0:T(8,128)(2,1)} %shard_map.72), calls=%async_computation.2 | async-start | bytes 2097152 | tf_op jit(solution)/shard_map/all_to_all | solution.py:268
  104.0 3.9 %shard_map.70 = bf16[32,128,128]{2,1,0:T(8,128)(2,1)} custom-call(s32[32]{0:T(128)} %get-tuple-element.34.picked, s32[2]{0:T(128)} %copy-done.7, s32[2]{0:T(128)} %get-tuple-element.26.after, bf16[32,128,128]{2,1,0:T(8,128)(2,1)} %get-tuple-element.14.packed, bf16[2,2048,128]{2,1,0:T(8,128)(2,1)} %copy-done.1, bf16[2,2048,128]{2,1,0:T(8,128)(2,1)} %copy-done.2), custom_call_target="tpu_custom_call" | custom-call | flops 1000000000 | bytes 4000000 | tf_op jit(solution)/shard_map/pallas_call | solution.py:170
  107.9 22.3 %all-to-all-done.2 = bf16[32,128,128]{2,1,0:T(8,128)(2,1)S(1)} async-done(((bf16[32,128,128]{2,1,0:T(8,128)(2,1)}), bf16[32,128,128]{2,1,0:T(8,128)(2,1)S(1)}, u32[]{:S(2)}, u32[]{:S(2)}) %all-to-all-start.2) | async-done | bytes 1048608 | tf_op jit(solution)/shard_map/all_to_all | solution.py:268
  130.2 3.6 %all-to-all-start = ((bf16[32,128,128]{2,1,0:T(8,128)(2,1)}), bf16[32,128,128]{2,1,0:T(8,128)(2,1)S(1)}, u32[]{:S(2)}, u32[]{:S(2)}) async-start(bf16[32,128,128]{2,1,0:T(8,128)(2,1)} %shard_map.70), calls=%async_computation | async-start | bytes 2097152 | tf_op jit(solution)/shard_map/all_to_all | solution.py:268
  134.8 8.0 %shard_map.74 = (bf16[32,128,512]{2,1,0:T(8,128)(2,1)}, f32[32,128,1024]{2,1,0:T(8,128)}) custom-call(s32[8]{0:T(128)} %get-tuple-element.35.position, bf16[4,8,128,128]{3,2,1,0:T(8,128)(2,1)} %bitcast.24, bf16[512,1024]{1,0:T(8,128)(2,1)} %probe.7), custom_call_target="tpu_custom_call" | custom-call | flops 1073741824 | bytes 6000000 | tf_op jit(solution)/shard_map/pallas_call | solution.py:196
  142.8 8.0 %shard_map.75 = (bf16[32,128,512]{2,1,0:T(8,128)(2,1)}, f32[32,128,1024]{2,1,0:T(8,128)}) custom-call(s32[8]{0:T(128)} %get-tuple-element.36.position, bf16[4,8,128,128]{3,2,1,0:T(8,128)(2,1)} %bitcast.23, bf16[512,1024]{1,0:T(8,128)(2,1)} %probe.7, bf16[32,128,512]{2,1,0:T(8,128)(2,1)} %get-tuple-element.20.refs_0_, ...), custom_call_target="tpu_custom_call", output_to_operand_aliasing={{0}: (3, {}), {1}: (4, {})} | custom-call | flops 1073741824 | bytes 6000000 | tf_op jit(solution)/shard_map/pallas_call | solution.py:196
  150.8 8.0 %shard_map.76 = (bf16[32,128,512]{2,1,0:T(8,128)(2,1)}, f32[32,128,1024]{2,1,0:T(8,128)}) custom-call(s32[8]{0:T(128)} %get-tuple-element.37.position, bf16[4,8,128,128]{3,2,1,0:T(8,128)(2,1)} %bitcast.21, bf16[512,1024]{1,0:T(8,128)(2,1)} %probe.7, bf16[32,128,512]{2,1,0:T(8,128)(2,1)} %get-tuple-element.22.refs_0_, ...), custom_call_target="tpu_custom_call", output_to_operand_aliasing={{0}: (3, {}), {1}: (4, {})} | custom-call | flops 1073741824 | bytes 6000000 | tf_op jit(solution)/shard_map/pallas_call | solution.py:196
  158.8 1.3 all-to-all-done
  160.0 1.0 copy-done.4
  161.0 8.0 %shard_map.77 = (bf16[32,128,512]{2,1,0:T(8,128)(2,1)}, f32[32,128,1024]{2,1,0:T(8,128)}) custom-call(s32[8]{0:T(128)} %get-tuple-element.38.position, bf16[4,8,128,128]{3,2,1,0:T(8,128)(2,1)} %bitcast.22, bf16[512,1024]{1,0:T(8,128)(2,1)} %probe.7, bf16[32,128,512]{2,1,0:T(8,128)(2,1)} %get-tuple-element.24.refs_0_, ...), custom_call_target="tpu_custom_call", output_to_operand_aliasing={{0}: (3, {}), {1}: (4, {})} | custom-call | flops 1073741824 | bytes 6000000 | tf_op jit(solution)/shard_map/pallas_call | solution.py:196
  (32 shorter events, 4.4 us)
Async XLA Ops:
  0.6 0.7 copy-start
  0.6 9.6 %copy-start.8 = (s32[1024]{0:T(1024)S(1)}, s32[1024]{0:T(1024)}, u32[]{:S(2)}) copy-start(s32[1024]{0:T(1024)} %param.8) | copy-start | bytes 12292
  2.2 9.7 %copy-start.7 = (s32[2]{0:T(128)}, s32[2]{0:T(128)S(1)}, u32[]{:S(2)}) copy-start(s32[2]{0:T(128)S(1)} %get-tuple-element.27.before) | copy-start | bytes 28
  6.8 24.7 %collective-permute-start = (bf16[2,2048,128]{2,1,0:T(8,128)(2,1)}, bf16[2,2048,128]{2,1,0:T(8,128)(2,1)S(1)}, u32[]{:S(2)}, u32[]{:S(2)}) collective-permute-start(bf16[2,2048,128]{2,1,0:T(8,128)(2,1)} %get-tuple-element.15), channel_id=1, source_target_pairs={{7,0},{0,1},{1,2},{2,3},{3,4},{4,5},{5,6},{6,7},{15,8},{8,9},{9,10... | collective-permute-start | bytes 3145736 | tf_op jit(solution)/shard_map/ppermute | solution.py:18
  7.4 25.8 %collective-permute-start.1 = (bf16[2,2048,128]{2,1,0:T(8,128)(2,1)}, bf16[2,2048,128]{2,1,0:T(8,128)(2,1)S(1)}, u32[]{:S(2)}, u32[]{:S(2)}) collective-permute-start(bf16[2,2048,128]{2,1,0:T(8,128)(2,1)} %get-tuple-element.16), channel_id=1, source_target_pairs={{1,0},{2,1},{3,2},{4,3},{5,4},{6,5},{7,6},{0,7},{9,8},{10,9},{11,1... | collective-permute-start | bytes 3145736 | tf_op jit(solution)/shard_map/ppermute | solution.py:18
  31.6 1.6 copy-start.1
  33.1 1.0 copy-start.2
  38.0 32.5 %all-to-all-start.1 = ((bf16[32,128,128]{2,1,0:T(8,128)(2,1)}), bf16[32,128,128]{2,1,0:T(8,128)(2,1)S(1)}, u32[]{:S(2)}, u32[]{:S(2)}) async-start(bf16[32,128,128]{2,1,0:T(8,128)(2,1)} %shard_map.71), calls=%async_computation.1 | async-start | bytes 2097152 | tf_op jit(solution)/shard_map/all_to_all | solution.py:268
  70.5 29.8 %copy-start.3 = (bf16[32,128,128]{2,1,0:T(8,128)(2,1)}, bf16[32,128,128]{2,1,0:T(8,128)(2,1)S(1)}, u32[]{:S(2)}) copy-start(bf16[32,128,128]{2,1,0:T(8,128)(2,1)S(1)} %all-to-all-done.1) | copy-start | bytes 3145732
  70.5 29.8 %all-to-all-start.3 = ((bf16[32,128,128]{2,1,0:T(8,128)(2,1)}), bf16[32,128,128]{2,1,0:T(8,128)(2,1)S(1)}, u32[]{:S(2)}, u32[]{:S(2)}) async-start(bf16[32,128,128]{2,1,0:T(8,128)(2,1)} %shard_map.73), calls=%async_computation.3 | async-start | bytes 2097152 | tf_op jit(solution)/shard_map/all_to_all | solution.py:268
  100.4 29.8 %copy-start.6 = (bf16[32,128,128]{2,1,0:T(8,128)(2,1)}, bf16[32,128,128]{2,1,0:T(8,128)(2,1)S(1)}, u32[]{:S(2)}) copy-start(bf16[32,128,128]{2,1,0:T(8,128)(2,1)S(1)} %all-to-all-done.3) | copy-start | bytes 3145732
  100.4 29.8 %all-to-all-start.2 = ((bf16[32,128,128]{2,1,0:T(8,128)(2,1)}), bf16[32,128,128]{2,1,0:T(8,128)(2,1)S(1)}, u32[]{:S(2)}, u32[]{:S(2)}) async-start(bf16[32,128,128]{2,1,0:T(8,128)(2,1)} %shard_map.72), calls=%async_computation.2 | async-start | bytes 2097152 | tf_op jit(solution)/shard_map/all_to_all | solution.py:268
  130.2 12.6 %copy-start.5 = (bf16[32,128,128]{2,1,0:T(8,128)(2,1)}, bf16[32,128,128]{2,1,0:T(8,128)(2,1)S(1)}, u32[]{:S(2)}) copy-start(bf16[32,128,128]{2,1,0:T(8,128)(2,1)S(1)} %all-to-all-done.2) | copy-start | bytes 3145732
  130.2 29.8 %all-to-all-start = ((bf16[32,128,128]{2,1,0:T(8,128)(2,1)}), bf16[32,128,128]{2,1,0:T(8,128)(2,1)S(1)}, u32[]{:S(2)}, u32[]{:S(2)}) async-start(bf16[32,128,128]{2,1,0:T(8,128)(2,1)} %shard_map.70), calls=%async_computation | async-start | bytes 2097152 | tf_op jit(solution)/shard_map/all_to_all | solution.py:268
  160.0 1.0 copy-start.4

commit v2 on v1

v2 whole, which is shorter than its diff:
```python
import functools

import jax
import jax.numpy as jnp
from jax import lax
from jax.experimental import pallas as pl
from jax.experimental.pallas import tpu as pltpu
from jax.sharding import PartitionSpec as P


R = 8192
BLOCK = 128
ALIGN = 16
MIB = 1 << 20


def from_behind(block, axis, distance):
    devices = range(lax.axis_size(axis))
    route = [((i - distance) % len(devices), i) for i in devices]
    return lax.ppermute(block, axis, route)


def any_space():
    return pl.BlockSpec(memory_space=pl.ANY)


def in_hbm():
    return pl.BlockSpec(memory_space=pltpu.HBM)


def smem():
    return pl.BlockSpec(memory_space=pltpu.SMEM)


def vmem():
    return pl.BlockSpec(memory_space=pltpu.VMEM)


def my_span(offsets, m):
    t = lax.axis_index("tensor")
    return offsets[m, t] - t * R, offsets[m, t + 1] - t * R


def edges_kernel(offsets, embed, head, lead_out, trail_out, rows, wide, sems):
    quarter = lead_out.shape[1]
    raws = [embed, head]
    copies = []
    for m in range(2):
        first = (R - my_span(offsets, m)[0]) // ALIGN * ALIGN
        window = pl.ds(pl.multiple_of(first, ALIGN), quarter + ALIGN)
        lead = pltpu.make_async_copy(
            raws[m].at[pl.ds(0, quarter)], rows.at[2 * m, pl.ds(0, quarter)], sems.at[2 * m]
        )
        trail = pltpu.make_async_copy(raws[m].at[window], rows.at[2 * m + 1], sems.at[2 * m + 1])
        lead.start()
        trail.start()
        copies.append((lead, trail))
    for m in range(2):
        lead, trail = copies[m]
        lead.wait()
        before = my_span(offsets, m)[0]
        count = jnp.clip(-before, 0, quarter)

        def widen_lead(i, _):
            at = pl.multiple_of(i * BLOCK, BLOCK)
            wide[pl.ds(quarter + at, BLOCK), :] = rows[2 * m, pl.ds(at, BLOCK), :].astype(jnp.float32)
            return _

        lax.fori_loop(0, quarter // BLOCK, widen_lead, 0)

        def put_lead(i, _):
            at = pl.multiple_of(i * BLOCK, BLOCK)
            lead_out[m, pl.ds(at, BLOCK), :] = wide[pl.ds(count + at, BLOCK), :].astype(jnp.bfloat16)
            return _

        lax.fori_loop(0, quarter // BLOCK, put_lead, 0)
        trail.wait()
        shift = (R - before) % ALIGN

        def widen_trail(i, _):
            at = pl.multiple_of(i * BLOCK, BLOCK)
            wide[pl.ds(at, BLOCK), :] = rows[2 * m + 1, pl.ds(at, BLOCK), :].astype(jnp.float32)
            return _

        lax.fori_loop(0, quarter // BLOCK, widen_trail, 0)
        wide[pl.ds(quarter, ALIGN), :] = rows[2 * m + 1, pl.ds(quarter, ALIGN), :].astype(jnp.float32)

        def put_trail(i, _):
            at = pl.multiple_of(i * BLOCK, BLOCK)
            trail_out[m, pl.ds(at, BLOCK), :] = wide[pl.ds(shift + at, BLOCK), :].astype(jnp.bfloat16)
            return _

        lax.fori_loop(0, quarter // BLOCK, put_trail, 0)


def cut_edges(offsets, embed, head, quarter):
    width = embed.shape[1]
    shape = jax.ShapeDtypeStruct((2, quarter, width), embed.dtype)
    return pl.pallas_call(
        edges_kernel,
        out_shape=(shape, shape),
        in_specs=[smem(), in_hbm(), in_hbm()],
        out_specs=[vmem()] * 2,
        scratch_shapes=[
            pltpu.VMEM((4, quarter + ALIGN, width), embed.dtype),
            pltpu.VMEM((2 * quarter, width), jnp.float32),
            pltpu.SemaphoreType.DMA((4,)),
        ],
        compiler_params=pltpu.CompilerParams(vmem_limit_bytes=61 * MIB),
    )(offsets, embed, head)


def target_of(step, n_data, n_tensor):
    z = lax.rem(lax.axis_index("dp") + step % n_data, n_data)
    t = lax.rem(lax.axis_index("tensor") + step // n_data, n_tensor)
    return z * n_tensor + t


def pack_kernel(n_data, n_tensor, picked, offsets, embed, head, *refs):
    outs, (rows, wide, sems) = refs[:-3], refs[-3:]
    height = embed.shape[0]
    per_rank = R // BLOCK
    copies = []
    for m, raw in enumerate([embed, head]):
        copy = pltpu.make_async_copy(
            raw, rows.at[pl.ds(BLOCK + m * height, height)], sems.at[m]
        )
        copy.start()
        copies.append(copy)
    for copy in copies:
        copy.wait()
    per_pair = picked.shape[1]
    step = 0
    for out in outs:

        def body(i, _, step=step, out=out):
            block = picked[target_of(step + i // per_pair, n_data, n_tensor), i % per_pair]
            m = block // per_rank
            start = block % per_rank * BLOCK - my_span(offsets, m)[0]
            start = jnp.maximum(start + BLOCK, 0) + m * height
            first = pl.multiple_of(start // ALIGN * ALIGN, ALIGN)
            slot = lax.rem(i, 2)
            wide[slot] = rows[pl.ds(first, BLOCK + ALIGN), :].astype(jnp.float32)
            out[i] = wide[slot, pl.ds(start - first, BLOCK), :].astype(jnp.bfloat16)
            return _

        lax.fori_loop(0, out.shape[0], body, 0)
        step += out.shape[0] // per_pair


def pack_local(picked, offsets, embed, head, groups, n_data, n_tensor):
    height, width = embed.shape
    return pl.pallas_call(
        functools.partial(pack_kernel, n_data, n_tensor),
        out_shape=[
            jax.ShapeDtypeStruct((count, BLOCK, width), embed.dtype) for count in groups
        ],
        in_specs=[smem(), smem(), in_hbm(), in_hbm()],
        out_specs=[vmem()] * len(groups),
        scratch_shapes=[
            pltpu.VMEM((BLOCK + 2 * height, width), embed.dtype),
            pltpu.VMEM((2, BLOCK + ALIGN, width), jnp.float32),
            pltpu.SemaphoreType.DMA((2,)),
        ],
        compiler_params=pltpu.CompilerParams(vmem_limit_bytes=16 * MIB),
        cost_estimate=pl.CostEstimate(flops=4_000_000_000, bytes_accessed=10_000_000, transcendentals=0),
    )(picked, offsets, embed, head)


def overlay_kernel(first_step, n_data, n_tensor, picked, offsets, packed, left, right, *outs):
    per_rank = R // BLOCK
    quarter = left.shape[1]
    per_pair = picked.shape[1]
    for k, out in enumerate(outs):
        target = target_of(first_step + k, n_data, n_tensor)

        def body(j, _, k=k, out=out, target=target):
            block = picked[target, j]
            m = block // per_rank
            before, after = my_span(offsets, m)
            first = block % per_rank * BLOCK
            out[j] = packed[k * per_pair + j]
            row = first + lax.broadcasted_iota(jnp.int32, (BLOCK, 1), 0)

            @pl.when(first < before)
            def _left():
                at = pl.multiple_of(first, BLOCK)
                out[j] = jnp.where(row < before, left[m, pl.ds(at, BLOCK), :], out[j])

            @pl.when(first + BLOCK > after)
            def _right():
                at = pl.multiple_of(first - (R - quarter), BLOCK)
                out[j] = jnp.where(row >= after, right[m, pl.ds(at, BLOCK), :], out[j])

            return _

        lax.fori_loop(0, per_pair, body, 0)


def overlay(first_step, picked, offsets, packed, left, right, n_data, n_tensor):
    per_pair = picked.shape[1]
    steps = packed.shape[0] // per_pair
    return pl.pallas_call(
        functools.partial(overlay_kernel, first_step, n_data, n_tensor),
        out_shape=[jax.ShapeDtypeStruct((per_pair,) + packed.shape[1:], packed.dtype)] * steps,
        in_specs=[smem()] * 2 + [vmem()] * 3,
        out_specs=[vmem()] * steps,
        compiler_params=pltpu.CompilerParams(vmem_limit_bytes=16 * MIB),
        cost_estimate=pl.CostEstimate(flops=1_000_000_000, bytes_accessed=4_000_000, transcendentals=0),
    )(picked, offsets, packed, left, right)


def store_kernel(n_data, position, *refs):
    incoming, probe = refs[:n_data], refs[n_data]
    stored, sketch, full, product, sems = refs[-5:]
    per_pair, _, width = incoming[0].shape
    for s in range(n_data):
        column = pl.multiple_of(lax.rem(lax.axis_index("dp") - s + n_data, n_data) * width, width)
        for j in range(per_pair):
            full[j, :, pl.ds(column, width)] = incoming[s][j]
    copies = []
    for j in range(per_pair):
        product[j] = jnp.dot(full[j], probe[...], preferred_element_type=jnp.float32)
        slot = position[j]
        copies.append(pltpu.make_async_copy(full.at[j], stored.at[slot], sems.at[2 * j]))
        copies.append(pltpu.make_async_copy(product.at[j], sketch.at[slot], sems.at[2 * j + 1]))
        copies[-2].start()
        copies[-1].start()
    for copy in copies:
        copy.wait()


def store_group(position, incoming, probe, slot_count, previous):
    n_data = len(incoming)
    per_pair, _, width = incoming[0].shape
    columns = n_data * width
    sketch_width = probe.shape[1]
    out_shape = [
        jax.ShapeDtypeStruct((slot_count, BLOCK, columns), incoming[0].dtype),
        jax.ShapeDtypeStruct((slot_count, BLOCK, sketch_width), jnp.float32),
    ]
    held = [] if previous is None else list(previous)
    at = 2 + n_data
    return pl.pallas_call(
        functools.partial(store_kernel, n_data),
        out_shape=out_shape,
        in_specs=[smem()] + [vmem()] * (n_data + 1) + [any_space() for _ in held],
        out_specs=[any_space(), any_space()],
        scratch_shapes=[
            pltpu.VMEM((per_pair, BLOCK, columns), incoming[0].dtype),
            pltpu.VMEM((per_pair, BLOCK, sketch_width), jnp.float32),
            pltpu.SemaphoreType.DMA((2 * per_pair,)),
        ],
        compiler_params=pltpu.CompilerParams(vmem_limit_bytes=10 * MIB),
        input_output_aliases={at: 0, at + 1: 1} if held else {},
        cost_estimate=pl.CostEstimate(
            flops=2 * per_pair * BLOCK * columns * sketch_width,
            bytes_accessed=4_000_000,
            transcendentals=0,
        ),
    )(position, *incoming, probe, *held)


def shards(embed_rows, head_rows, row_offsets, slot_table, probe):
    n_tensor = lax.axis_size("tensor")
    n_data = lax.axis_size("dp")
    my_tensor = lax.axis_index("tensor")
    my_data = lax.axis_index("dp")
    quarter = R // 4
    devices = n_tensor * n_data
    per_rank = R // BLOCK
    total_blocks = per_rank * n_tensor
    slot_count = 2 * total_blocks // devices
    per_pair = slot_count // n_tensor
    lead_part, trail_part = cut_edges(row_offsets, embed_rows, head_rows, quarter)
    from_right = from_behind(lead_part, "tensor", -1)
    from_left = from_behind(trail_part, "tensor", 1)

    slot_grid = slot_table.reshape(devices, slot_count)
    source = slot_grid % total_blocks // per_rank
    local_block = slot_grid // total_blocks * per_rank + slot_grid % per_rank
    from_me = source == my_tensor
    rank_order = jnp.cumsum(from_me.astype(jnp.int32), axis=1) - 1
    slot_index = jnp.arange(per_pair, dtype=jnp.int32)
    select = from_me[:, None, :] & (rank_order[:, None, :] == slot_index[None, :, None])
    picked = jnp.sum(jnp.where(select, local_block[:, None, :], 0), axis=2)

    writer = my_data * n_tensor + my_tensor
    my_source = lax.dynamic_slice_in_dim(source, writer, 1, 0)[0]
    slot_range = jnp.arange(slot_count, dtype=jnp.int32)
    earlier = (my_source[None, :] == my_source[:, None]) & (
        slot_range[None, :] < slot_range[:, None]
    )
    rank_within = jnp.sum(earlier.astype(jnp.int32), axis=1)
    hops = (my_tensor - my_source + n_tensor) % n_tensor
    order = hops * per_pair + rank_within
    position = jnp.sum(
        jnp.where(order[None, :] == slot_range[:, None], slot_range[None, :], 0), axis=1
    ).reshape(n_tensor, per_pair)

    def move(block, step):
        u, s = step // n_data, step % n_data
        route = []
        for z in range(n_data):
            for t in range(n_tensor):
                to = (z + s) % n_data * n_tensor + (t + u) % n_tensor
                route.append((z * n_tensor + t, to))
        if not step:
            return block
        return lax.ppermute(block, ("dp", "tensor"), route)

    groups = [n_data * per_pair, (devices - n_data) * per_pair]
    packed = pack_local(picked, row_offsets, embed_rows, head_rows, groups, n_data, n_tensor)
    outgoing = []
    for k, first_step in enumerate([0, n_data]):
        outgoing += overlay(
            first_step, picked, row_offsets, packed[k], from_left, from_right, n_data, n_tensor
        )
    outputs = None
    for u in range(n_tensor):
        incoming = [move(outgoing[u * n_data + s], u * n_data + s) for s in range(n_data)]
        outputs = store_group(position[u], incoming, probe, slot_count, outputs)
    return tuple(outputs)


def solution(mesh):
    return jax.shard_map(
        shards,
        mesh=mesh,
        in_specs=(P("tensor", "dp"), P("tensor", "dp"), P(), P(), P()),
        out_specs=(P(("dp", "tensor"), None, None), P(("dp", "tensor"), None, None)),
        check_vma=False,
    )
```

time: 170 us -> 157 us (0.924)
  waiting for transfers between devices: 79.2 us -> 31.2 us
  starting transfers between devices: 20.6 us -> 62.4 us
  Pallas kernels: 61.9 us -> 40.6 us
  local copies, waits for them, and re-layouts: 4.51 us -> 19.1 us
    all_to_all x4 -> x0, waiting for transfers between devices: 68 us -> none  [shards(): lax.all_to_all(outgoing, ('dp', 'tensor'), split_axis=0, concat_axis=0, t...]
    ppermute x0 -> x31, starting transfers between devices: none -> 58.9 us  [move(): return lax.ppermute(block, ('dp', 'tensor'), route)]
    ppermute x0 -> x31, waiting for transfers between devices: none -> 23 us  [move(): return lax.ppermute(block, ('dp', 'tensor'), route)]
    pallas_call x10 -> x12, Pallas kernels: 61.9 us -> 40.6 us  [the longest x8 20.4 us: store_group(): pl.pallas_call(functools.partial(store_kernel, n_data), out_shape=out_sha...]
    all_to_all x4 -> x0, starting transfers between devices: 17.1 us -> none  [shards(): lax.all_to_all(outgoing, ('dp', 'tensor'), split_axis=0, concat_axis=0, t...]
    unnamed x18 -> x78, local copies, waits for them, and re-layouts: 2.62 us -> 18.1 us
    ppermute x2, waiting for transfers between devices: 11.2 us -> 8.19 us  [from_behind(): return lax.ppermute(block, axis, route)]
  transfers between devices with their start and end apart: 6 -> 33, of which waited for: 6 -> 8; matrix products, arithmetic and copies ran while one was open for 1% -> 2% of each run, Pallas kernels for 27% -> 18%
where the time goes in v2:
time: 157 us; the launch traced here: 156 us
  starting transfers between devices  62.4 us (40%)
  Pallas kernels  40.6 us (26%)
  waiting for transfers between devices  31.2 us (20%)
  local copies, waits for them, and re-layouts  19.1 us (12%)
  other arithmetic  1.96 us (1%)
    ppermute x31, starting transfers between devices, move(): return lax.ppermute(block, ('dp', 'tensor'), route)  58.9 us
    ppermute x31, waiting for transfers between devices, move(): return lax.ppermute(block, ('dp', 'tensor'), route)  23 us
    pallas_call x8, Pallas kernels, store_group(): pl.pallas_call(functools.partial(store_kernel, n_data), out_shape=out_sha...  20.4 us
    unnamed x78, local copies, waits for them, and re-layouts  18.1 us
    pallas_call x1, Pallas kernels, pack_local(): pl.pallas_call(functools.partial(pack_kernel, n_data, n_tensor), out_shap...  8.86 us
    ppermute x2, waiting for transfers between devices, from_behind(): return lax.ppermute(block, axis, route)  8.19 us
    pallas_call x2, Pallas kernels, overlay(): pl.pallas_call(functools.partial(overlay_kernel, first_step, n_data, n_te...  7.03 us
    pallas_call x1, Pallas kernels, cut_edges(): pl.pallas_call(edges_kernel, out_shape=(shape, shape), in_specs=[smem(),...  4.22 us
  transfers between devices with their start and end apart: 33, of which 8 were waited for; matrix products, arithmetic and copies ran while one was open for 2% of the time, Pallas kernels for 18%

profile of v2, /device:TPU:0, one launch (start us, length us, event | category | flops | bytes accessed | tf_op | source)
XLA Modules:
  0.0 156.2 jit_solution(17628320455968770269)
XLA Ops:
  0.7 4.2 %shard_map.69 = (bf16[2,2048,128]{2,1,0:T(8,128)(2,1)}, bf16[2,2048,128]{2,1,0:T(8,128)(2,1)}) custom-call(s32[2,9]{1,0:T(2,128)} %offsets.7, bf16[12288,128]{1,0:T(8,128)(2,1)} %embed.3, bf16[12288,128]{1,0:T(8,128)(2,1)} %head.3), custom_call_target="tpu_custom_call" | custom-call | tf_op jit(solution)/shard_map/pallas_call | solution.py:99
  5.4 2.9 %collective-permute-start.1 = (bf16[2,2048,128]{2,1,0:T(8,128)(2,1)}, bf16[2,2048,128]{2,1,0:T(8,128)(2,1)S(1)}, u32[]{:S(2)}, u32[]{:S(2)}) collective-permute-start(bf16[2,2048,128]{2,1,0:T(8,128)(2,1)} %get-tuple-element.54), channel_id=1, source_target_pairs={{1,0},{2,1},{3,2},{4,3},{5,4},{6,5},{7,6},{0,7},{9,8},{10,9},{11,1... | collective-permute-start | bytes 3145736 | tf_op jit(solution)/shard_map/ppermute | solution.py:20
  13.3 8.9 %shard_map.68 = (bf16[16,128,128]{2,1,0:T(8,128)(2,1)S(1)}, bf16[112,128,128]{2,1,0:T(8,128)(2,1)S(1)}) custom-call(s32[32,4]{1,0:T(8,128)S(1)} %copy.22.picked, s32[2,9]{1,0:T(2,128)S(1)} %copy-done.3, bf16[12288,128]{1,0:T(8,128)(2,1)S(1)} %copy-done.1, bf16[12288,128]{1,0:T(8,128)(2,1)S(1)} %copy-done.2), custom_call_target="tpu_custom_call" | custom-call | flops 4000000000 | bytes 10000000 | tf_op jit(solution)/shard_map/pallas_call | solution.py:153
  23.0 6.6 %collective-permute-done.left = bf16[2,2048,128]{2,1,0:T(8,128)(2,1)S(1)} collective-permute-done((bf16[2,2048,128]{2,1,0:T(8,128)(2,1)}, bf16[2,2048,128]{2,1,0:T(8,128)(2,1)S(1)}, u32[]{:S(2)}, u32[]{:S(2)}) %collective-permute-start) | collective-permute-done | bytes 1048608 | tf_op jit(solution)/shard_map/ppermute | solution.py:20
  31.2 5.7 %shard_map.70 = (bf16[4,128,128]{2,1,0:T(8,128)(2,1)S(1)}, bf16[4,128,128]{2,1,0:T(8,128)(2,1)S(1)}, bf16[4,128,128]{2,1,0:T(8,128)(2,1)S(1)}, bf16[4,128,128]{2...) custom-call(s32[32,4]{1,0:T(8,128)S(1)} %copy.22.picked, ...), custom_call_target="tpu_custom_call" | custom-call | flops 1000000000 | bytes 4000000 | tf_op jit(solution)/shard_map/pallas_call | solution.py:203
  50.4 3.5 %collective-permute-start.7 = (bf16[4,128,128]{2,1,0:T(8,128)(2,1)}, bf16[4,128,128]{2,1,0:T(8,128)(2,1)S(1)}, u32[]{:S(2)}, u32[]{:S(2)}) collective-permute-start(bf16[4,128,128]{2,1,0:T(8,128)(2,1)} %get-tuple-element.60), channel_id=1, source_target_pairs={{0,14},{1,15},{2,8},{3,9},{4,10},{5,11},{6,12},{7,13},{8,22},{9,23... | collective-permute-start | bytes 393224 | tf_op jit(solution)/shard_map/ppermute | solution.py:310
  58.8 4.4 %collective-permute-start.12 = (bf16[4,128,128]{2,1,0:T(8,128)(2,1)}, bf16[4,128,128]{2,1,0:T(8,128)(2,1)}, u32[]{:S(2)}, u32[]{:S(2)}) collective-permute-start(bf16[4,128,128]{2,1,0:T(8,128)(2,1)} %get-tuple-element.65), channel_id=1, source_target_pairs={{0,21},{1,22},{2,23},{3,16},{4,17},{5,18},{6,19},{7,20},{8,29},{9,... | collective-permute-start | bytes 393224 | tf_op jit(solution)/shard_map/ppermute | solution.py:310
  64.7 5.0 %collective-permute-done.8.refs_2_ = bf16[4,128,128]{2,1,0:T(8,128)(2,1)S(1)} collective-permute-done((bf16[4,128,128]{2,1,0:T(8,128)(2,1)}, bf16[4,128,128]{2,1,0:T(8,128)(2,1)S(1)}, u32[]{:S(2)}, u32[]{:S(2)}) %collective-permute-start.8) | collective-permute-done | bytes 131104 | tf_op jit(solution)/shard_map/ppermute | solution.py:310
  69.7 2.6 %collective-permute-start.18 = (bf16[4,128,128]{2,1,0:T(8,128)(2,1)}, bf16[4,128,128]{2,1,0:T(8,128)(2,1)S(1)}, u32[]{:S(2)}, u32[]{:S(2)}) collective-permute-start(bf16[4,128,128]{2,1,0:T(8,128)(2,1)} %copy-done.34), channel_id=1, source_target_pairs={{0,3},{1,4},{2,5},{3,6},{4,7},{5,0},{6,1},{7,2},{8,11},{9,12},{10,... | collective-permute-start | bytes 393224 | tf_op jit(solution)/shard_map/ppermute | solution.py:310
  72.3 2.6 %collective-permute-start.20 = (bf16[4,128,128]{2,1,0:T(8,128)(2,1)}, bf16[4,128,128]{2,1,0:T(8,128)(2,1)S(1)}, u32[]{:S(2)}, u32[]{:S(2)}) collective-permute-start(bf16[4,128,128]{2,1,0:T(8,128)(2,1)} %copy-done.32), channel_id=1, source_target_pairs={{0,19},{1,20},{2,21},{3,22},{4,23},{5,16},{6,17},{7,18},{8,27},{9,... | collective-permute-start | bytes 393224 | tf_op jit(solution)/shard_map/ppermute | solution.py:310
  79.2 3.2 %collective-permute-start.23 = (bf16[4,128,128]{2,1,0:T(8,128)(2,1)}, bf16[4,128,128]{2,1,0:T(8,128)(2,1)S(1)}, u32[]{:S(2)}, u32[]{:S(2)}) collective-permute-start(bf16[4,128,128]{2,1,0:T(8,128)(2,1)} %copy-done.30), channel_id=1, source_target_pairs={{0,10},{1,11},{2,12},{3,13},{4,14},{5,15},{6,8},{7,9},{8,18},{9,19... | collective-permute-start | bytes 393224 | tf_op jit(solution)/shard_map/ppermute | solution.py:310
  82.4 3.9 %collective-permute-start.24 = (bf16[4,128,128]{2,1,0:T(8,128)(2,1)}, bf16[4,128,128]{2,1,0:T(8,128)(2,1)S(1)}, u32[]{:S(2)}, u32[]{:S(2)}) collective-permute-start(bf16[4,128,128]{2,1,0:T(8,128)(2,1)} %copy-done.29), channel_id=1, source_target_pairs={{0,18},{1,19},{2,20},{3,21},{4,22},{5,23},{6,16},{7,17},{8,26},{9,... | collective-permute-start | bytes 393224 | tf_op jit(solution)/shard_map/ppermute | solution.py:310
  90.0 5.4 %collective-permute-done.24.refs_2_ = bf16[4,128,128]{2,1,0:T(8,128)(2,1)S(1)} collective-permute-done((bf16[4,128,128]{2,1,0:T(8,128)(2,1)}, bf16[4,128,128]{2,1,0:T(8,128)(2,1)S(1)}, u32[]{:S(2)}, u32[]{:S(2)}) %collective-permute-start.24) | collective-permute-done | bytes 131104 | tf_op jit(solution)/shard_map/ppermute | solution.py:310
  95.4 3.3 %collective-permute-done.25.refs_3_ = bf16[4,128,128]{2,1,0:T(8,128)(2,1)S(1)} collective-permute-done((bf16[4,128,128]{2,1,0:T(8,128)(2,1)}, bf16[4,128,128]{2,1,0:T(8,128)(2,1)S(1)}, u32[]{:S(2)}, u32[]{:S(2)}) %collective-permute-start.25) | collective-permute-done | bytes 131104 | tf_op jit(solution)/shard_map/ppermute | solution.py:310
  98.7 5.2 %collective-permute-start.28 = (bf16[4,128,128]{2,1,0:T(8,128)(2,1)}, bf16[4,128,128]{2,1,0:T(8,128)(2,1)S(1)}, u32[]{:S(2)}, u32[]{:S(2)}) collective-permute-start(bf16[4,128,128]{2,1,0:T(8,128)(2,1)} %copy-done.25), channel_id=1, source_target_pairs={{0,17},{1,18},{2,19},{3,20},{4,21},{5,22},{6,23},{7,16},{8,25},{9,... | collective-permute-start | bytes 393224 | tf_op jit(solution)/shard_map/ppermute | solution.py:310
  103.8 4.5 %collective-permute-start.29 = (bf16[4,128,128]{2,1,0:T(8,128)(2,1)}, bf16[4,128,128]{2,1,0:T(8,128)(2,1)S(1)}, u32[]{:S(2)}, u32[]{:S(2)}) collective-permute-start(bf16[4,128,128]{2,1,0:T(8,128)(2,1)} %copy-done.24), channel_id=1, source_target_pairs={{0,25},{1,26},{2,27},{3,28},{4,29},{5,30},{6,31},{7,24},{8,1},{9,2... | collective-permute-start | bytes 393224 | tf_op jit(solution)/shard_map/ppermute | solution.py:310
  109.1 8.3 %collective-permute-done.32.refs_3_ = bf16[4,128,128]{2,1,0:T(8,128)(2,1)S(1)} collective-permute-done((bf16[4,128,128]{2,1,0:T(8,128)(2,1)S(1)}, bf16[4,128,128]{2,1,0:T(8,128)(2,1)S(1)}, u32[]{:S(2)}, u32[]{:S(2)}) %collective-permute-start.32) | collective-permute-done | bytes 131104 | tf_op jit(solution)/shard_map/ppermute | solution.py:310
  117.4 3.7 %collective-permute-start.21 = (bf16[4,128,128]{2,1,0:T(8,128)(2,1)}, bf16[4,128,128]{2,1,0:T(8,128)(2,1)S(1)}, u32[]{:S(2)}, u32[]{:S(2)}) collective-permute-start(bf16[4,128,128]{2,1,0:T(8,128)(2,1)} %copy-done.23), channel_id=1, source_target_pairs={{0,27},{1,28},{2,29},{3,30},{4,31},{5,24},{6,25},{7,26},{8,3},{9,4... | collective-permute-start | bytes 393224 | tf_op jit(solution)/shard_map/ppermute | solution.py:310
  121.1 2.5 %shard_map.72 = (bf16[32,128,512]{2,1,0:T(8,128)(2,1)}, f32[32,128,1024]{2,1,0:T(8,128)}) custom-call(s32[4]{0:T(128)S(1)} %get-tuple-element.105.position, bf16[4,128,128]{2,1,0:T(8,128)(2,1)S(1)} %get-tuple-element.84.refs_0_, bf16[4,128,128]{2,1,0:T(8,128)(2,1)S(1)} %collective-permute-done.30.refs_1_, ...), custom_call_target="tpu_custom_call" | custom-call | flops 536870912 | bytes 4000000 | tf_op jit(solution)/shard_map/pallas_call | solution.py:244
  126.7 3.7 %collective-permute-start.17 = (bf16[4,128,128]{2,1,0:T(8,128)(2,1)S(1)}, bf16[4,128,128]{2,1,0:T(8,128)(2,1)S(1)}, u32[]{:S(2)}, u32[]{:S(2)}) collective-permute-start(bf16[4,128,128]{2,1,0:T(8,128)(2,1)S(1)} %copy-done.16), channel_id=1, source_target_pairs={{0,28},{1,29},{2,30},{3,31},{4,24},{5,25},{6,26},{7,27},{8,4},{9,5... | collective-permute-start | bytes 393224 | tf_op jit(solution)/shard_map/ppermute | solution.py:310
  133.0 2.5 %shard_map.74 = (bf16[32,128,512]{2,1,0:T(8,128)(2,1)}, f32[32,128,1024]{2,1,0:T(8,128)}) custom-call(s32[4]{0:T(128)S(1)} %get-tuple-element.107.position, bf16[4,128,128]{2,1,0:T(8,128)(2,1)S(1)} %collective-permute-done.22.refs_0_, bf16[4,128,128]{2,1,0:T(8,128)(2,1)S(1)} %collective-permute-done.23.refs_1_, ...), custom_call_target="tpu_custom_call", output_to_operand_aliasing={{0}: (6, {}), {1}: (7, {})} | custom-call | flops 536870912 | bytes 4000000 | tf_op jit(solution)/shard_map/pallas_call | solution.py:244
  135.8 2.5 %shard_map.75 = (bf16[32,128,512]{2,1,0:T(8,128)(2,1)}, f32[32,128,1024]{2,1,0:T(8,128)}) custom-call(s32[4]{0:T(128)S(1)} %get-tuple-element.108.position, bf16[4,128,128]{2,1,0:T(8,128)(2,1)S(1)} %collective-permute-done.18.refs_0_, bf16[4,128,128]{2,1,0:T(8,128)(2,1)S(1)} %collective-permute-done.19.refs_1_, ...), custom_call_target="tpu_custom_call", output_to_operand_aliasing={{0}: (6, {}), {1}: (7, {})} | custom-call | flops 536870912 | bytes 4000000 | tf_op jit(solution)/shard_map/pallas_call | solution.py:244
  143.1 2.6 %collective-permute-start.5 = (bf16[4,128,128]{2,1,0:T(8,128)(2,1)S(1)}, bf16[4,128,128]{2,1,0:T(8,128)(2,1)S(1)}, u32[]{:S(2)}, u32[]{:S(2)}) collective-permute-start(bf16[4,128,128]{2,1,0:T(8,128)(2,1)S(1)} %copy-done.6), channel_id=1, source_target_pairs={{0,31},{1,24},{2,25},{3,26},{4,27},{5,28},{6,29},{7,30},{8,7},{9,0... | collective-permute-start | bytes 393224 | tf_op jit(solution)/shard_map/ppermute | solution.py:310
  148.1 3.0 %shard_map.77 = (bf16[32,128,512]{2,1,0:T(8,128)(2,1)}, f32[32,128,1024]{2,1,0:T(8,128)}) custom-call(s32[4]{0:T(128)S(1)} %get-tuple-element.110.position, bf16[4,128,128]{2,1,0:T(8,128)(2,1)} %collective-permute-done.10.refs_0_, bf16[4,128,128]{2,1,0:T(8,128)(2,1)} %collective-permute-done.11.refs_1_, ...), custom_call_target="tpu_custom_call", output_to_operand_aliasing={{0}: (6, {}), {1}: (7, {})} | custom-call | flops 536870912 | bytes 4000000 | tf_op jit(solution)/shard_map/pallas_call | solution.py:244
  (143 shorter events, 54.6 us)
Async XLA Ops:
  4.9 24.7 %collective-permute-start = (bf16[2,2048,128]{2,1,0:T(8,128)(2,1)}, bf16[2,2048,128]{2,1,0:T(8,128)(2,1)S(1)}, u32[]{:S(2)}, u32[]{:S(2)}) collective-permute-start(bf16[2,2048,128]{2,1,0:T(8,128)(2,1)} %get-tuple-element.53), channel_id=1, source_target_pairs={{7,0},{0,1},{1,2},{2,3},{3,4},{4,5},{5,6},{6,7},{15,8},{8,9},{9,10... | collective-permute-start | bytes 3145736 | tf_op jit(solution)/shard_map/ppermute | solution.py:20
  5.4 25.8 %collective-permute-start.1 = (bf16[2,2048,128]{2,1,0:T(8,128)(2,1)}, bf16[2,2048,128]{2,1,0:T(8,128)(2,1)S(1)}, u32[]{:S(2)}, u32[]{:S(2)}) collective-permute-start(bf16[2,2048,128]{2,1,0:T(8,128)(2,1)} %get-tuple-element.54), channel_id=1, source_target_pairs={{1,0},{2,1},{3,2},{4,3},{5,4},{6,5},{7,6},{0,7},{9,8},{10,9},{11,1... | collective-permute-start | bytes 3145736 | tf_op jit(solution)/shard_map/ppermute | solution.py:20
  53.9 15.8 %collective-permute-start.8 = (bf16[4,128,128]{2,1,0:T(8,128)(2,1)}, bf16[4,128,128]{2,1,0:T(8,128)(2,1)S(1)}, u32[]{:S(2)}, u32[]{:S(2)}) collective-permute-start(bf16[4,128,128]{2,1,0:T(8,128)(2,1)} %get-tuple-element.61), channel_id=1, source_target_pairs={{0,22},{1,23},{2,16},{3,17},{4,18},{5,19},{6,20},{7,21},{8,30},{9,... | collective-permute-start | bytes 393224 | tf_op jit(solution)/shard_map/ppermute | solution.py:310
  56.3 16.0 %collective-permute-start.10 = (bf16[4,128,128]{2,1,0:T(8,128)(2,1)}, bf16[4,128,128]{2,1,0:T(8,128)(2,1)}, u32[]{:S(2)}, u32[]{:S(2)}) collective-permute-start(bf16[4,128,128]{2,1,0:T(8,128)(2,1)} %get-tuple-element.63), channel_id=1, source_target_pairs={{0,5},{1,6},{2,7},{3,0},{4,1},{5,2},{6,3},{7,4},{8,13},{9,14},{10,... | collective-permute-start | bytes 393224 | tf_op jit(solution)/shard_map/ppermute | solution.py:310
  57.2 15.1 %collective-permute-start.11 = (bf16[4,128,128]{2,1,0:T(8,128)(2,1)}, bf16[4,128,128]{2,1,0:T(8,128)(2,1)}, u32[]{:S(2)}, u32[]{:S(2)}) collective-permute-start(bf16[4,128,128]{2,1,0:T(8,128)(2,1)} %get-tuple-element.64), channel_id=1, source_target_pairs={{0,13},{1,14},{2,15},{3,8},{4,9},{5,10},{6,11},{7,12},{8,21},{9,22... | collective-permute-start | bytes 393224 | tf_op jit(solution)/shard_map/ppermute | solution.py:310
  58.8 16.1 %collective-permute-start.12 = (bf16[4,128,128]{2,1,0:T(8,128)(2,1)}, bf16[4,128,128]{2,1,0:T(8,128)(2,1)}, u32[]{:S(2)}, u32[]{:S(2)}) collective-permute-start(bf16[4,128,128]{2,1,0:T(8,128)(2,1)} %get-tuple-element.65), channel_id=1, source_target_pairs={{0,21},{1,22},{2,23},{3,16},{4,17},{5,18},{6,19},{7,20},{8,29},{9,... | collective-permute-start | bytes 393224 | tf_op jit(solution)/shard_map/ppermute | solution.py:310
  63.8 15.4 %collective-permute-start.13 = (bf16[4,128,128]{2,1,0:T(8,128)(2,1)}, bf16[4,128,128]{2,1,0:T(8,128)(2,1)S(1)}, u32[]{:S(2)}, u32[]{:S(2)}) collective-permute-start(bf16[4,128,128]{2,1,0:T(8,128)(2,1)} %copy-done.35), channel_id=1, source_target_pairs={{0,29},{1,30},{2,31},{3,24},{4,25},{5,26},{6,27},{7,28},{8,5},{9,6... | collective-permute-start | bytes 393224 | tf_op jit(solution)/shard_map/ppermute | solution.py:310
  72.3 14.1 %collective-permute-start.19 = (bf16[4,128,128]{2,1,0:T(8,128)(2,1)}, bf16[4,128,128]{2,1,0:T(8,128)(2,1)S(1)}, u32[]{:S(2)}, u32[]{:S(2)}) collective-permute-start(bf16[4,128,128]{2,1,0:T(8,128)(2,1)} %copy-done.33), channel_id=1, source_target_pairs={{0,11},{1,12},{2,13},{3,14},{4,15},{5,8},{6,9},{7,10},{8,19},{9,20... | collective-permute-start | bytes 393224 | tf_op jit(solution)/shard_map/ppermute | solution.py:310
  72.3 14.1 %collective-permute-start.20 = (bf16[4,128,128]{2,1,0:T(8,128)(2,1)}, bf16[4,128,128]{2,1,0:T(8,128)(2,1)S(1)}, u32[]{:S(2)}, u32[]{:S(2)}) collective-permute-start(bf16[4,128,128]{2,1,0:T(8,128)(2,1)} %copy-done.32), channel_id=1, source_target_pairs={{0,19},{1,20},{2,21},{3,22},{4,23},{5,16},{6,17},{7,18},{8,27},{9,... | collective-permute-start | bytes 393224 | tf_op jit(solution)/shard_map/ppermute | solution.py:310
  74.9 13.9 %collective-permute-start.22 = (bf16[4,128,128]{2,1,0:T(8,128)(2,1)}, bf16[4,128,128]{2,1,0:T(8,128)(2,1)S(1)}, u32[]{:S(2)}, u32[]{:S(2)}) collective-permute-start(bf16[4,128,128]{2,1,0:T(8,128)(2,1)} %copy-done.31), channel_id=1, source_target_pairs={{0,2},{1,3},{2,4},{3,5},{4,6},{5,7},{6,0},{7,1},{8,10},{9,11},{10,... | collective-permute-start | bytes 393224 | tf_op jit(solution)/shard_map/ppermute | solution.py:310
  86.4 17.5 %collective-permute-start.30 = (bf16[4,128,128]{2,1,0:T(8,128)(2,1)S(1)}, bf16[4,128,128]{2,1,0:T(8,128)(2,1)S(1)}, u32[]{:S(2)}, u32[]{:S(2)}) collective-permute-start(bf16[4,128,128]{2,1,0:T(8,128)(2,1)S(1)} %get-tuple-element.85), channel_id=1, source_target_pairs={{0,8},{1,9},{2,10},{3,11},{4,12},{5,13},{6,14},{7,15},{8,16},{9,17... | collective-permute-start | bytes 393224 | tf_op jit(solution)/shard_map/ppermute | solution.py:310
  88.8 20.2 %collective-permute-start.31 = (bf16[4,128,128]{2,1,0:T(8,128)(2,1)S(1)}, bf16[4,128,128]{2,1,0:T(8,128)(2,1)S(1)}, u32[]{:S(2)}, u32[]{:S(2)}) collective-permute-start(bf16[4,128,128]{2,1,0:T(8,128)(2,1)S(1)} %get-tuple-element.86), channel_id=1, source_target_pairs={{0,16},{1,17},{2,18},{3,19},{4,20},{5,21},{6,22},{7,23},{8,24},{9,... | collective-permute-start | bytes 393224 | tf_op jit(solution)/shard_map/ppermute | solution.py:310
  90.0 33.6 %collective-permute-start.26 = (bf16[4,128,128]{2,1,0:T(8,128)(2,1)}, bf16[4,128,128]{2,1,0:T(8,128)(2,1)S(1)}, u32[]{:S(2)}, u32[]{:S(2)}) collective-permute-start(bf16[4,128,128]{2,1,0:T(8,128)(2,1)} %copy-done.27), channel_id=1, source_target_pairs={{0,1},{1,2},{2,3},{3,4},{4,5},{5,6},{6,7},{7,0},{8,9},{9,10},{10,1... | collective-permute-start | bytes 393224 | tf_op jit(solution)/shard_map/ppermute | solution.py:310
  95.4 28.3 %collective-permute-start.27 = (bf16[4,128,128]{2,1,0:T(8,128)(2,1)}, bf16[4,128,128]{2,1,0:T(8,128)(2,1)S(1)}, u32[]{:S(2)}, u32[]{:S(2)}) collective-permute-start(bf16[4,128,128]{2,1,0:T(8,128)(2,1)} %copy-done.26), channel_id=1, source_target_pairs={{0,9},{1,10},{2,11},{3,12},{4,13},{5,14},{6,15},{7,8},{8,17},{9,18... | collective-permute-start | bytes 393224 | tf_op jit(solution)/shard_map/ppermute | solution.py:310
  98.7 26.2 %collective-permute-start.28 = (bf16[4,128,128]{2,1,0:T(8,128)(2,1)}, bf16[4,128,128]{2,1,0:T(8,128)(2,1)S(1)}, u32[]{:S(2)}, u32[]{:S(2)}) collective-permute-start(bf16[4,128,128]{2,1,0:T(8,128)(2,1)} %copy-done.25), channel_id=1, source_target_pairs={{0,17},{1,18},{2,19},{3,20},{4,21},{5,22},{6,23},{7,16},{8,25},{9,... | collective-permute-start | bytes 393224 | tf_op jit(solution)/shard_map/ppermute | solution.py:310
  103.8 22.9 %collective-permute-start.29 = (bf16[4,128,128]{2,1,0:T(8,128)(2,1)}, bf16[4,128,128]{2,1,0:T(8,128)(2,1)S(1)}, u32[]{:S(2)}, u32[]{:S(2)}) collective-permute-start(bf16[4,128,128]{2,1,0:T(8,128)(2,1)} %copy-done.24), channel_id=1, source_target_pairs={{0,25},{1,26},{2,27},{3,28},{4,29},{5,30},{6,31},{7,24},{8,1},{9,2... | collective-permute-start | bytes 393224 | tf_op jit(solution)/shard_map/ppermute | solution.py:310
  117.4 18.1 %collective-permute-start.21 = (bf16[4,128,128]{2,1,0:T(8,128)(2,1)}, bf16[4,128,128]{2,1,0:T(8,128)(2,1)S(1)}, u32[]{:S(2)}, u32[]{:S(2)}) collective-permute-start(bf16[4,128,128]{2,1,0:T(8,128)(2,1)} %copy-done.23), channel_id=1, source_target_pairs={{0,27},{1,28},{2,29},{3,30},{4,31},{5,24},{6,25},{7,26},{8,3},{9,4... | collective-permute-start | bytes 393224 | tf_op jit(solution)/shard_map/ppermute | solution.py:310
  123.6 14.7 %collective-permute-start.14 = (bf16[4,128,128]{2,1,0:T(8,128)(2,1)S(1)}, bf16[4,128,128]{2,1,0:T(8,128)(2,1)S(1)}, u32[]{:S(2)}, u32[]{:S(2)}) collective-permute-start(bf16[4,128,128]{2,1,0:T(8,128)(2,1)S(1)} %copy-done.22), channel_id=1, source_target_pairs={{0,4},{1,5},{2,6},{3,7},{4,0},{5,1},{6,2},{7,3},{8,12},{9,13},{10,... | collective-permute-start | bytes 393224 | tf_op jit(solution)/shard_map/ppermute | solution.py:310
  123.7 14.9 %collective-permute-start.15 = (bf16[4,128,128]{2,1,0:T(8,128)(2,1)S(1)}, bf16[4,128,128]{2,1,0:T(8,128)(2,1)S(1)}, u32[]{:S(2)}, u32[]{:S(2)}) collective-permute-start(bf16[4,128,128]{2,1,0:T(8,128)(2,1)S(1)} %copy-done.20), channel_id=1, source_target_pairs={{0,12},{1,13},{2,14},{3,15},{4,8},{5,9},{6,10},{7,11},{8,20},{9,21... | collective-permute-start | bytes 393224 | tf_op jit(solution)/shard_map/ppermute | solution.py:310
  124.8 15.9 %collective-permute-start.16 = (bf16[4,128,128]{2,1,0:T(8,128)(2,1)S(1)}, bf16[4,128,128]{2,1,0:T(8,128)(2,1)S(1)}, u32[]{:S(2)}, u32[]{:S(2)}) collective-permute-start(bf16[4,128,128]{2,1,0:T(8,128)(2,1)S(1)} %copy-done.18), channel_id=1, source_target_pairs={{0,20},{1,21},{2,22},{3,23},{4,16},{5,17},{6,18},{7,19},{8,28},{9,... | collective-permute-start | bytes 393224 | tf_op jit(solution)/shard_map/ppermute | solution.py:310
  126.7 16.4 %collective-permute-start.17 = (bf16[4,128,128]{2,1,0:T(8,128)(2,1)S(1)}, bf16[4,128,128]{2,1,0:T(8,128)(2,1)S(1)}, u32[]{:S(2)}, u32[]{:S(2)}) collective-permute-start(bf16[4,128,128]{2,1,0:T(8,128)(2,1)S(1)} %copy-done.16), channel_id=1, source_target_pairs={{0,28},{1,29},{2,30},{3,31},{4,24},{5,25},{6,26},{7,27},{8,4},{9,5... | collective-permute-start | bytes 393224 | tf_op jit(solution)/shard_map/ppermute | solution.py:310
  135.5 15.6 %collective-permute-start.9 = (bf16[4,128,128]{2,1,0:T(8,128)(2,1)S(1)}, bf16[4,128,128]{2,1,0:T(8,128)(2,1)S(1)}, u32[]{:S(2)}, u32[]{:S(2)}) collective-permute-start(bf16[4,128,128]{2,1,0:T(8,128)(2,1)S(1)} %copy-done.14), channel_id=1, source_target_pairs={{0,30},{1,31},{2,24},{3,25},{4,26},{5,27},{6,28},{7,29},{8,6},{9,7... | collective-permute-start | bytes 393224 | tf_op jit(solution)/shard_map/ppermute | solution.py:310
  138.3 15.3 %collective-permute-start.2 = (bf16[4,128,128]{2,1,0:T(8,128)(2,1)S(1)}, bf16[4,128,128]{2,1,0:T(8,128)(2,1)S(1)}, u32[]{:S(2)}, u32[]{:S(2)}) collective-permute-start(bf16[4,128,128]{2,1,0:T(8,128)(2,1)S(1)} %copy-done.12), channel_id=1, source_target_pairs={{0,7},{1,0},{2,1},{3,2},{4,3},{5,4},{6,5},{7,6},{8,15},{9,8},{10,9... | collective-permute-start | bytes 393224 | tf_op jit(solution)/shard_map/ppermute | solution.py:310
  138.6 15.1 %collective-permute-start.3 = (bf16[4,128,128]{2,1,0:T(8,128)(2,1)S(1)}, bf16[4,128,128]{2,1,0:T(8,128)(2,1)S(1)}, u32[]{:S(2)}, u32[]{:S(2)}) collective-permute-start(bf16[4,128,128]{2,1,0:T(8,128)(2,1)S(1)} %copy-done.10), channel_id=1, source_target_pairs={{0,15},{1,8},{2,9},{3,10},{4,11},{5,12},{6,13},{7,14},{8,23},{9,16... | collective-permute-start | bytes 393224 | tf_op jit(solution)/shard_map/ppermute | solution.py:310
  (48 other events, 477.3 us)

commit v3 on v2

v3 whole, which is shorter than its diff:
```python
import functools

import jax
import jax.numpy as jnp
from jax import lax
from jax.experimental import pallas as pl
from jax.experimental.pallas import tpu as pltpu
from jax.sharding import PartitionSpec as P


R = 8192
BLOCK = 128
LATE = 1
DIRECT = 2
ALIGN = 16
MIB = 1 << 20


def from_behind(block, axis, distance):
    devices = range(lax.axis_size(axis))
    route = [((i - distance) % len(devices), i) for i in devices]
    return lax.ppermute(block, axis, route)


def any_space():
    return pl.BlockSpec(memory_space=pl.ANY)


def in_hbm():
    return pl.BlockSpec(memory_space=pltpu.HBM)


def smem():
    return pl.BlockSpec(memory_space=pltpu.SMEM)


def vmem():
    return pl.BlockSpec(memory_space=pltpu.VMEM)


def my_span(offsets, m):
    t = lax.axis_index("tensor")
    return offsets[m, t] - t * R, offsets[m, t + 1] - t * R


def edges_kernel(offsets, embed, head, lead_out, trail_out, rows, wide, sems):
    quarter = lead_out.shape[1]
    raws = [embed, head]
    copies = []
    for m in range(2):
        first = (R - my_span(offsets, m)[0]) & -ALIGN
        window = pl.ds(pl.multiple_of(first, ALIGN), quarter + ALIGN)
        lead = pltpu.make_async_copy(
            raws[m].at[pl.ds(0, quarter)], rows.at[2 * m, pl.ds(0, quarter)], sems.at[2 * m]
        )
        trail = pltpu.make_async_copy(raws[m].at[window], rows.at[2 * m + 1], sems.at[2 * m + 1])
        lead.start()
        trail.start()
        copies.append((lead, trail))
    blocks = quarter // BLOCK
    for m in range(2):
        lead, trail = copies[m]
        before, after = my_span(offsets, m)
        lead.wait()
        count = jnp.clip(-before, 0, quarter)
        used = (count + BLOCK - 1) >> log2(BLOCK)

        def widen_lead(i, _):
            at = pl.multiple_of(i * BLOCK, BLOCK)
            wide[pl.ds(quarter + at, BLOCK), :] = rows[2 * m, pl.ds(at, BLOCK), :].astype(jnp.float32)
            return _

        lax.fori_loop(0, used, widen_lead, 0)

        def put_lead(i, _):
            at = pl.multiple_of(i * BLOCK, BLOCK)
            lead_out[m, pl.ds(at, BLOCK), :] = wide[pl.ds(count + at, BLOCK), :].astype(jnp.bfloat16)
            return _

        lax.fori_loop(blocks - used, blocks, put_lead, 0)
        trail.wait()
        shift = (R - before) & (ALIGN - 1)
        used = (jnp.clip(after - R, 0, quarter) + BLOCK - 1) >> log2(BLOCK)

        def widen_trail(i, _):
            at = pl.multiple_of(i * BLOCK, BLOCK)
            wide[pl.ds(at, BLOCK), :] = rows[2 * m + 1, pl.ds(at, BLOCK), :].astype(jnp.float32)
            return _

        lax.fori_loop(0, jnp.minimum(used + 1, blocks), widen_trail, 0)

        @pl.when(used == blocks)
        def _last():
            wide[pl.ds(quarter, ALIGN), :] = rows[2 * m + 1, pl.ds(quarter, ALIGN), :].astype(jnp.float32)

        def put_trail(i, _):
            at = pl.multiple_of(i * BLOCK, BLOCK)
            trail_out[m, pl.ds(at, BLOCK), :] = wide[pl.ds(shift + at, BLOCK), :].astype(jnp.bfloat16)
            return _

        lax.fori_loop(0, used, put_trail, 0)


def cut_edges(offsets, embed, head, quarter):
    width = embed.shape[1]
    shape = jax.ShapeDtypeStruct((2, quarter, width), embed.dtype)
    return pl.pallas_call(
        edges_kernel,
        out_shape=(shape, shape),
        in_specs=[smem(), in_hbm(), in_hbm()],
        out_specs=[vmem()] * 2,
        scratch_shapes=[
            pltpu.VMEM((4, quarter + ALIGN, width), embed.dtype),
            pltpu.VMEM((2 * quarter, width), jnp.float32),
            pltpu.SemaphoreType.DMA((4,)),
        ],
        compiler_params=pltpu.CompilerParams(vmem_limit_bytes=61 * MIB),
    )(offsets, embed, head)


def log2(size):
    assert size & (size - 1) == 0
    return size.bit_length() - 1


def wrap(index, size):
    return index & (size - 1)


def target(s, u, n_data, n_tensor):
    z = wrap(lax.axis_index("dp") + s, n_data)
    t = wrap(lax.axis_index("tensor") + u, n_tensor)
    return z * n_tensor + t


def split_block(block):
    bits = log2(R // BLOCK)
    return block >> bits, (block & (R // BLOCK - 1)) * BLOCK


def plan_kernel(n_data, n_tensor, per_pair, offsets, slots, plan):
    devices, count = slots.shape
    per_rank = R // BLOCK
    total = per_rank * n_tensor
    slot = slots[...]
    matrix = slot >> log2(total)
    rest = slot & (total - 1)
    source = rest >> log2(per_rank)
    k = rest & (per_rank - 1)
    local = jnp.zeros_like(slot)
    for m in range(2):
        for t in range(n_tensor):
            begin = offsets[m, t] - t * R
            end = offsets[m, t + 1] - t * R
            inside = (k * BLOCK >= begin) & (k * BLOCK + BLOCK <= end)
            here = (source == t) & (matrix == m)
            local = jnp.where(here & inside, 1, local)
    column = lax.broadcasted_iota(jnp.int32, slot.shape, 1)
    lowest = source * (2 * count)
    key = lowest + (1 - local) * count + column
    rank = jnp.zeros_like(slot)
    for j in range(count):
        other = key[:, j : j + 1]
        rank += jnp.where((other >= lowest) & (other < key), 1, 0)
    my_t = lax.axis_index("tensor")
    me = lax.axis_index("dp") * n_tensor + my_t
    lane = lax.broadcasted_iota(jnp.int32, plan.shape, 1)
    row = lax.broadcasted_iota(jnp.int32, slot.shape, 0)
    out = jnp.zeros(plan.shape, jnp.int32)
    block = matrix * per_rank + k
    for r in range(per_pair):
        mine = (source == my_t) & (rank == r)
        picked = jnp.sum(jnp.where(mine, block, 0), axis=1, keepdims=True)
        out = jnp.where(lane == r, picked, out)
        if r == 0:
            flag = jnp.sum(jnp.where(mine, local, 0), axis=1, keepdims=True)
            out = jnp.where(lane == per_pair, flag, out)
    hops = (my_t - source) & (n_tensor - 1)
    order = jnp.where(row == me, hops * per_pair + rank, 0)
    order = jnp.sum(order, axis=0, keepdims=True)
    found = jnp.where(order == row, column, 0)
    out = jnp.where(lane == per_pair + 1, jnp.sum(found, axis=1, keepdims=True), out)
    empty = jnp.zeros(plan.shape, jnp.int32)
    for t in range(n_tensor):
        has = jnp.max(jnp.where(source == t, local, 0), axis=1, keepdims=True)
        empty = jnp.where(lane == t, 1 - has, empty)
    worst = jnp.zeros((1, 1), jnp.int32)
    for z in range(n_data):
        layer = jnp.sum(empty[z * n_tensor : (z + 1) * n_tensor], axis=0, keepdims=True)
        worst = jnp.maximum(worst, jnp.max(layer, axis=1, keepdims=True))
    plan[...] = jnp.where(lane == per_pair + 2, worst, out)


def make_plan(offsets, slot_table, n_data, n_tensor, per_pair):
    devices = n_data * n_tensor
    return pl.pallas_call(
        functools.partial(plan_kernel, n_data, n_tensor, per_pair),
        out_shape=jax.ShapeDtypeStruct((devices, 128), jnp.int32),
        in_specs=[smem(), vmem()],
        out_specs=vmem(),
        compiler_params=pltpu.CompilerParams(vmem_limit_bytes=4 * MIB),
    )(offsets, slot_table.reshape(devices, -1))


class Layout:
    def __init__(self, n_data, n_tensor, per_pair):
        self.n_data, self.n_tensor, self.per_pair = n_data, n_tensor, per_pair
        self.staged = per_pair > DIRECT + 1
        self.direct_ranks = DIRECT if self.staged else per_pair

    def target(self, s, u):
        return target(s, u, self.n_data, self.n_tensor)

    def along_z(self, s, rank):
        return (0, self.n_tensor, lambda plan, i: plan[self.target(s, i), rank])

    def late_block(self, plan, s):
        chosen = self.target(s, 0)
        for u in reversed(range(self.n_tensor)):
            to = self.target(s, u)
            chosen = jnp.where(plan[to, self.per_pair] == 0, to, chosen)
        return plan[chosen, 0]

    def late(self):
        return [
            [(0, LATE, lambda plan, i, s=s: self.late_block(plan, s))] for s in range(self.n_data)
        ]

    def stage(self, rank):
        return [[self.along_z(s, rank)] for s in range(self.n_data)]

    def direct(self):
        count, first = self.direct_ranks, self.per_pair - self.direct_ranks
        bits = log2(count)
        which = lambda plan, i: plan[i >> bits, first + (i & (count - 1))]
        return [[(0, self.n_data * self.n_tensor * count, which)]]

    def size(self, parts):
        return sum(part[1] for part in parts)


def pack_kernel(arrays, plan, offsets, embed, head, *refs):
    outs, (windows, wide, sems) = refs[: len(arrays)], refs[len(arrays) :]
    height = embed.shape[0]

    t = lax.axis_index("tensor")
    begins = [offsets[m, t] - t * R for m in range(2)]

    def where_from(block):
        m, row = split_block(block)
        start = row - jnp.where(m == 0, begins[0], begins[1])
        start = jnp.minimum(jnp.maximum(start + BLOCK, 0), height - ALIGN)
        first = jnp.maximum((start & -ALIGN) - BLOCK, 0)
        return m, start - BLOCK, pl.multiple_of(first, ALIGN)

    at = 0
    for parts in arrays:
        for begin, count, which in parts:

            def fetch(i, _, at=at, which=which):
                m, _start, first = where_from(which(plan, i))
                for k, raw in enumerate([embed, head]):

                    @pl.when(m == k)
                    def _fetch(raw=raw):
                        pltpu.make_async_copy(
                            raw.at[pl.ds(first, BLOCK + ALIGN)], windows.at[at + i], sems.at[at + i]
                        ).start()

                return _

            lax.fori_loop(0, count, fetch, 0)
            at += count
    at = 0
    for parts, out in zip(arrays, outs):
        for begin, count, which in parts:

            def shift(i, _, at=at, which=which, out=out, begin=begin):
                m, start, first = where_from(which(plan, i))
                pltpu.make_async_copy(
                    embed.at[pl.ds(0, BLOCK + ALIGN)], windows.at[at + i], sems.at[at + i]
                ).wait()
                slot = i & 1
                wide[slot, pl.ds(BLOCK, BLOCK + ALIGN), :] = windows[at + i].astype(jnp.float32)
                moved = wide[slot, pl.ds(BLOCK + start - first, BLOCK), :]
                out[begin + i] = moved.astype(jnp.bfloat16)
                return _

            lax.fori_loop(0, count, shift, 0)
            at += count


def pack(layout, arrays, plan, offsets, embed, head, limit):
    width = embed.shape[1]
    total = sum(layout.size(parts) for parts in arrays)
    return pl.pallas_call(
        functools.partial(pack_kernel, arrays),
        out_shape=[
            jax.ShapeDtypeStruct((layout.size(parts), BLOCK, width), embed.dtype) for parts in arrays
        ],
        in_specs=[smem(), smem(), in_hbm(), in_hbm()],
        out_specs=[vmem()] * len(arrays),
        scratch_shapes=[
            pltpu.VMEM((total, BLOCK + ALIGN, width), embed.dtype),
            pltpu.VMEM((2, 2 * BLOCK + ALIGN, width), jnp.float32),
            pltpu.SemaphoreType.DMA((total,)),
        ],
        compiler_params=pltpu.CompilerParams(vmem_limit_bytes=limit * MIB),
        cost_estimate=pl.CostEstimate(flops=total * 30_000_000, bytes_accessed=total * 70_000, transcendentals=0),
    )(plan, offsets, embed, head)


def overlay_kernel(arrays, plan, offsets, *refs):
    packed, left, right, outs = refs[: len(arrays)], refs[-len(arrays) - 2], refs[-len(arrays) - 1], refs[-len(arrays) :]
    quarter = left.shape[1]
    t = lax.axis_index("tensor")
    begins = [offsets[m, t] - t * R for m in range(2)]
    ends = [offsets[m, t + 1] - t * R for m in range(2)]
    for parts, source, out in zip(arrays, packed, outs):
        out[...] = source[...]
        for begin, count, which in parts:

            def fix(i, _, begin=begin, which=which, out=out):
                m, first = split_block(which(plan, i))
                before = jnp.where(m == 0, begins[0], begins[1])
                after = jnp.where(m == 0, ends[0], ends[1])

                @pl.when(first < before)
                def _left():
                    row = first + lax.broadcasted_iota(jnp.int32, (BLOCK, 1), 0)
                    edge = left[m, pl.ds(pl.multiple_of(first, BLOCK), BLOCK), :]
                    out[begin + i] = jnp.where(row < before, edge, out[begin + i])

                @pl.when(first + BLOCK > after)
                def _right():
                    row = first + lax.broadcasted_iota(jnp.int32, (BLOCK, 1), 0)
                    at = pl.multiple_of(first - (R - quarter), BLOCK)
                    edge = right[m, pl.ds(at, BLOCK), :]
                    out[begin + i] = jnp.where(row >= after, edge, out[begin + i])

                return _

            lax.fori_loop(0, count, fix, 0)


def overlay(layout, arrays, plan, offsets, packed, left, right):
    return pl.pallas_call(
        functools.partial(overlay_kernel, arrays),
        out_shape=[
            jax.ShapeDtypeStruct((layout.size(parts),) + packed[0].shape[1:], left.dtype)
            for parts in arrays
        ],
        in_specs=[smem()] * 2 + [vmem()] * (len(packed) + 2),
        out_specs=[vmem()] * len(arrays),
        compiler_params=pltpu.CompilerParams(vmem_limit_bytes=16 * MIB),
        cost_estimate=pl.CostEstimate(flops=1_000_000_000, bytes_accessed=4_000_000, transcendentals=0),
    )(plan, offsets, *packed, left, right)


def forward_kernel(layout, ranks, plan, *refs):
    n_data, n_tensor, per_pair = layout.n_data, layout.n_tensor, layout.per_pair
    outs = refs[-n_tensor:]
    for u in range(n_tensor):
        to = layout.target(0, u)
        swap = (plan[to, per_pair] == 0) & (plan[0, per_pair + 2] <= LATE)
        for k, rank in enumerate(ranks):
            for s in range(n_data):
                if rank == 0:

                    @pl.when(swap)
                    def _late(s=s, u=u):
                        outs[u][s] = refs[n_data + s][0]

                    @pl.when(jnp.logical_not(swap))
                    def _early(s=s, u=u):
                        outs[u][s] = refs[s][u]

                else:
                    outs[u][k * n_data + s] = refs[k * n_data + s][u]


def gather_forward(layout, ranks, plan, arrays):
    n_tensor = layout.n_tensor
    _, _, width = arrays[0].shape
    shape = jax.ShapeDtypeStruct((len(ranks) * layout.n_data, BLOCK, width), arrays[0].dtype)
    return pl.pallas_call(
        functools.partial(forward_kernel, layout, ranks),
        out_shape=[shape] * n_tensor,
        in_specs=[smem()] + [vmem()] * len(arrays),
        out_specs=[vmem()] * n_tensor,
        compiler_params=pltpu.CompilerParams(vmem_limit_bytes=12 * MIB),
        cost_estimate=pl.CostEstimate(flops=1_000_000_000, bytes_accessed=2_000_000, transcendentals=0),
    )(plan, *arrays)


def store_kernel(layout, ranks, direct, count, plan, *refs):
    n_data, n_tensor, per_pair = layout.n_data, layout.n_tensor, layout.per_pair
    incoming, probe = refs[:count], refs[count]
    stored, sketch, full, product, sems = refs[-5:]
    width = incoming[0].shape[-1]
    slots = len(ranks) * n_tensor
    step = min(4, slots)
    copies = []
    for begin in range(0, slots, step):
        for i in range(begin, begin + step):
            k, hop = i // n_tensor, i % n_tensor
            for s in range(n_data):
                if direct:
                    full[i, :, s * width : (s + 1) * width] = incoming[0][s, hop, k]
                else:
                    column = wrap(lax.axis_index("dp") - s + n_data, n_data)
                    columns = pl.ds(pl.multiple_of(column * width, width), width)
                    full[i, :, columns] = incoming[hop][k * n_data + s]
        span = pl.ds(begin, step)
        rows = full[span].reshape(step * BLOCK, n_data * width)
        dot = jnp.dot(rows, probe[...], preferred_element_type=jnp.float32)
        product[span] = dot.reshape(step, BLOCK, probe.shape[1])
        for i in range(begin, begin + step):
            k, u = i // n_tensor, i % n_tensor
            if direct:
                u = wrap(lax.axis_index("tensor") - u + n_tensor, n_tensor)
            slot = plan[u * per_pair + ranks[k], per_pair + 1]
            copies.append(pltpu.make_async_copy(full.at[i], stored.at[slot], sems.at[2 * i]))
            copies.append(pltpu.make_async_copy(product.at[i], sketch.at[slot], sems.at[2 * i + 1]))
            copies[-2].start()
            copies[-1].start()
    for copy in copies:
        copy.wait()


def store_ranks(layout, ranks, direct, plan, incoming, probe, previous):
    n_data, n_tensor, per_pair = layout.n_data, layout.n_tensor, layout.per_pair
    count = len(incoming)
    slots = len(ranks) * n_tensor
    columns = n_data * incoming[0].shape[-1]
    sketch_width = probe.shape[1]
    slot_count = n_tensor * per_pair
    out_shape = [
        jax.ShapeDtypeStruct((slot_count, BLOCK, columns), incoming[0].dtype),
        jax.ShapeDtypeStruct((slot_count, BLOCK, sketch_width), jnp.float32),
    ]
    held = [] if previous is None else list(previous)
    return pl.pallas_call(
        functools.partial(store_kernel, layout, ranks, direct, count),
        out_shape=out_shape,
        in_specs=[smem()] + [vmem()] * (count + 1) + [any_space() for _ in held],
        out_specs=[any_space(), any_space()],
        scratch_shapes=[
            pltpu.VMEM((slots, BLOCK, columns), incoming[0].dtype),
            pltpu.VMEM((slots, BLOCK, sketch_width), jnp.float32),
            pltpu.SemaphoreType.DMA((2 * slots,)),
        ],
        compiler_params=pltpu.CompilerParams(vmem_limit_bytes=(8 + 7 * slots // 8) * MIB),
        input_output_aliases={count + 2: 0, count + 3: 1} if held else {},
        cost_estimate=pl.CostEstimate(
            flops=2 * slots * BLOCK * columns * sketch_width,
            bytes_accessed=800_000 * slots,
            transcendentals=0,
        ),
    )(plan, *incoming, probe, *held)


def shards(embed_rows, head_rows, row_offsets, slot_table, probe):
    n_tensor = lax.axis_size("tensor")
    n_data = lax.axis_size("dp")
    quarter = R // 4
    devices = n_tensor * n_data
    per_pair = slot_table.shape[0] // devices // n_tensor
    layout = Layout(n_data, n_tensor, per_pair)

    lead_part, trail_part = cut_edges(row_offsets, embed_rows, head_rows, quarter)
    from_right = from_behind(lead_part, "tensor", -1)
    from_left = from_behind(trail_part, "tensor", 1)
    plan = make_plan(row_offsets, slot_table, n_data, n_tensor, per_pair)

    def move(block, s):
        if s == 0:
            return block
        return from_behind(block, "dp", s)

    def pack_all(arrays, limit):
        return pack(layout, arrays, plan, row_offsets, embed_rows, head_rows, limit)

    def overlay_all(arrays, packed):
        return overlay(layout, arrays, plan, row_offsets, packed, from_left, from_right)

    every_z = range(n_data)

    def send_z(group):
        return [move(group[s], s) for s in every_z]

    ranks = list(range(per_pair - layout.direct_ranks))
    rest = [layout.stage(rank) for rank in ranks[1:]] + [layout.direct()]
    if ranks:
        first = pack_all(layout.stage(0), 60)
        stages = {0: send_z(first)}
        rest = [layout.late()] + rest
    packed = pack_all([parts for group in rest for parts in group], 50)
    complete, at = [], 0
    for group in rest:
        complete.append(overlay_all(group, packed[at : at + len(group)]))
        at += len(group)
    if ranks:
        late = send_z(complete[0])
        for rank in ranks[1:]:
            stages[rank] = send_z(complete[rank])

        def resend(early):
            return send_z(overlay_all(layout.stage(0), first))

        crowded = plan[0, per_pair + 2] > LATE
        stages[0] = lax.cond(crowded, resend, lambda early: early, stages[0])
    direct = lax.all_to_all(
        complete[-1][0], ("dp", "tensor"), split_axis=0, concat_axis=0, tiled=True
    )
    direct = direct.reshape((n_data, n_tensor, layout.direct_ranks) + direct.shape[1:])
    outputs = None
    for rank in ranks:
        arrays = stages[rank] + (late if rank == 0 else [])
        gathered = gather_forward(layout, [rank], plan, arrays)
        forwarded = [gathered[0]]
        for u in range(1, n_tensor):
            forwarded.append(from_behind(gathered[u], "tensor", u))
        outputs = store_ranks(layout, [rank], False, plan, forwarded, probe, outputs)
    last = list(range(per_pair - layout.direct_ranks, per_pair))
    return tuple(store_ranks(layout, last, True, plan, [direct], probe, outputs))


def solution(mesh):
    return jax.shard_map(
        shards,
        mesh=mesh,
        in_specs=(P("tensor", "dp"), P("tensor", "dp"), P(), P(), P()),
        out_specs=(P(("dp", "tensor"), None, None), P(("dp", "tensor"), None, None)),
        check_vma=False,
    )
```

time: 157 us -> 179 us (1.14)
  the two profiles are of different devices: /device:TPU:0 before, /device:TPU:19 now
where the time goes in v3:
time: 179 us
  waiting for transfers between devices  102 us (57%)
  Pallas kernels  39.5 us (22%)
  starting transfers between devices  33.7 us (19%)
  local copies, waits for them, and re-layouts  2.75 us (2%)
    ppermute x25, waiting for transfers between devices, from_behind(): return lax.ppermute(block, axis, route)  102 us
    ppermute x25, starting transfers between devices, from_behind(): return lax.ppermute(block, axis, route)  29 us
    pallas_call x3, Pallas kernels, store_ranks(): pl.pallas_call(functools.partial(store_kernel, layout, ranks, direct, cou...  13.6 us
    pallas_call x2, Pallas kernels, pack(): pl.pallas_call(functools.partial(pack_kernel, arrays), out_shape=[jax.Sha...  9.89 us
    pallas_call x3, Pallas kernels, overlay(): pl.pallas_call(functools.partial(overlay_kernel, arrays), out_shape=[jax....  8.5 us
    all_to_all x1, starting transfers between devices, shards(): lax.all_to_all(complete[-1][0], ('dp', 'tensor'), split_axis=0, concat_ax...  4.67 us
    pallas_call x1, Pallas kernels, cut_edges(): pl.pallas_call(edges_kernel, out_shape=(shape, shape), in_specs=[smem(),...  3.87 us
  transfers between devices with their start and end apart: 26, of which 11 were waited for; matrix products, arithmetic and copies ran while one was open for 0% of the time, Pallas kernels for 15%

profile of v3, /device:TPU:19, one launch (start us, length us, event | category | flops | bytes accessed | tf_op | source)
XLA Modules:
  0.0 178.9 jit_solution(9282186042114049934)
XLA Ops:
  0.6 3.9 %shard_map.70 = (bf16[2,2048,128]{2,1,0:T(8,128)(2,1)}, bf16[2,2048,128]{2,1,0:T(8,128)(2,1)}) custom-call(s32[2,9]{1,0:T(2,128)} %offsets.13, bf16[12288,128]{1,0:T(8,128)(2,1)} %embed.5, bf16[12288,128]{1,0:T(8,128)(2,1)} %head.5), custom_call_target="tpu_custom_call" | custom-call | tf_op jit(solution)/shard_map/pallas_call | solution.py:107
  7.6 6.3 %shard_map.69 = (bf16[1,128,128]{2,1,0:T(8,128)(2,1)S(1)}, bf16[1,128,128]{2,1,0:T(8,128)(2,1)S(1)}, bf16[1,128,128]{2,1,0:T(8,128)(2,1)S(1)}, bf16[1,128,128]{2...) custom-call(s32[32,128]{1,0:T(8,128)S(1)} %shard_map.68.plan, ...), custom_call_target="tpu_custom_call" | custom-call | flops 3000000000 | bytes 7000000 | tf_op jit(solution)/shard_map/pallas_call | solution.py:296
  13.9 14.9 %collective-permute-done.3.refs_1_.refs_4_ = bf16[2,2048,128]{2,1,0:T(8,128)(2,1)} collective-permute-done((bf16[2,2048,128]{2,1,0:T(8,128)(2,1)}, bf16[2,2048,128]{2,1,0:T(8,128)(2,1)}, u32[]{:S(2)}, u32[]{:S(2)}) %collective-permute-start.3) | collective-permute-done | bytes 1048608 | tf_op jit(solution)/shard_map/ppermute | solution.py:22
  28.8 2.6 %collective-permute-done.4.refs_2_.refs_5_ = bf16[2,2048,128]{2,1,0:T(8,128)(2,1)} collective-permute-done((bf16[2,2048,128]{2,1,0:T(8,128)(2,1)}, bf16[2,2048,128]{2,1,0:T(8,128)(2,1)}, u32[]{:S(2)}, u32[]{:S(2)}) %collective-permute-start.4) | collective-permute-done | bytes 1048608 | tf_op jit(solution)/shard_map/ppermute | solution.py:22
  31.4 3.4 %shard_map.71 = bf16[64,128,128]{2,1,0:T(8,128)(2,1)S(1)} custom-call(s32[32,128]{1,0:T(8,128)S(1)} %shard_map.68.plan, s32[2,9]{1,0:T(2,128)S(1)} %copy-done.4, bf16[64,128,128]{2,1,0:T(8,128)(2,1)S(1)} %get-tuple-element.85.refs_0_, bf16[2,2048,128]{2,1,0:T(8,128)(2,1)} %collective-permute-done.3.refs_1_.refs_4_, ...), custom_call_target="tpu_custom_call" | custom-call | flops 1000000000 | bytes 4000000 | tf_op jit(solution)/shard_map/pallas_call | solution.py:347
  36.2 4.7 %all-to-all-start = ((bf16[64,128,128]{2,1,0:T(8,128)(2,1)}), bf16[64,128,128]{2,1,0:T(8,128)(2,1)S(1)}, u32[]{:S(2)}, u32[]{:S(2)}) async-start(bf16[64,128,128]{2,1,0:T(8,128)(2,1)} %copy-done), calls=%async_computation | async-start | bytes 4194304 | tf_op jit(solution)/shard_map/all_to_all | solution.py:513
  40.9 3.6 %shard_map.74 = (bf16[8,128,128]{2,1,0:T(8,128)(2,1)}, bf16[8,128,128]{2,1,0:T(8,128)(2,1)S(1)}, bf16[8,128,128]{2,1,0:T(8,128)(2,1)S(1)}, bf16[8,128,128]{2,1,0:T(8,128)(2,1)}) custom-call(s32[32,128]{1,0:T(8,128)S(1)} %shard_map.68.plan, s32[2,9]{1,0:T(2,128)S(1)} %copy-done.4, bf16[12288,128]{1,0:T(8,128)(2,1)} %embed.5, bf16[12288,128]{1,0:T(8,128)(2,1)} %head.5), custom_call_target="tpu_custom_call" | custom-call | flops 960000000 | bytes 2240000 | tf_op jit(solution)/shard_map/pallas_call | solution.py:296
  47.2 3.3 %shard_map.72 = (bf16[8,128,128]{2,1,0:T(8,128)(2,1)S(1)}, bf16[8,128,128]{2,1,0:T(8,128)(2,1)}, bf16[8,128,128]{2,1,0:T(8,128)(2,1)}, bf16[8,128,128]{2,1,0:T(8,128)(2,1)}) custom-call(s32[32,128]{1,0:T(8,128)S(1)} %shard_map.68.plan, s32[2,9]{1,0:T(2,128)S(1)} %copy-done.4, bf16[8,128,128]{2,1,0:T(8,128)(2,1)S(1)} %get-tuple-element.88.refs_0_, ...), custom_call_target="tpu_custom_call" | custom-call | flops 1000000000 | bytes 4000000 | tf_op jit(solution)/shard_map/pallas_call | solution.py:347
  51.5 2.2 %collective-permute-start.6 = (bf16[8,128,128]{2,1,0:T(8,128)(2,1)}, bf16[8,128,128]{2,1,0:T(8,128)(2,1)}, u32[]{:S(2)}, u32[]{:S(2)}) collective-permute-start(bf16[8,128,128]{2,1,0:T(8,128)(2,1)} %get-tuple-element.94), channel_id=1, source_target_pairs={{16,0},{24,8},{0,16},{8,24},{17,1},{25,9},{1,17},{9,25},{18,2},{26... | collective-permute-start | bytes 786440 | tf_op jit(solution)/shard_map/ppermute | solution.py:22
  54.9 54.7 %collective-permute-done.15 = bf16[8,128,128]{2,1,0:T(8,128)(2,1)} collective-permute-done((bf16[8,128,128]{2,1,0:T(8,128)(2,1)S(1)}, bf16[8,128,128]{2,1,0:T(8,128)(2,1)}, u32[]{:S(2)}, u32[]{:S(2)}) %collective-permute-start.15) | collective-permute-done | bytes 262176 | tf_op jit(solution)/shard_map/ppermute | solution.py:22
  109.6 4.5 %collective-permute-done.16 = bf16[8,128,128]{2,1,0:T(8,128)(2,1)} collective-permute-done((bf16[8,128,128]{2,1,0:T(8,128)(2,1)S(1)}, bf16[8,128,128]{2,1,0:T(8,128)(2,1)}, u32[]{:S(2)}, u32[]{:S(2)}) %collective-permute-start.16) | collective-permute-done | bytes 262176 | tf_op jit(solution)/shard_map/ppermute | solution.py:22
  114.1 5.7 %collective-permute-done.17 = bf16[8,128,128]{2,1,0:T(8,128)(2,1)} collective-permute-done((bf16[8,128,128]{2,1,0:T(8,128)(2,1)}, bf16[8,128,128]{2,1,0:T(8,128)(2,1)}, u32[]{:S(2)}, u32[]{:S(2)}) %collective-permute-start.17) | collective-permute-done | bytes 262176 | tf_op jit(solution)/shard_map/ppermute | solution.py:22
  119.8 2.2 %collective-permute-start.7 = (bf16[8,128,128]{2,1,0:T(8,128)(2,1)}, bf16[8,128,128]{2,1,0:T(8,128)(2,1)S(1)}, u32[]{:S(2)}, u32[]{:S(2)}) collective-permute-start(bf16[8,128,128]{2,1,0:T(8,128)(2,1)} %get-tuple-element.95), channel_id=1, source_target_pairs={{8,0},{16,8},{24,16},{0,24},{9,1},{17,9},{25,17},{1,25},{10,2},{18... | collective-permute-start | bytes 786440 | tf_op jit(solution)/shard_map/ppermute | solution.py:22
  125.1 8.7 %collective-permute-done.18.refs_5_ = bf16[1,128,128]{2,1,0:T(8,128)(2,1)S(1)} collective-permute-done((bf16[1,128,128]{2,1,0:T(8,128)(2,1)S(1)}, bf16[1,128,128]{2,1,0:T(8,128)(2,1)S(1)}, u32[]{:S(2)}, u32[]{:S(2)}) %collective-permute-start.18) | collective-permute-done | bytes 32800 | tf_op jit(solution)/shard_map/ppermute | solution.py:22
  133.8 2.8 %collective-permute-done.20.refs_7_ = bf16[1,128,128]{2,1,0:T(8,128)(2,1)S(1)} collective-permute-done((bf16[1,128,128]{2,1,0:T(8,128)(2,1)S(1)}, bf16[1,128,128]{2,1,0:T(8,128)(2,1)S(1)}, u32[]{:S(2)}, u32[]{:S(2)}) %collective-permute-start.20) | collective-permute-done | bytes 32800 | tf_op jit(solution)/shard_map/ppermute | solution.py:22
  137.9 3.5 %collective-permute-start.21 = (bf16[4,128,128]{2,1,0:T(8,128)(2,1)S(1)}, bf16[4,128,128]{2,1,0:T(8,128)(2,1)S(1)}, u32[]{:S(2)}, u32[]{:S(2)}) collective-permute-start(bf16[4,128,128]{2,1,0:T(8,128)(2,1)S(1)} %get-tuple-element.121), channel_id=1, source_target_pairs={{7,0},{0,1},{1,2},{2,3},{3,4},{4,5},{5,6},{6,7},{15,8},{8,9},{9,10... | collective-permute-start | bytes 393224 | tf_op jit(solution)/shard_map/ppermute | solution.py:22
  143.3 2.0 %collective-permute-start.25 = (bf16[4,128,128]{2,1,0:T(8,128)(2,1)S(1)}, bf16[4,128,128]{2,1,0:T(8,128)(2,1)S(1)}, u32[]{:S(2)}, u32[]{:S(2)}) collective-permute-start(bf16[4,128,128]{2,1,0:T(8,128)(2,1)S(1)} %get-tuple-element.125), channel_id=1, source_target_pairs={{3,0},{4,1},{5,2},{6,3},{7,4},{0,5},{1,6},{2,7},{11,8},{12,9},{13,... | collective-permute-start | bytes 393224 | tf_op jit(solution)/shard_map/ppermute | solution.py:22
  149.6 4.0 %collective-permute-start.8 = (bf16[4,128,128]{2,1,0:T(8,128)(2,1)S(1)}, bf16[4,128,128]{2,1,0:T(8,128)(2,1)S(1)}, u32[]{:S(2)}, u32[]{:S(2)}) collective-permute-start(bf16[4,128,128]{2,1,0:T(8,128)(2,1)S(1)} %get-tuple-element.97), channel_id=1, source_target_pairs={{7,0},{0,1},{1,2},{2,3},{3,4},{4,5},{5,6},{6,7},{15,8},{8,9},{9,10... | collective-permute-start | bytes 393224 | tf_op jit(solution)/shard_map/ppermute | solution.py:22
  153.6 2.2 %collective-permute-start.9 = (bf16[4,128,128]{2,1,0:T(8,128)(2,1)S(1)}, bf16[4,128,128]{2,1,0:T(8,128)(2,1)S(1)}, u32[]{:S(2)}, u32[]{:S(2)}) collective-permute-start(bf16[4,128,128]{2,1,0:T(8,128)(2,1)S(1)} %get-tuple-element.98), channel_id=1, source_target_pairs={{6,0},{7,1},{0,2},{1,3},{2,4},{3,5},{4,6},{5,7},{14,8},{15,9},{8,1... | collective-permute-start | bytes 393224 | tf_op jit(solution)/shard_map/ppermute | solution.py:22
  157.1 2.0 %collective-permute-start.12 = (bf16[4,128,128]{2,1,0:T(8,128)(2,1)S(1)}, bf16[4,128,128]{2,1,0:T(8,128)(2,1)S(1)}, u32[]{:S(2)}, u32[]{:S(2)}) collective-permute-start(bf16[4,128,128]{2,1,0:T(8,128)(2,1)S(1)} %get-tuple-element.101), channel_id=1, source_target_pairs={{3,0},{4,1},{5,2},{6,3},{7,4},{0,5},{1,6},{2,7},{11,8},{12,9},{13,... | collective-permute-start | bytes 393224 | tf_op jit(solution)/shard_map/ppermute | solution.py:22
  159.6 4.0 %shard_map.77 = (bf16[32,128,512]{2,1,0:T(8,128)(2,1)}, f32[32,128,1024]{2,1,0:T(8,128)}) custom-call(s32[32,128]{1,0:T(8,128)S(1)} %shard_map.68.plan, bf16[4,128,128]{2,1,0:T(8,128)(2,1)S(1)} %get-tuple-element.120.refs_0_, bf16[4,128,128]{2,1,0:T(8,128)(2,1)S(1)} %collective-permute-done.21.refs_1_, ...), custom_call_target="tpu_custom_call" | custom-call | flops 1073741824 | bytes 6400000 | tf_op jit(solution)/shard_map/pallas_call | solution.py:443
  163.6 4.4 %collective-permute-done.11.refs_4_ = bf16[4,128,128]{2,1,0:T(8,128)(2,1)S(1)} collective-permute-done((bf16[4,128,128]{2,1,0:T(8,128)(2,1)S(1)}, bf16[4,128,128]{2,1,0:T(8,128)(2,1)S(1)}, u32[]{:S(2)}, u32[]{:S(2)}) %collective-permute-start.11) | collective-permute-done | bytes 131104 | tf_op jit(solution)/shard_map/ppermute | solution.py:22
  169.3 4.0 %shard_map.78 = (bf16[32,128,512]{2,1,0:T(8,128)(2,1)}, f32[32,128,1024]{2,1,0:T(8,128)}) custom-call(s32[32,128]{1,0:T(8,128)S(1)} %shard_map.68.plan, bf16[4,128,128]{2,1,0:T(8,128)(2,1)S(1)} %get-tuple-element.96.refs_0_, bf16[4,128,128]{2,1,0:T(8,128)(2,1)S(1)} %collective-permute-done.8.refs_1_, ...), custom_call_target="tpu_custom_call", output_to_operand_aliasing={{0}: (10, {}), {1}: (11, {})} | custom-call | flops 1073741824 | bytes 6400000 | tf_op jit(solution)/shard_map/pallas_call | solution.py:443
  173.3 5.7 %shard_map.79 = (bf16[32,128,512]{2,1,0:T(8,128)(2,1)}, f32[32,128,1024]{2,1,0:T(8,128)}) custom-call(s32[32,128]{1,0:T(8,128)S(1)} %shard_map.68.plan, bf16[4,8,2,128,128]{4,3,2,1,0:T(8,128)(2,1)S(1)} %bitcast.2, bf16[512,1024]{1,0:T(8,128)(2,1)S(1)} %copy-done.1, ...), custom_call_target="tpu_custom_call", output_to_operand_aliasing={{0}: (3, {}), {1}: (4, {})} | custom-call | flops 2147483648 | bytes 12800000 | tf_op jit(solution)/shard_map/pallas_call | solution.py:443
  (55 shorter events, 22.2 us)
Async XLA Ops:
  4.5 24.3 %collective-permute-start.3 = (bf16[2,2048,128]{2,1,0:T(8,128)(2,1)}, bf16[2,2048,128]{2,1,0:T(8,128)(2,1)}, u32[]{:S(2)}, u32[]{:S(2)}) collective-permute-start(bf16[2,2048,128]{2,1,0:T(8,128)(2,1)} %get-tuple-element.86), channel_id=1, source_target_pairs={{7,0},{0,1},{1,2},{2,3},{3,4},{4,5},{5,6},{6,7},{15,8},{8,9},{9,10... | collective-permute-start | bytes 3145736 | tf_op jit(solution)/shard_map/ppermute | solution.py:22
  6.2 25.2 %collective-permute-start.4 = (bf16[2,2048,128]{2,1,0:T(8,128)(2,1)}, bf16[2,2048,128]{2,1,0:T(8,128)(2,1)}, u32[]{:S(2)}, u32[]{:S(2)}) collective-permute-start(bf16[2,2048,128]{2,1,0:T(8,128)(2,1)} %get-tuple-element.87), channel_id=1, source_target_pairs={{1,0},{2,1},{3,2},{4,3},{5,4},{6,5},{7,6},{0,7},{9,8},{10,9},{11,1... | collective-permute-start | bytes 3145736 | tf_op jit(solution)/shard_map/ppermute | solution.py:22
  36.2 137.1 %all-to-all-start = ((bf16[64,128,128]{2,1,0:T(8,128)(2,1)}), bf16[64,128,128]{2,1,0:T(8,128)(2,1)S(1)}, u32[]{:S(2)}, u32[]{:S(2)}) async-start(bf16[64,128,128]{2,1,0:T(8,128)(2,1)} %copy-done), calls=%async_computation | async-start | bytes 4194304 | tf_op jit(solution)/shard_map/all_to_all | solution.py:513
  44.4 65.1 %collective-permute-start.15 = (bf16[8,128,128]{2,1,0:T(8,128)(2,1)S(1)}, bf16[8,128,128]{2,1,0:T(8,128)(2,1)}, u32[]{:S(2)}, u32[]{:S(2)}) collective-permute-start(bf16[8,128,128]{2,1,0:T(8,128)(2,1)S(1)} %get-tuple-element.105), channel_id=1, source_target_pairs={{24,0},{0,8},{8,16},{16,24},{25,1},{1,9},{9,17},{17,25},{26,2},{2,... | collective-permute-start | bytes 786440 | tf_op jit(solution)/shard_map/ppermute | solution.py:22
  45.7 68.4 %collective-permute-start.16 = (bf16[8,128,128]{2,1,0:T(8,128)(2,1)S(1)}, bf16[8,128,128]{2,1,0:T(8,128)(2,1)}, u32[]{:S(2)}, u32[]{:S(2)}) collective-permute-start(bf16[8,128,128]{2,1,0:T(8,128)(2,1)S(1)} %get-tuple-element.106), channel_id=1, source_target_pairs={{16,0},{24,8},{0,16},{8,24},{17,1},{25,9},{1,17},{9,25},{18,2},{26... | collective-permute-start | bytes 786440 | tf_op jit(solution)/shard_map/ppermute | solution.py:22
  45.9 73.9 %collective-permute-start.17 = (bf16[8,128,128]{2,1,0:T(8,128)(2,1)}, bf16[8,128,128]{2,1,0:T(8,128)(2,1)}, u32[]{:S(2)}, u32[]{:S(2)}) collective-permute-start(bf16[8,128,128]{2,1,0:T(8,128)(2,1)} %get-tuple-element.107), channel_id=1, source_target_pairs={{8,0},{16,8},{24,16},{0,24},{9,1},{17,9},{25,17},{1,25},{10,2},{18... | collective-permute-start | bytes 786440 | tf_op jit(solution)/shard_map/ppermute | solution.py:22
  51.2 91.9 %collective-permute-start.5 = (bf16[8,128,128]{2,1,0:T(8,128)(2,1)}, bf16[8,128,128]{2,1,0:T(8,128)(2,1)S(1)}, u32[]{:S(2)}, u32[]{:S(2)}) collective-permute-start(bf16[8,128,128]{2,1,0:T(8,128)(2,1)} %get-tuple-element.93), channel_id=1, source_target_pairs={{24,0},{0,8},{8,16},{16,24},{25,1},{1,9},{9,17},{17,25},{26,2},{2,... | collective-permute-start | bytes 786440 | tf_op jit(solution)/shard_map/ppermute | solution.py:22
  51.5 91.7 %collective-permute-start.6 = (bf16[8,128,128]{2,1,0:T(8,128)(2,1)}, bf16[8,128,128]{2,1,0:T(8,128)(2,1)}, u32[]{:S(2)}, u32[]{:S(2)}) collective-permute-start(bf16[8,128,128]{2,1,0:T(8,128)(2,1)} %get-tuple-element.94), channel_id=1, source_target_pairs={{16,0},{24,8},{0,16},{8,24},{17,1},{25,9},{1,17},{9,25},{18,2},{26... | collective-permute-start | bytes 786440 | tf_op jit(solution)/shard_map/ppermute | solution.py:22
  119.8 23.5 %collective-permute-start.7 = (bf16[8,128,128]{2,1,0:T(8,128)(2,1)}, bf16[8,128,128]{2,1,0:T(8,128)(2,1)S(1)}, u32[]{:S(2)}, u32[]{:S(2)}) collective-permute-start(bf16[8,128,128]{2,1,0:T(8,128)(2,1)} %get-tuple-element.95), channel_id=1, source_target_pairs={{8,0},{16,8},{24,16},{0,24},{9,1},{17,9},{25,17},{1,25},{10,2},{18... | collective-permute-start | bytes 786440 | tf_op jit(solution)/shard_map/ppermute | solution.py:22
  123.8 10.0 %collective-permute-start.18 = (bf16[1,128,128]{2,1,0:T(8,128)(2,1)S(1)}, bf16[1,128,128]{2,1,0:T(8,128)(2,1)S(1)}, u32[]{:S(2)}, u32[]{:S(2)}) collective-permute-start(bf16[1,128,128]{2,1,0:T(8,128)(2,1)S(1)} %get-tuple-element.117), channel_id=1, source_target_pairs={{24,0},{0,8},{8,16},{16,24},{25,1},{1,9},{9,17},{17,25},{26,2},{2,... | collective-permute-start | bytes 98312 | tf_op jit(solution)/shard_map/ppermute | solution.py:22
  123.8 9.9 %collective-permute-start.19 = (bf16[1,128,128]{2,1,0:T(8,128)(2,1)S(1)}, bf16[1,128,128]{2,1,0:T(8,128)(2,1)S(1)}, u32[]{:S(2)}, u32[]{:S(2)}) collective-permute-start(bf16[1,128,128]{2,1,0:T(8,128)(2,1)S(1)} %get-tuple-element.118), channel_id=1, source_target_pairs={{16,0},{24,8},{0,16},{8,24},{17,1},{25,9},{1,17},{9,25},{18,2},{26... | collective-permute-start | bytes 98312 | tf_op jit(solution)/shard_map/ppermute | solution.py:22
  137.9 8.4 %collective-permute-start.21 = (bf16[4,128,128]{2,1,0:T(8,128)(2,1)S(1)}, bf16[4,128,128]{2,1,0:T(8,128)(2,1)S(1)}, u32[]{:S(2)}, u32[]{:S(2)}) collective-permute-start(bf16[4,128,128]{2,1,0:T(8,128)(2,1)S(1)} %get-tuple-element.121), channel_id=1, source_target_pairs={{7,0},{0,1},{1,2},{2,3},{3,4},{4,5},{5,6},{6,7},{15,8},{8,9},{9,10... | collective-permute-start | bytes 393224 | tf_op jit(solution)/shard_map/ppermute | solution.py:22
  141.4 6.9 %collective-permute-start.22 = (bf16[4,128,128]{2,1,0:T(8,128)(2,1)S(1)}, bf16[4,128,128]{2,1,0:T(8,128)(2,1)S(1)}, u32[]{:S(2)}, u32[]{:S(2)}) collective-permute-start(bf16[4,128,128]{2,1,0:T(8,128)(2,1)S(1)} %get-tuple-element.122), channel_id=1, source_target_pairs={{6,0},{7,1},{0,2},{1,3},{2,4},{3,5},{4,6},{5,7},{14,8},{15,9},{8,1... | collective-permute-start | bytes 393224 | tf_op jit(solution)/shard_map/ppermute | solution.py:22
  143.1 6.5 %collective-permute-start.23 = (bf16[4,128,128]{2,1,0:T(8,128)(2,1)S(1)}, bf16[4,128,128]{2,1,0:T(8,128)(2,1)S(1)}, u32[]{:S(2)}, u32[]{:S(2)}) collective-permute-start(bf16[4,128,128]{2,1,0:T(8,128)(2,1)S(1)} %get-tuple-element.123), channel_id=1, source_target_pairs={{5,0},{6,1},{7,2},{0,3},{1,4},{2,5},{3,6},{4,7},{13,8},{14,9},{15,... | collective-permute-start | bytes 393224 | tf_op jit(solution)/shard_map/ppermute | solution.py:22
  143.1 10.5 %collective-permute-start.24 = (bf16[4,128,128]{2,1,0:T(8,128)(2,1)S(1)}, bf16[4,128,128]{2,1,0:T(8,128)(2,1)S(1)}, u32[]{:S(2)}, u32[]{:S(2)}) collective-permute-start(bf16[4,128,128]{2,1,0:T(8,128)(2,1)S(1)} %get-tuple-element.124), channel_id=1, source_target_pairs={{4,0},{5,1},{6,2},{7,3},{0,4},{1,5},{2,6},{3,7},{12,8},{13,9},{14,... | collective-permute-start | bytes 393224 | tf_op jit(solution)/shard_map/ppermute | solution.py:22
  143.3 12.5 %collective-permute-start.25 = (bf16[4,128,128]{2,1,0:T(8,128)(2,1)S(1)}, bf16[4,128,128]{2,1,0:T(8,128)(2,1)S(1)}, u32[]{:S(2)}, u32[]{:S(2)}) collective-permute-start(bf16[4,128,128]{2,1,0:T(8,128)(2,1)S(1)} %get-tuple-element.125), channel_id=1, source_target_pairs={{3,0},{4,1},{5,2},{6,3},{7,4},{0,5},{1,6},{2,7},{11,8},{12,9},{13,... | collective-permute-start | bytes 393224 | tf_op jit(solution)/shard_map/ppermute | solution.py:22
  146.3 9.5 %collective-permute-start.26 = (bf16[4,128,128]{2,1,0:T(8,128)(2,1)S(1)}, bf16[4,128,128]{2,1,0:T(8,128)(2,1)S(1)}, u32[]{:S(2)}, u32[]{:S(2)}) collective-permute-start(bf16[4,128,128]{2,1,0:T(8,128)(2,1)S(1)} %get-tuple-element.126), channel_id=1, source_target_pairs={{2,0},{3,1},{4,2},{5,3},{6,4},{7,5},{0,6},{1,7},{10,8},{11,9},{12,... | collective-permute-start | bytes 393224 | tf_op jit(solution)/shard_map/ppermute | solution.py:22
  148.3 8.8 %collective-permute-start.27 = (bf16[4,128,128]{2,1,0:T(8,128)(2,1)S(1)}, bf16[4,128,128]{2,1,0:T(8,128)(2,1)S(1)}, u32[]{:S(2)}, u32[]{:S(2)}) collective-permute-start(bf16[4,128,128]{2,1,0:T(8,128)(2,1)S(1)} %get-tuple-element.127), channel_id=1, source_target_pairs={{1,0},{2,1},{3,2},{4,3},{5,4},{6,5},{7,6},{0,7},{9,8},{10,9},{11,1... | collective-permute-start | bytes 393224 | tf_op jit(solution)/shard_map/ppermute | solution.py:22
  149.6 9.5 %collective-permute-start.8 = (bf16[4,128,128]{2,1,0:T(8,128)(2,1)S(1)}, bf16[4,128,128]{2,1,0:T(8,128)(2,1)S(1)}, u32[]{:S(2)}, u32[]{:S(2)}) collective-permute-start(bf16[4,128,128]{2,1,0:T(8,128)(2,1)S(1)} %get-tuple-element.97), channel_id=1, source_target_pairs={{7,0},{0,1},{1,2},{2,3},{3,4},{4,5},{5,6},{6,7},{15,8},{8,9},{9,10... | collective-permute-start | bytes 393224 | tf_op jit(solution)/shard_map/ppermute | solution.py:22
  155.8 7.8 %collective-permute-start.10 = (bf16[4,128,128]{2,1,0:T(8,128)(2,1)S(1)}, bf16[4,128,128]{2,1,0:T(8,128)(2,1)S(1)}, u32[]{:S(2)}, u32[]{:S(2)}) collective-permute-start(bf16[4,128,128]{2,1,0:T(8,128)(2,1)S(1)} %get-tuple-element.99), channel_id=1, source_target_pairs={{5,0},{6,1},{7,2},{0,3},{1,4},{2,5},{3,6},{4,7},{13,8},{14,9},{15,... | collective-permute-start | bytes 393224 | tf_op jit(solution)/shard_map/ppermute | solution.py:22
  155.8 12.2 %collective-permute-start.11 = (bf16[4,128,128]{2,1,0:T(8,128)(2,1)S(1)}, bf16[4,128,128]{2,1,0:T(8,128)(2,1)S(1)}, u32[]{:S(2)}, u32[]{:S(2)}) collective-permute-start(bf16[4,128,128]{2,1,0:T(8,128)(2,1)S(1)} %get-tuple-element.100), channel_id=1, source_target_pairs={{4,0},{5,1},{6,2},{7,3},{0,4},{1,5},{2,6},{3,7},{12,8},{13,9},{14,... | collective-permute-start | bytes 393224 | tf_op jit(solution)/shard_map/ppermute | solution.py:22
  157.1 12.2 %collective-permute-start.12 = (bf16[4,128,128]{2,1,0:T(8,128)(2,1)S(1)}, bf16[4,128,128]{2,1,0:T(8,128)(2,1)S(1)}, u32[]{:S(2)}, u32[]{:S(2)}) collective-permute-start(bf16[4,128,128]{2,1,0:T(8,128)(2,1)S(1)} %get-tuple-element.101), channel_id=1, source_target_pairs={{3,0},{4,1},{5,2},{6,3},{7,4},{0,5},{1,6},{2,7},{11,8},{12,9},{13,... | collective-permute-start | bytes 393224 | tf_op jit(solution)/shard_map/ppermute | solution.py:22
  159.1 10.2 %collective-permute-start.13 = (bf16[4,128,128]{2,1,0:T(8,128)(2,1)S(1)}, bf16[4,128,128]{2,1,0:T(8,128)(2,1)S(1)}, u32[]{:S(2)}, u32[]{:S(2)}) collective-permute-start(bf16[4,128,128]{2,1,0:T(8,128)(2,1)S(1)} %get-tuple-element.102), channel_id=1, source_target_pairs={{2,0},{3,1},{4,2},{5,3},{6,4},{7,5},{0,6},{1,7},{10,8},{11,9},{12,... | collective-permute-start | bytes 393224 | tf_op jit(solution)/shard_map/ppermute | solution.py:22
  159.2 10.1 %collective-permute-start.14 = (bf16[4,128,128]{2,1,0:T(8,128)(2,1)S(1)}, bf16[4,128,128]{2,1,0:T(8,128)(2,1)S(1)}, u32[]{:S(2)}, u32[]{:S(2)}) collective-permute-start(bf16[4,128,128]{2,1,0:T(8,128)(2,1)S(1)} %get-tuple-element.103), channel_id=1, source_target_pairs={{1,0},{2,1},{3,2},{4,3},{5,4},{6,5},{7,6},{0,7},{9,8},{10,9},{11,1... | collective-permute-start | bytes 393224 | tf_op jit(solution)/shard_map/ppermute | solution.py:22
  (8 other events, 83.1 us)

commit v4 on v3

--- a/solution.py
+++ b/solution.py
@@ -399,9 +399,10 @@
     stored, sketch, full, product, sems = refs[-5:]
     width = incoming[0].shape[-1]
     slots = len(ranks) * n_tensor
-    step = min(4, slots)
     copies = []
-    for begin in range(0, slots, step):
+    begin = 0
+    while begin < slots:
+        step = min(max(begin, 1), 4, slots - begin)
         for i in range(begin, begin + step):
             k, hop = i // n_tensor, i % n_tensor
             for s in range(n_data):
@@ -424,6 +425,7 @@
             copies.append(pltpu.make_async_copy(product.at[i], sketch.at[slot], sems.at[2 * i + 1]))
             copies[-2].start()
             copies[-1].start()
+        begin += step
     for copy in copies:
         copy.wait()
 
@@ -494,16 +496,16 @@
     if ranks:
         first = pack_all(layout.stage(0), 60)
         stages = {0: send_z(first)}
-        rest = [layout.late()] + rest
+        rest = [layout.late() + rest[0]] + rest[1:]
     packed = pack_all([parts for group in rest for parts in group], 50)
     complete, at = [], 0
     for group in rest:
         complete.append(overlay_all(group, packed[at : at + len(group)]))
         at += len(group)
     if ranks:
-        late = send_z(complete[0])
+        late = send_z(complete[0][:n_data])
         for rank in ranks[1:]:
-            stages[rank] = send_z(complete[rank])
+            stages[rank] = send_z(complete[0][n_data * rank :])
 
         def resend(early):
             return send_z(overlay_all(layout.stage(0), first))

time: 179 us -> 179 us (level)
  Pallas kernels: 39.5 us -> 37.7 us
    unnamed x12 -> x14, local copies, waits for them, and re-layouts: 2.07 us -> 3.72 us
    pallas_call x3 -> x2, Pallas kernels: 8.5 us -> 6.92 us  [overlay(): pl.pallas_call(functools.partial(overlay_kernel, arrays), out_shape=[jax....]
  transfers between devices with their start and end apart: 26 -> 26, of which waited for: 11 -> 10; matrix products, arithmetic and copies ran while one was open for 0% -> 0% of each run, Pallas kernels for 15% -> 14%
where the time goes in v4:
time: 179 us
  waiting for transfers between devices  102 us (57%)
  Pallas kernels  37.7 us (21%)
  starting transfers between devices  33.6 us (19%)
  local copies, waits for them, and re-layouts  4.4 us (2%)
    ppermute x25, waiting for transfers between devices, from_behind(): return lax.ppermute(block, axis, route)  102 us
    ppermute x25, starting transfers between devices, from_behind(): return lax.ppermute(block, axis, route)  29 us
    pallas_call x3, Pallas kernels, store_ranks(): pl.pallas_call(functools.partial(store_kernel, layout, ranks, direct, cou...  13.4 us
    pallas_call x2, Pallas kernels, pack(): pl.pallas_call(functools.partial(pack_kernel, arrays), out_shape=[jax.Sha...  9.89 us
    pallas_call x2, Pallas kernels, overlay(): pl.pallas_call(functools.partial(overlay_kernel, arrays), out_shape=[jax....  6.92 us
    all_to_all x1, starting transfers between devices, shards(): lax.all_to_all(complete[-1][0], ('dp', 'tensor'), split_axis=0, concat_ax...  4.67 us
    pallas_call x1, Pallas kernels, cut_edges(): pl.pallas_call(edges_kernel, out_shape=(shape, shape), in_specs=[smem(),...  3.87 us
    unnamed x14, local copies, waits for them, and re-layouts  3.72 us
  transfers between devices with their start and end apart: 26, of which 10 were waited for; matrix products, arithmetic and copies ran while one was open for 0% of the time, Pallas kernels for 14%

profile of v4, /device:TPU:19, one launch (start us, length us, event | category | flops | bytes accessed | tf_op | source)
XLA Modules:
  0.0 178.7 jit_solution(8183885900003632965)
XLA Ops:
  0.7 3.9 %shard_map.70 = (bf16[2,2048,128]{2,1,0:T(8,128)(2,1)}, bf16[2,2048,128]{2,1,0:T(8,128)(2,1)}) custom-call(s32[2,9]{1,0:T(2,128)} %offsets.11, bf16[12288,128]{1,0:T(8,128)(2,1)} %embed.5, bf16[12288,128]{1,0:T(8,128)(2,1)} %head.5), custom_call_target="tpu_custom_call" | custom-call | tf_op jit(solution)/shard_map/pallas_call | solution.py:107
  7.6 6.3 %shard_map.69 = (bf16[1,128,128]{2,1,0:T(8,128)(2,1)S(1)}, bf16[1,128,128]{2,1,0:T(8,128)(2,1)S(1)}, bf16[1,128,128]{2,1,0:T(8,128)(2,1)S(1)}, bf16[1,128,128]{2...) custom-call(s32[32,128]{1,0:T(8,128)S(1)} %shard_map.68.plan, ...), custom_call_target="tpu_custom_call" | custom-call | flops 3000000000 | bytes 7000000 | tf_op jit(solution)/shard_map/pallas_call | solution.py:296
  13.9 14.9 %collective-permute-done.3.refs_1_.refs_8_ = bf16[2,2048,128]{2,1,0:T(8,128)(2,1)} collective-permute-done((bf16[2,2048,128]{2,1,0:T(8,128)(2,1)}, bf16[2,2048,128]{2,1,0:T(8,128)(2,1)}, u32[]{:S(2)}, u32[]{:S(2)}) %collective-permute-start.3) | collective-permute-done | bytes 1048608 | tf_op jit(solution)/shard_map/ppermute | solution.py:22
  28.8 2.6 %collective-permute-done.4.refs_2_.refs_9_ = bf16[2,2048,128]{2,1,0:T(8,128)(2,1)} collective-permute-done((bf16[2,2048,128]{2,1,0:T(8,128)(2,1)}, bf16[2,2048,128]{2,1,0:T(8,128)(2,1)}, u32[]{:S(2)}, u32[]{:S(2)}) %collective-permute-start.4) | collective-permute-done | bytes 1048608 | tf_op jit(solution)/shard_map/ppermute | solution.py:22
  31.4 3.4 %shard_map.71 = bf16[64,128,128]{2,1,0:T(8,128)(2,1)S(1)} custom-call(s32[32,128]{1,0:T(8,128)S(1)} %shard_map.68.plan, s32[2,9]{1,0:T(2,128)S(1)} %copy-done.5, bf16[64,128,128]{2,1,0:T(8,128)(2,1)S(1)} %get-tuple-element.85.refs_0_, bf16[2,2048,128]{2,1,0:T(8,128)(2,1)} %collective-permute-done.3.refs_1_.refs_8_, ...), custom_call_target="tpu_custom_call" | custom-call | flops 1000000000 | bytes 4000000 | tf_op jit(solution)/shard_map/pallas_call | solution.py:347
  36.2 4.7 %all-to-all-start = ((bf16[64,128,128]{2,1,0:T(8,128)(2,1)}), bf16[64,128,128]{2,1,0:T(8,128)(2,1)S(1)}, u32[]{:S(2)}, u32[]{:S(2)}) async-start(bf16[64,128,128]{2,1,0:T(8,128)(2,1)} %copy-done), calls=%async_computation | async-start | bytes 4194304 | tf_op jit(solution)/shard_map/all_to_all | solution.py:515
  40.9 3.6 %shard_map.74 = (bf16[8,128,128]{2,1,0:T(8,128)(2,1)}, bf16[8,128,128]{2,1,0:T(8,128)(2,1)S(1)}, bf16[8,128,128]{2,1,0:T(8,128)(2,1)S(1)}, bf16[8,128,128]{2,1,0:T(8,128)(2,1)}) custom-call(s32[32,128]{1,0:T(8,128)S(1)} %shard_map.68.plan, s32[2,9]{1,0:T(2,128)S(1)} %copy-done.5, bf16[12288,128]{1,0:T(8,128)(2,1)} %embed.5, bf16[12288,128]{1,0:T(8,128)(2,1)} %head.5), custom_call_target="tpu_custom_call" | custom-call | flops 960000000 | bytes 2240000 | tf_op jit(solution)/shard_map/pallas_call | solution.py:296
  47.2 3.5 %shard_map.72 = (bf16[1,128,128]{2,1,0:T(8,128)(2,1)S(1)}, bf16[1,128,128]{2,1,0:T(8,128)(2,1)S(1)}, bf16[1,128,128]{2,1,0:T(8,128)(2,1)S(1)}, bf16[1,128,128]{2...) custom-call(s32[32,128]{1,0:T(8,128)S(1)} %shard_map.68.plan, ...), custom_call_target="tpu_custom_call" | custom-call | flops 1000000000 | bytes 4000000 | tf_op jit(solution)/shard_map/pallas_call | solution.py:347
  52.3 2.2 %collective-permute-start.6 = (bf16[8,128,128]{2,1,0:T(8,128)(2,1)}, bf16[8,128,128]{2,1,0:T(8,128)(2,1)}, u32[]{:S(2)}, u32[]{:S(2)}) collective-permute-start(bf16[8,128,128]{2,1,0:T(8,128)(2,1)} %get-tuple-element.98), channel_id=1, source_target_pairs={{16,0},{24,8},{0,16},{8,24},{17,1},{25,9},{1,17},{9,25},{18,2},{26... | collective-permute-start | bytes 786440 | tf_op jit(solution)/shard_map/ppermute | solution.py:22
  55.7 53.9 %collective-permute-done.15 = bf16[8,128,128]{2,1,0:T(8,128)(2,1)} collective-permute-done((bf16[8,128,128]{2,1,0:T(8,128)(2,1)S(1)}, bf16[8,128,128]{2,1,0:T(8,128)(2,1)}, u32[]{:S(2)}, u32[]{:S(2)}) %collective-permute-start.15) | collective-permute-done | bytes 262176 | tf_op jit(solution)/shard_map/ppermute | solution.py:22
  109.6 4.5 %collective-permute-done.16 = bf16[8,128,128]{2,1,0:T(8,128)(2,1)} collective-permute-done((bf16[8,128,128]{2,1,0:T(8,128)(2,1)S(1)}, bf16[8,128,128]{2,1,0:T(8,128)(2,1)}, u32[]{:S(2)}, u32[]{:S(2)}) %collective-permute-start.16) | collective-permute-done | bytes 262176 | tf_op jit(solution)/shard_map/ppermute | solution.py:22
  114.1 5.7 %collective-permute-done.17 = bf16[8,128,128]{2,1,0:T(8,128)(2,1)} collective-permute-done((bf16[8,128,128]{2,1,0:T(8,128)(2,1)}, bf16[8,128,128]{2,1,0:T(8,128)(2,1)}, u32[]{:S(2)}, u32[]{:S(2)}) %collective-permute-start.17) | collective-permute-done | bytes 262176 | tf_op jit(solution)/shard_map/ppermute | solution.py:22
  119.8 2.2 %collective-permute-start.7 = (bf16[8,128,128]{2,1,0:T(8,128)(2,1)}, bf16[8,128,128]{2,1,0:T(8,128)(2,1)S(1)}, u32[]{:S(2)}, u32[]{:S(2)}) collective-permute-start(bf16[8,128,128]{2,1,0:T(8,128)(2,1)} %copy-done.2), channel_id=1, source_target_pairs={{8,0},{16,8},{24,16},{0,24},{9,1},{17,9},{25,17},{1,25},{10,2},{18... | collective-permute-start | bytes 786440 | tf_op jit(solution)/shard_map/ppermute | solution.py:22
  123.2 10.5 %collective-permute-done.18.refs_5_ = bf16[1,128,128]{2,1,0:T(8,128)(2,1)S(1)} collective-permute-done((bf16[1,128,128]{2,1,0:T(8,128)(2,1)S(1)}, bf16[1,128,128]{2,1,0:T(8,128)(2,1)S(1)}, u32[]{:S(2)}, u32[]{:S(2)}) %collective-permute-start.18) | collective-permute-done | bytes 32800 | tf_op jit(solution)/shard_map/ppermute | solution.py:22
  133.8 2.8 %collective-permute-done.20.refs_7_ = bf16[1,128,128]{2,1,0:T(8,128)(2,1)S(1)} collective-permute-done((bf16[1,128,128]{2,1,0:T(8,128)(2,1)S(1)}, bf16[1,128,128]{2,1,0:T(8,128)(2,1)S(1)}, u32[]{:S(2)}, u32[]{:S(2)}) %collective-permute-start.20) | collective-permute-done | bytes 32800 | tf_op jit(solution)/shard_map/ppermute | solution.py:22
  137.9 3.5 %collective-permute-start.21 = (bf16[4,128,128]{2,1,0:T(8,128)(2,1)S(1)}, bf16[4,128,128]{2,1,0:T(8,128)(2,1)S(1)}, u32[]{:S(2)}, u32[]{:S(2)}) collective-permute-start(bf16[4,128,128]{2,1,0:T(8,128)(2,1)S(1)} %get-tuple-element.121), channel_id=1, source_target_pairs={{7,0},{0,1},{1,2},{2,3},{3,4},{4,5},{5,6},{6,7},{15,8},{8,9},{9,10... | collective-permute-start | bytes 393224 | tf_op jit(solution)/shard_map/ppermute | solution.py:22
  143.3 2.0 %collective-permute-start.25 = (bf16[4,128,128]{2,1,0:T(8,128)(2,1)S(1)}, bf16[4,128,128]{2,1,0:T(8,128)(2,1)S(1)}, u32[]{:S(2)}, u32[]{:S(2)}) collective-permute-start(bf16[4,128,128]{2,1,0:T(8,128)(2,1)S(1)} %get-tuple-element.125), channel_id=1, source_target_pairs={{3,0},{4,1},{5,2},{6,3},{7,4},{0,5},{1,6},{2,7},{11,8},{12,9},{13,... | collective-permute-start | bytes 393224 | tf_op jit(solution)/shard_map/ppermute | solution.py:22
  149.6 4.0 %collective-permute-start.8 = (bf16[4,128,128]{2,1,0:T(8,128)(2,1)S(1)}, bf16[4,128,128]{2,1,0:T(8,128)(2,1)S(1)}, u32[]{:S(2)}, u32[]{:S(2)}) collective-permute-start(bf16[4,128,128]{2,1,0:T(8,128)(2,1)S(1)} %get-tuple-element.101), channel_id=1, source_target_pairs={{7,0},{0,1},{1,2},{2,3},{3,4},{4,5},{5,6},{6,7},{15,8},{8,9},{9,10... | collective-permute-start | bytes 393224 | tf_op jit(solution)/shard_map/ppermute | solution.py:22
  153.6 2.2 %collective-permute-start.9 = (bf16[4,128,128]{2,1,0:T(8,128)(2,1)S(1)}, bf16[4,128,128]{2,1,0:T(8,128)(2,1)S(1)}, u32[]{:S(2)}, u32[]{:S(2)}) collective-permute-start(bf16[4,128,128]{2,1,0:T(8,128)(2,1)S(1)} %get-tuple-element.102), channel_id=1, source_target_pairs={{6,0},{7,1},{0,2},{1,3},{2,4},{3,5},{4,6},{5,7},{14,8},{15,9},{8,1... | collective-permute-start | bytes 393224 | tf_op jit(solution)/shard_map/ppermute | solution.py:22
  157.1 2.0 %collective-permute-start.12 = (bf16[4,128,128]{2,1,0:T(8,128)(2,1)S(1)}, bf16[4,128,128]{2,1,0:T(8,128)(2,1)S(1)}, u32[]{:S(2)}, u32[]{:S(2)}) collective-permute-start(bf16[4,128,128]{2,1,0:T(8,128)(2,1)S(1)} %get-tuple-element.105), channel_id=1, source_target_pairs={{3,0},{4,1},{5,2},{6,3},{7,4},{0,5},{1,6},{2,7},{11,8},{12,9},{13,... | collective-permute-start | bytes 393224 | tf_op jit(solution)/shard_map/ppermute | solution.py:22
  159.6 3.9 %shard_map.76 = (bf16[32,128,512]{2,1,0:T(8,128)(2,1)}, f32[32,128,1024]{2,1,0:T(8,128)}) custom-call(s32[32,128]{1,0:T(8,128)S(1)} %shard_map.68.plan, bf16[4,128,128]{2,1,0:T(8,128)(2,1)S(1)} %get-tuple-element.120.refs_0_, bf16[4,128,128]{2,1,0:T(8,128)(2,1)S(1)} %collective-permute-done.21.refs_1_, ...), custom_call_target="tpu_custom_call" | custom-call | flops 1073741824 | bytes 6400000 | tf_op jit(solution)/shard_map/pallas_call | solution.py:445
  163.6 4.5 %collective-permute-done.11.refs_4_ = bf16[4,128,128]{2,1,0:T(8,128)(2,1)S(1)} collective-permute-done((bf16[4,128,128]{2,1,0:T(8,128)(2,1)S(1)}, bf16[4,128,128]{2,1,0:T(8,128)(2,1)S(1)}, u32[]{:S(2)}, u32[]{:S(2)}) %collective-permute-start.11) | collective-permute-done | bytes 131104 | tf_op jit(solution)/shard_map/ppermute | solution.py:22
  169.3 3.9 %shard_map.77 = (bf16[32,128,512]{2,1,0:T(8,128)(2,1)}, f32[32,128,1024]{2,1,0:T(8,128)}) custom-call(s32[32,128]{1,0:T(8,128)S(1)} %shard_map.68.plan, bf16[4,128,128]{2,1,0:T(8,128)(2,1)S(1)} %get-tuple-element.100.refs_0_, bf16[4,128,128]{2,1,0:T(8,128)(2,1)S(1)} %collective-permute-done.8.refs_1_, ...), custom_call_target="tpu_custom_call", output_to_operand_aliasing={{0}: (10, {}), {1}: (11, {})} | custom-call | flops 1073741824 | bytes 6400000 | tf_op jit(solution)/shard_map/pallas_call | solution.py:445
  173.2 5.5 %shard_map.78 = (bf16[32,128,512]{2,1,0:T(8,128)(2,1)}, f32[32,128,1024]{2,1,0:T(8,128)}) custom-call(s32[32,128]{1,0:T(8,128)S(1)} %shard_map.68.plan, bf16[4,8,2,128,128]{4,3,2,1,0:T(8,128)(2,1)S(1)} %bitcast.2, bf16[512,1024]{1,0:T(8,128)(2,1)S(1)} %copy-done.1, ...), custom_call_target="tpu_custom_call", output_to_operand_aliasing={{0}: (3, {}), {1}: (4, {})} | custom-call | flops 2147483648 | bytes 12800000 | tf_op jit(solution)/shard_map/pallas_call | solution.py:445
  (56 shorter events, 21.1 us)
Async XLA Ops:
  4.5 24.3 %collective-permute-start.3 = (bf16[2,2048,128]{2,1,0:T(8,128)(2,1)}, bf16[2,2048,128]{2,1,0:T(8,128)(2,1)}, u32[]{:S(2)}, u32[]{:S(2)}) collective-permute-start(bf16[2,2048,128]{2,1,0:T(8,128)(2,1)} %get-tuple-element.86), channel_id=1, source_target_pairs={{7,0},{0,1},{1,2},{2,3},{3,4},{4,5},{5,6},{6,7},{15,8},{8,9},{9,10... | collective-permute-start | bytes 3145736 | tf_op jit(solution)/shard_map/ppermute | solution.py:22
  6.2 25.2 %collective-permute-start.4 = (bf16[2,2048,128]{2,1,0:T(8,128)(2,1)}, bf16[2,2048,128]{2,1,0:T(8,128)(2,1)}, u32[]{:S(2)}, u32[]{:S(2)}) collective-permute-start(bf16[2,2048,128]{2,1,0:T(8,128)(2,1)} %get-tuple-element.87), channel_id=1, source_target_pairs={{1,0},{2,1},{3,2},{4,3},{5,4},{6,5},{7,6},{0,7},{9,8},{10,9},{11,1... | collective-permute-start | bytes 3145736 | tf_op jit(solution)/shard_map/ppermute | solution.py:22
  36.2 137.0 %all-to-all-start = ((bf16[64,128,128]{2,1,0:T(8,128)(2,1)}), bf16[64,128,128]{2,1,0:T(8,128)(2,1)S(1)}, u32[]{:S(2)}, u32[]{:S(2)}) async-start(bf16[64,128,128]{2,1,0:T(8,128)(2,1)} %copy-done), calls=%async_computation | async-start | bytes 4194304 | tf_op jit(solution)/shard_map/all_to_all | solution.py:515
  44.4 65.1 %collective-permute-start.15 = (bf16[8,128,128]{2,1,0:T(8,128)(2,1)S(1)}, bf16[8,128,128]{2,1,0:T(8,128)(2,1)}, u32[]{:S(2)}, u32[]{:S(2)}) collective-permute-start(bf16[8,128,128]{2,1,0:T(8,128)(2,1)S(1)} %get-tuple-element.109), channel_id=1, source_target_pairs={{24,0},{0,8},{8,16},{16,24},{25,1},{1,9},{9,17},{17,25},{26,2},{2,... | collective-permute-start | bytes 786440 | tf_op jit(solution)/shard_map/ppermute | solution.py:22
  45.7 68.4 %collective-permute-start.16 = (bf16[8,128,128]{2,1,0:T(8,128)(2,1)S(1)}, bf16[8,128,128]{2,1,0:T(8,128)(2,1)}, u32[]{:S(2)}, u32[]{:S(2)}) collective-permute-start(bf16[8,128,128]{2,1,0:T(8,128)(2,1)S(1)} %get-tuple-element.110), channel_id=1, source_target_pairs={{16,0},{24,8},{0,16},{8,24},{17,1},{25,9},{1,17},{9,25},{18,2},{26... | collective-permute-start | bytes 786440 | tf_op jit(solution)/shard_map/ppermute | solution.py:22
  45.9 73.9 %collective-permute-start.17 = (bf16[8,128,128]{2,1,0:T(8,128)(2,1)}, bf16[8,128,128]{2,1,0:T(8,128)(2,1)}, u32[]{:S(2)}, u32[]{:S(2)}) collective-permute-start(bf16[8,128,128]{2,1,0:T(8,128)(2,1)} %get-tuple-element.111), channel_id=1, source_target_pairs={{8,0},{16,8},{24,16},{0,24},{9,1},{17,9},{25,17},{1,25},{10,2},{18... | collective-permute-start | bytes 786440 | tf_op jit(solution)/shard_map/ppermute | solution.py:22
  52.1 91.1 %collective-permute-start.5 = (bf16[8,128,128]{2,1,0:T(8,128)(2,1)}, bf16[8,128,128]{2,1,0:T(8,128)(2,1)S(1)}, u32[]{:S(2)}, u32[]{:S(2)}) collective-permute-start(bf16[8,128,128]{2,1,0:T(8,128)(2,1)} %get-tuple-element.97), channel_id=1, source_target_pairs={{24,0},{0,8},{8,16},{16,24},{25,1},{1,9},{9,17},{17,25},{26,2},{2,... | collective-permute-start | bytes 786440 | tf_op jit(solution)/shard_map/ppermute | solution.py:22
  52.3 90.8 %collective-permute-start.6 = (bf16[8,128,128]{2,1,0:T(8,128)(2,1)}, bf16[8,128,128]{2,1,0:T(8,128)(2,1)}, u32[]{:S(2)}, u32[]{:S(2)}) collective-permute-start(bf16[8,128,128]{2,1,0:T(8,128)(2,1)} %get-tuple-element.98), channel_id=1, source_target_pairs={{16,0},{24,8},{0,16},{8,24},{17,1},{25,9},{1,17},{9,25},{18,2},{26... | collective-permute-start | bytes 786440 | tf_op jit(solution)/shard_map/ppermute | solution.py:22
  119.8 23.5 %collective-permute-start.7 = (bf16[8,128,128]{2,1,0:T(8,128)(2,1)}, bf16[8,128,128]{2,1,0:T(8,128)(2,1)S(1)}, u32[]{:S(2)}, u32[]{:S(2)}) collective-permute-start(bf16[8,128,128]{2,1,0:T(8,128)(2,1)} %copy-done.2), channel_id=1, source_target_pairs={{8,0},{16,8},{24,16},{0,24},{9,1},{17,9},{25,17},{1,25},{10,2},{18... | collective-permute-start | bytes 786440 | tf_op jit(solution)/shard_map/ppermute | solution.py:22
  122.0 11.7 %collective-permute-start.18 = (bf16[1,128,128]{2,1,0:T(8,128)(2,1)S(1)}, bf16[1,128,128]{2,1,0:T(8,128)(2,1)S(1)}, u32[]{:S(2)}, u32[]{:S(2)}) collective-permute-start(bf16[1,128,128]{2,1,0:T(8,128)(2,1)S(1)} %get-tuple-element.117), channel_id=1, source_target_pairs={{24,0},{0,8},{8,16},{16,24},{25,1},{1,9},{9,17},{17,25},{26,2},{2,... | collective-permute-start | bytes 98312 | tf_op jit(solution)/shard_map/ppermute | solution.py:22
  122.0 11.7 %collective-permute-start.19 = (bf16[1,128,128]{2,1,0:T(8,128)(2,1)S(1)}, bf16[1,128,128]{2,1,0:T(8,128)(2,1)S(1)}, u32[]{:S(2)}, u32[]{:S(2)}) collective-permute-start(bf16[1,128,128]{2,1,0:T(8,128)(2,1)S(1)} %get-tuple-element.118), channel_id=1, source_target_pairs={{16,0},{24,8},{0,16},{8,24},{17,1},{25,9},{1,17},{9,25},{18,2},{26... | collective-permute-start | bytes 98312 | tf_op jit(solution)/shard_map/ppermute | solution.py:22
  137.9 9.4 %collective-permute-start.21 = (bf16[4,128,128]{2,1,0:T(8,128)(2,1)S(1)}, bf16[4,128,128]{2,1,0:T(8,128)(2,1)S(1)}, u32[]{:S(2)}, u32[]{:S(2)}) collective-permute-start(bf16[4,128,128]{2,1,0:T(8,128)(2,1)S(1)} %get-tuple-element.121), channel_id=1, source_target_pairs={{7,0},{0,1},{1,2},{2,3},{3,4},{4,5},{5,6},{6,7},{15,8},{8,9},{9,10... | collective-permute-start | bytes 393224 | tf_op jit(solution)/shard_map/ppermute | solution.py:22
  141.4 7.3 %collective-permute-start.22 = (bf16[4,128,128]{2,1,0:T(8,128)(2,1)S(1)}, bf16[4,128,128]{2,1,0:T(8,128)(2,1)S(1)}, u32[]{:S(2)}, u32[]{:S(2)}) collective-permute-start(bf16[4,128,128]{2,1,0:T(8,128)(2,1)S(1)} %get-tuple-element.122), channel_id=1, source_target_pairs={{6,0},{7,1},{0,2},{1,3},{2,4},{3,5},{4,6},{5,7},{14,8},{15,9},{8,1... | collective-permute-start | bytes 393224 | tf_op jit(solution)/shard_map/ppermute | solution.py:22
  143.1 6.5 %collective-permute-start.23 = (bf16[4,128,128]{2,1,0:T(8,128)(2,1)S(1)}, bf16[4,128,128]{2,1,0:T(8,128)(2,1)S(1)}, u32[]{:S(2)}, u32[]{:S(2)}) collective-permute-start(bf16[4,128,128]{2,1,0:T(8,128)(2,1)S(1)} %get-tuple-element.123), channel_id=1, source_target_pairs={{5,0},{6,1},{7,2},{0,3},{1,4},{2,5},{3,6},{4,7},{13,8},{14,9},{15,... | collective-permute-start | bytes 393224 | tf_op jit(solution)/shard_map/ppermute | solution.py:22
  143.1 10.5 %collective-permute-start.24 = (bf16[4,128,128]{2,1,0:T(8,128)(2,1)S(1)}, bf16[4,128,128]{2,1,0:T(8,128)(2,1)S(1)}, u32[]{:S(2)}, u32[]{:S(2)}) collective-permute-start(bf16[4,128,128]{2,1,0:T(8,128)(2,1)S(1)} %get-tuple-element.124), channel_id=1, source_target_pairs={{4,0},{5,1},{6,2},{7,3},{0,4},{1,5},{2,6},{3,7},{12,8},{13,9},{14,... | collective-permute-start | bytes 393224 | tf_op jit(solution)/shard_map/ppermute | solution.py:22
  143.3 12.5 %collective-permute-start.25 = (bf16[4,128,128]{2,1,0:T(8,128)(2,1)S(1)}, bf16[4,128,128]{2,1,0:T(8,128)(2,1)S(1)}, u32[]{:S(2)}, u32[]{:S(2)}) collective-permute-start(bf16[4,128,128]{2,1,0:T(8,128)(2,1)S(1)} %get-tuple-element.125), channel_id=1, source_target_pairs={{3,0},{4,1},{5,2},{6,3},{7,4},{0,5},{1,6},{2,7},{11,8},{12,9},{13,... | collective-permute-start | bytes 393224 | tf_op jit(solution)/shard_map/ppermute | solution.py:22
  147.3 8.5 %collective-permute-start.26 = (bf16[4,128,128]{2,1,0:T(8,128)(2,1)S(1)}, bf16[4,128,128]{2,1,0:T(8,128)(2,1)S(1)}, u32[]{:S(2)}, u32[]{:S(2)}) collective-permute-start(bf16[4,128,128]{2,1,0:T(8,128)(2,1)S(1)} %get-tuple-element.126), channel_id=1, source_target_pairs={{2,0},{3,1},{4,2},{5,3},{6,4},{7,5},{0,6},{1,7},{10,8},{11,9},{12,... | collective-permute-start | bytes 393224 | tf_op jit(solution)/shard_map/ppermute | solution.py:22
  148.6 8.4 %collective-permute-start.27 = (bf16[4,128,128]{2,1,0:T(8,128)(2,1)S(1)}, bf16[4,128,128]{2,1,0:T(8,128)(2,1)S(1)}, u32[]{:S(2)}, u32[]{:S(2)}) collective-permute-start(bf16[4,128,128]{2,1,0:T(8,128)(2,1)S(1)} %get-tuple-element.127), channel_id=1, source_target_pairs={{1,0},{2,1},{3,2},{4,3},{5,4},{6,5},{7,6},{0,7},{9,8},{10,9},{11,1... | collective-permute-start | bytes 393224 | tf_op jit(solution)/shard_map/ppermute | solution.py:22
  149.6 9.5 %collective-permute-start.8 = (bf16[4,128,128]{2,1,0:T(8,128)(2,1)S(1)}, bf16[4,128,128]{2,1,0:T(8,128)(2,1)S(1)}, u32[]{:S(2)}, u32[]{:S(2)}) collective-permute-start(bf16[4,128,128]{2,1,0:T(8,128)(2,1)S(1)} %get-tuple-element.101), channel_id=1, source_target_pairs={{7,0},{0,1},{1,2},{2,3},{3,4},{4,5},{5,6},{6,7},{15,8},{8,9},{9,10... | collective-permute-start | bytes 393224 | tf_op jit(solution)/shard_map/ppermute | solution.py:22
  155.8 7.7 %collective-permute-start.10 = (bf16[4,128,128]{2,1,0:T(8,128)(2,1)S(1)}, bf16[4,128,128]{2,1,0:T(8,128)(2,1)S(1)}, u32[]{:S(2)}, u32[]{:S(2)}) collective-permute-start(bf16[4,128,128]{2,1,0:T(8,128)(2,1)S(1)} %get-tuple-element.103), channel_id=1, source_target_pairs={{5,0},{6,1},{7,2},{0,3},{1,4},{2,5},{3,6},{4,7},{13,8},{14,9},{15,... | collective-permute-start | bytes 393224 | tf_op jit(solution)/shard_map/ppermute | solution.py:22
  155.8 12.2 %collective-permute-start.11 = (bf16[4,128,128]{2,1,0:T(8,128)(2,1)S(1)}, bf16[4,128,128]{2,1,0:T(8,128)(2,1)S(1)}, u32[]{:S(2)}, u32[]{:S(2)}) collective-permute-start(bf16[4,128,128]{2,1,0:T(8,128)(2,1)S(1)} %get-tuple-element.104), channel_id=1, source_target_pairs={{4,0},{5,1},{6,2},{7,3},{0,4},{1,5},{2,6},{3,7},{12,8},{13,9},{14,... | collective-permute-start | bytes 393224 | tf_op jit(solution)/shard_map/ppermute | solution.py:22
  157.1 12.2 %collective-permute-start.12 = (bf16[4,128,128]{2,1,0:T(8,128)(2,1)S(1)}, bf16[4,128,128]{2,1,0:T(8,128)(2,1)S(1)}, u32[]{:S(2)}, u32[]{:S(2)}) collective-permute-start(bf16[4,128,128]{2,1,0:T(8,128)(2,1)S(1)} %get-tuple-element.105), channel_id=1, source_target_pairs={{3,0},{4,1},{5,2},{6,3},{7,4},{0,5},{1,6},{2,7},{11,8},{12,9},{13,... | collective-permute-start | bytes 393224 | tf_op jit(solution)/shard_map/ppermute | solution.py:22
  159.1 10.2 %collective-permute-start.13 = (bf16[4,128,128]{2,1,0:T(8,128)(2,1)S(1)}, bf16[4,128,128]{2,1,0:T(8,128)(2,1)S(1)}, u32[]{:S(2)}, u32[]{:S(2)}) collective-permute-start(bf16[4,128,128]{2,1,0:T(8,128)(2,1)S(1)} %get-tuple-element.106), channel_id=1, source_target_pairs={{2,0},{3,1},{4,2},{5,3},{6,4},{7,5},{0,6},{1,7},{10,8},{11,9},{12,... | collective-permute-start | bytes 393224 | tf_op jit(solution)/shard_map/ppermute | solution.py:22
  159.2 10.1 %collective-permute-start.14 = (bf16[4,128,128]{2,1,0:T(8,128)(2,1)S(1)}, bf16[4,128,128]{2,1,0:T(8,128)(2,1)S(1)}, u32[]{:S(2)}, u32[]{:S(2)}) collective-permute-start(bf16[4,128,128]{2,1,0:T(8,128)(2,1)S(1)} %get-tuple-element.107), channel_id=1, source_target_pairs={{1,0},{2,1},{3,2},{4,3},{5,4},{6,5},{7,6},{0,7},{9,8},{10,9},{11,1... | collective-permute-start | bytes 393224 | tf_op jit(solution)/shard_map/ppermute | solution.py:22
  (9 other events, 63.2 us)

commit v5 on v4

--- a/solution.py
+++ b/solution.py
@@ -43,75 +43,41 @@
     return offsets[m, t] - t * R, offsets[m, t + 1] - t * R
 
 
-def edges_kernel(offsets, embed, head, lead_out, trail_out, rows, wide, sems):
+def edges_kernel(offsets, embed, head, lead_out, trail_out, lead_in, trail_in, sems, out_sems):
     quarter = lead_out.shape[1]
-    raws = [embed, head]
     copies = []
-    for m in range(2):
+    writes = []
+    for m, raw in enumerate([embed, head]):
         first = (R - my_span(offsets, m)[0]) & -ALIGN
         window = pl.ds(pl.multiple_of(first, ALIGN), quarter + ALIGN)
-        lead = pltpu.make_async_copy(
-            raws[m].at[pl.ds(0, quarter)], rows.at[2 * m, pl.ds(0, quarter)], sems.at[2 * m]
+        copies.append(
+            pltpu.make_async_copy(raw.at[pl.ds(0, quarter)], lead_in.at[m], sems.at[2 * m])
         )
-        trail = pltpu.make_async_copy(raws[m].at[window], rows.at[2 * m + 1], sems.at[2 * m + 1])
-        lead.start()
-        trail.start()
-        copies.append((lead, trail))
-    blocks = quarter // BLOCK
-    for m in range(2):
-        lead, trail = copies[m]
-        before, after = my_span(offsets, m)
-        lead.wait()
-        count = jnp.clip(-before, 0, quarter)
-        used = (count + BLOCK - 1) >> log2(BLOCK)
-
-        def widen_lead(i, _):
-            at = pl.multiple_of(i * BLOCK, BLOCK)
-            wide[pl.ds(quarter + at, BLOCK), :] = rows[2 * m, pl.ds(at, BLOCK), :].astype(jnp.float32)
-            return _
-
-        lax.fori_loop(0, used, widen_lead, 0)
-
-        def put_lead(i, _):
-            at = pl.multiple_of(i * BLOCK, BLOCK)
-            lead_out[m, pl.ds(at, BLOCK), :] = wide[pl.ds(count + at, BLOCK), :].astype(jnp.bfloat16)
-            return _
-
-        lax.fori_loop(blocks - used, blocks, put_lead, 0)
-        trail.wait()
-        shift = (R - before) & (ALIGN - 1)
-        used = (jnp.clip(after - R, 0, quarter) + BLOCK - 1) >> log2(BLOCK)
-
-        def widen_trail(i, _):
-            at = pl.multiple_of(i * BLOCK, BLOCK)
-            wide[pl.ds(at, BLOCK), :] = rows[2 * m + 1, pl.ds(at, BLOCK), :].astype(jnp.float32)
-            return _
-
-        lax.fori_loop(0, jnp.minimum(used + 1, blocks), widen_trail, 0)
-
-        @pl.when(used == blocks)
-        def _last():
-            wide[pl.ds(quarter, ALIGN), :] = rows[2 * m + 1, pl.ds(quarter, ALIGN), :].astype(jnp.float32)
-
-        def put_trail(i, _):
-            at = pl.multiple_of(i * BLOCK, BLOCK)
-            trail_out[m, pl.ds(at, BLOCK), :] = wide[pl.ds(shift + at, BLOCK), :].astype(jnp.bfloat16)
-            return _
-
-        lax.fori_loop(0, used, put_trail, 0)
+        copies.append(pltpu.make_async_copy(raw.at[window], trail_in.at[m], sems.at[2 * m + 1]))
+        writes.append(pltpu.make_async_copy(lead_in.at[m], lead_out.at[m], out_sems.at[2 * m]))
+        writes.append(pltpu.make_async_copy(trail_in.at[m], trail_out.at[m], out_sems.at[2 * m + 1]))
+    for copy in copies:
+        copy.start()
+    for copy, write in zip(copies, writes):
+        copy.wait()
+        write.start()
+    for write in writes:
+        write.wait()
 
 
 def cut_edges(offsets, embed, head, quarter):
     width = embed.shape[1]
-    shape = jax.ShapeDtypeStruct((2, quarter, width), embed.dtype)
     return pl.pallas_call(
         edges_kernel,
-        out_shape=(shape, shape),
+        out_shape=[
+            jax.ShapeDtypeStruct((2, rows, width), embed.dtype) for rows in (quarter, quarter + ALIGN)
+        ],
         in_specs=[smem(), in_hbm(), in_hbm()],
-        out_specs=[vmem()] * 2,
+        out_specs=[in_hbm()] * 2,
         scratch_shapes=[
-            pltpu.VMEM((4, quarter + ALIGN, width), embed.dtype),
-            pltpu.VMEM((2 * quarter, width), jnp.float32),
+            pltpu.VMEM((2, quarter, width), embed.dtype),
+            pltpu.VMEM((2, quarter + ALIGN, width), embed.dtype),
+            pltpu.SemaphoreType.DMA((4,)),
             pltpu.SemaphoreType.DMA((4,)),
         ],
         compiler_params=pltpu.CompilerParams(vmem_limit_bytes=61 * MIB),
@@ -310,48 +276,60 @@
     )(plan, offsets, embed, head)
 
 
-def overlay_kernel(arrays, plan, offsets, *refs):
-    packed, left, right, outs = refs[: len(arrays)], refs[-len(arrays) - 2], refs[-len(arrays) - 1], refs[-len(arrays) :]
-    quarter = left.shape[1]
+def overlay_kernel(arrays, n_tensor, plan, offsets, *refs):
+    count = len(arrays)
+    packed, left, right, outs, wide = refs[:count], refs[count], refs[count + 1], refs[-count - 1 : -1], refs[-1]
+    quarter = right.shape[1]
     t = lax.axis_index("tensor")
     begins = [offsets[m, t] - t * R for m in range(2)]
     ends = [offsets[m, t + 1] - t * R for m in range(2)]
+    behind = wrap(t + n_tensor - 1, n_tensor)
+    shifts = [(R - offsets[m, behind] + behind * R) & (ALIGN - 1) for m in range(2)]
     for parts, source, out in zip(arrays, packed, outs):
         out[...] = source[...]
-        for begin, count, which in parts:
+        for begin, blocks, which in parts:
 
             def fix(i, _, begin=begin, which=which, out=out):
                 m, first = split_block(which(plan, i))
                 before = jnp.where(m == 0, begins[0], begins[1])
                 after = jnp.where(m == 0, ends[0], ends[1])
 
-                @pl.when(first < before)
-                def _left():
-                    row = first + lax.broadcasted_iota(jnp.int32, (BLOCK, 1), 0)
-                    edge = left[m, pl.ds(pl.multiple_of(first, BLOCK), BLOCK), :]
-                    out[begin + i] = jnp.where(row < before, edge, out[begin + i])
-
-                @pl.when(first + BLOCK > after)
-                def _right():
-                    row = first + lax.broadcasted_iota(jnp.int32, (BLOCK, 1), 0)
-                    at = pl.multiple_of(first - (R - quarter), BLOCK)
-                    edge = right[m, pl.ds(at, BLOCK), :]
-                    out[begin + i] = jnp.where(row >= after, edge, out[begin + i])
+                @pl.when((first < before) | (first + BLOCK > after))
+                def _edge():
+                    @pl.when(first < before)
+                    def _left():
+                        row = first + lax.broadcasted_iota(jnp.int32, (BLOCK, 1), 0)
+                        window = pl.ds(pl.multiple_of(first, BLOCK), BLOCK + ALIGN)
+                        wide[pl.ds(0, BLOCK + ALIGN), :] = left[m, window, :].astype(jnp.float32)
+                        shift = jnp.where(m == 0, shifts[0], shifts[1])
+                        edge = wide[pl.ds(shift, BLOCK), :].astype(out.dtype)
+                        out[begin + i] = jnp.where(row < before, edge, out[begin + i])
+
+                    @pl.when(first + BLOCK > after)
+                    def _right():
+                        row = first + lax.broadcasted_iota(jnp.int32, (BLOCK, 1), 0)
+                        start = first - after
+                        at = jnp.clip(start & -ALIGN, 0, quarter - BLOCK - ALIGN)
+                        window = pl.ds(pl.multiple_of(at, ALIGN), BLOCK + ALIGN)
+                        wide[pl.ds(BLOCK, BLOCK + ALIGN), :] = right[m, window, :].astype(jnp.float32)
+                        edge = wide[pl.ds(BLOCK + start - at, BLOCK), :].astype(out.dtype)
+                        out[begin + i] = jnp.where(row >= after, edge, out[begin + i])
 
                 return _
 
-            lax.fori_loop(0, count, fix, 0)
+            lax.fori_loop(0, blocks, fix, 0)
 
 
 def overlay(layout, arrays, plan, offsets, packed, left, right):
     return pl.pallas_call(
-        functools.partial(overlay_kernel, arrays),
+        functools.partial(overlay_kernel, arrays, layout.n_tensor),
         out_shape=[
             jax.ShapeDtypeStruct((layout.size(parts),) + packed[0].shape[1:], left.dtype)
             for parts in arrays
         ],
         in_specs=[smem()] * 2 + [vmem()] * (len(packed) + 2),
         out_specs=[vmem()] * len(arrays),
+        scratch_shapes=[pltpu.VMEM((2 * BLOCK + ALIGN, packed[0].shape[2]), jnp.float32)],
         compiler_params=pltpu.CompilerParams(vmem_limit_bytes=16 * MIB),
         cost_estimate=pl.CostEstimate(flops=1_000_000_000, bytes_accessed=4_000_000, transcendentals=0),
     )(plan, offsets, *packed, left, right)
@@ -396,13 +374,15 @@
 def store_kernel(layout, ranks, direct, count, plan, *refs):
     n_data, n_tensor, per_pair = layout.n_data, layout.n_tensor, layout.per_pair
     incoming, probe = refs[:count], refs[count]
-    stored, sketch, full, product, sems = refs[-5:]
+    stored, sketch, full, product, places, sems, plan_sem = refs[-7:]
     width = incoming[0].shape[-1]
     slots = len(ranks) * n_tensor
+    fetch = pltpu.make_async_copy(plan, places, plan_sem)
+    fetch.start()
     copies = []
     begin = 0
     while begin < slots:
-        step = min(max(begin, 1), 4, slots - begin)
+        step = min(2, slots - begin)
         for i in range(begin, begin + step):
             k, hop = i // n_tensor, i % n_tensor
             for s in range(n_data):
@@ -416,11 +396,13 @@
         rows = full[span].reshape(step * BLOCK, n_data * width)
         dot = jnp.dot(rows, probe[...], preferred_element_type=jnp.float32)
         product[span] = dot.reshape(step, BLOCK, probe.shape[1])
+        if begin == 0:
+            fetch.wait()
         for i in range(begin, begin + step):
             k, u = i // n_tensor, i % n_tensor
             if direct:
                 u = wrap(lax.axis_index("tensor") - u + n_tensor, n_tensor)
-            slot = plan[u * per_pair + ranks[k], per_pair + 1]
+            slot = places[u * per_pair + ranks[k], per_pair + 1]
             copies.append(pltpu.make_async_copy(full.at[i], stored.at[slot], sems.at[2 * i]))
             copies.append(pltpu.make_async_copy(product.at[i], sketch.at[slot], sems.at[2 * i + 1]))
             copies[-2].start()
@@ -445,12 +427,14 @@
     return pl.pallas_call(
         functools.partial(store_kernel, layout, ranks, direct, count),
         out_shape=out_shape,
-        in_specs=[smem()] + [vmem()] * (count + 1) + [any_space() for _ in held],
+        in_specs=[any_space()] + [vmem()] * (count + 1) + [any_space() for _ in held],
         out_specs=[any_space(), any_space()],
         scratch_shapes=[
             pltpu.VMEM((slots, BLOCK, columns), incoming[0].dtype),
             pltpu.VMEM((slots, BLOCK, sketch_width), jnp.float32),
+            pltpu.SMEM(plan.shape, jnp.int32),
             pltpu.SemaphoreType.DMA((2 * slots,)),
+            pltpu.SemaphoreType.DMA,
         ],
         compiler_params=pltpu.CompilerParams(vmem_limit_bytes=(8 + 7 * slots // 8) * MIB),
         input_output_aliases={count + 2: 0, count + 3: 1} if held else {},
@@ -494,7 +478,10 @@
     ranks = list(range(per_pair - layout.direct_ranks))
     rest = [layout.stage(rank) for rank in ranks[1:]] + [layout.direct()]
     if ranks:
-        first = pack_all(layout.stage(0), 60)
+        apart = near_half(n_data)
+        whole, first = layout.stage(0), {}
+        for shifts in (apart[:1], apart[1:] + [0]):
+            first.update(zip(shifts, pack_all([whole[s] for s in shifts], 60)))
         stages = {0: send_z(first)}
         rest = [layout.late() + rest[0]] + rest[1:]
     packed = pack_all([parts for group in rest for parts in group], 50)
@@ -508,7 +495,7 @@
             stages[rank] = send_z(complete[0][n_data * rank :])
 
         def resend(early):
-            return send_z(overlay_all(layout.stage(0), first))
+            return send_z(overlay_all(layout.stage(0), [first[s] for s in every_z]))
 
         crowded = plan[0, per_pair + 2] > LATE
         stages[0] = lax.cond(crowded, resend, lambda early: early, stages[0])
@@ -528,6 +515,10 @@
     return tuple(store_ranks(layout, last, True, plan, [direct], probe, outputs))
 
 
+def near_half(n_data):
+    return sorted(range(1, n_data), key=lambda s: (abs(2 * s - n_data), s))
+
+
 def solution(mesh):
     return jax.shard_map(
         shards,

time: 179 us -> 178 us (level)
    pallas_call x2 -> x3, Pallas kernels: 9.89 us -> 11.6 us  [pack(): pl.pallas_call(functools.partial(pack_kernel, arrays), out_shape=[jax.Sha...]
    unnamed x14 -> x12, local copies, waits for them, and re-layouts: 3.72 us -> 3.02 us
  transfers between devices with their start and end apart: 26 -> 26, of which waited for: 10 -> 9; matrix products, arithmetic and copies ran while one was open for 0% -> 0% of each run, Pallas kernels for 14% -> 14%
where the time goes in v5:
time: 178 us; the launch traced here: 177 us
  waiting for transfers between devices  101 us (57%)
  Pallas kernels  37.1 us (21%)
  starting transfers between devices  34.8 us (20%)
  local copies, waits for them, and re-layouts  3.68 us (2%)
    ppermute x25, waiting for transfers between devices, from_behind(): return lax.ppermute(block, axis, route)  101 us
    ppermute x25, starting transfers between devices, from_behind(): return lax.ppermute(block, axis, route)  29.7 us
    pallas_call x3, Pallas kernels, store_ranks(): pl.pallas_call(functools.partial(store_kernel, layout, ranks, direct, cou...  11.7 us
    pallas_call x3, Pallas kernels, pack(): pl.pallas_call(functools.partial(pack_kernel, arrays), out_shape=[jax.Sha...  11.6 us
    pallas_call x2, Pallas kernels, overlay(): pl.pallas_call(functools.partial(overlay_kernel, arrays, layout.n_tensor)...  6.83 us
    all_to_all x1, starting transfers between devices, shards(): lax.all_to_all(complete[-1][0], ('dp', 'tensor'), split_axis=0, concat_ax...  5.12 us
  transfers between devices with their start and end apart: 26, of which 9 were waited for; matrix products, arithmetic and copies ran while one was open for 0% of the time, Pallas kernels for 14%

profile of v5, /device:TPU:19, one launch (start us, length us, event | category | flops | bytes accessed | tf_op | source)
XLA Modules:
  0.0 177.5 jit_solution(16652587439098728122)
XLA Ops:
  0.6 3.2 %shard_map.70 = (bf16[2,2048,128]{2,1,0:T(8,128)(2,1)}, bf16[2,2064,128]{2,1,0:T(8,128)(2,1)}) custom-call(s32[2,9]{1,0:T(2,128)} %offsets.13, bf16[12288,128]{1,0:T(8,128)(2,1)} %embed.7, bf16[12288,128]{1,0:T(8,128)(2,1)} %head.7), custom_call_target="tpu_custom_call" | custom-call | tf_op jit(solution)/shard_map/pallas_call | solution.py:70
  3.9 1.8 %collective-permute-start.3 = (bf16[2,2064,128]{2,1,0:T(8,128)(2,1)}, bf16[2,2064,128]{2,1,0:T(8,128)(2,1)}, u32[]{:S(2)}, u32[]{:S(2)}) collective-permute-start(bf16[2,2064,128]{2,1,0:T(8,128)(2,1)} %get-tuple-element.85), channel_id=1, source_target_pairs={{7,0},{0,1},{1,2},{2,3},{3,4},{4,5},{5,6},{6,7},{15,8},{8,9},{9,10... | collective-permute-start | bytes 3170312 | tf_op jit(solution)/shard_map/ppermute | solution.py:22
  7.0 6.3 %shard_map.69 = (bf16[1,128,128]{2,1,0:T(8,128)(2,1)S(1)}, bf16[1,128,128]{2,1,0:T(8,128)(2,1)S(1)}, bf16[1,128,128]{2,1,0:T(8,128)(2,1)S(1)}, bf16[1,128,128]{2...) custom-call(s32[32,128]{1,0:T(8,128)S(1)} %shard_map.68.plan, ...), custom_call_target="tpu_custom_call" | custom-call | flops 3000000000 | bytes 7000000 | tf_op jit(solution)/shard_map/pallas_call | solution.py:262
  13.4 17.4 %collective-permute-done.4.refs_2_.refs_9_ = bf16[2,2048,128]{2,1,0:T(8,128)(2,1)} collective-permute-done((bf16[2,2048,128]{2,1,0:T(8,128)(2,1)}, bf16[2,2048,128]{2,1,0:T(8,128)(2,1)}, u32[]{:S(2)}, u32[]{:S(2)}) %collective-permute-start.4) | collective-permute-done | bytes 1048608 | tf_op jit(solution)/shard_map/ppermute | solution.py:22
  30.8 3.4 %shard_map.71 = bf16[64,128,128]{2,1,0:T(8,128)(2,1)S(1)} custom-call(s32[32,128]{1,0:T(8,128)S(1)} %shard_map.68.plan, s32[2,9]{1,0:T(2,128)S(1)} %copy-done.4, bf16[64,128,128]{2,1,0:T(8,128)(2,1)S(1)} %get-tuple-element.84.refs_0_, bf16[2,2064,128]{2,1,0:T(8,128)(2,1)} %collective-permute-done.3.refs_1_.refs_8_, ...), custom_call_target="tpu_custom_call" | custom-call | flops 1000000000 | bytes 4000000 | tf_op jit(solution)/shard_map/pallas_call | solution.py:324
  35.5 5.1 %all-to-all-start = ((bf16[64,128,128]{2,1,0:T(8,128)(2,1)}), bf16[64,128,128]{2,1,0:T(8,128)(2,1)S(1)}, u32[]{:S(2)}, u32[]{:S(2)}) async-start(bf16[64,128,128]{2,1,0:T(8,128)(2,1)} %copy-done), calls=%async_computation | async-start | bytes 4194304 | tf_op jit(solution)/shard_map/all_to_all | solution.py:502
  40.7 1.9 %shard_map.75 = bf16[8,128,128]{2,1,0:T(8,128)(2,1)S(1)} custom-call(s32[32,128]{1,0:T(8,128)S(1)} %shard_map.68.plan, s32[2,9]{1,0:T(2,128)S(1)} %copy-done.4, bf16[12288,128]{1,0:T(8,128)(2,1)} %embed.7, bf16[12288,128]{1,0:T(8,128)(2,1)} %head.7), custom_call_target="tpu_custom_call" | custom-call | flops 240000000 | bytes 560000 | tf_op jit(solution)/shard_map/pallas_call | solution.py:262
  42.9 3.3 %shard_map.74 = (bf16[8,128,128]{2,1,0:T(8,128)(2,1)}, bf16[8,128,128]{2,1,0:T(8,128)(2,1)}, bf16[8,128,128]{2,1,0:T(8,128)(2,1)}) custom-call(s32[32,128]{1,0:T(8,128)S(1)} %shard_map.68.plan, s32[2,9]{1,0:T(2,128)S(1)} %copy-done.4, bf16[12288,128]{1,0:T(8,128)(2,1)} %embed.7, bf16[12288,128]{1,0:T(8,128)(2,1)} %head.7), custom_call_target="tpu_custom_call" | custom-call | flops 720000000 | bytes 1680000 | tf_op jit(solution)/shard_map/pallas_call | solution.py:262
  48.5 3.4 %shard_map.72 = (bf16[1,128,128]{2,1,0:T(8,128)(2,1)S(1)}, bf16[1,128,128]{2,1,0:T(8,128)(2,1)S(1)}, bf16[1,128,128]{2,1,0:T(8,128)(2,1)S(1)}, bf16[1,128,128]{2...) custom-call(s32[32,128]{1,0:T(8,128)S(1)} %shard_map.68.plan, ...), custom_call_target="tpu_custom_call" | custom-call | flops 1000000000 | bytes 4000000 | tf_op jit(solution)/shard_map/pallas_call | solution.py:324
  53.7 2.1 %collective-permute-start.6 = (bf16[8,128,128]{2,1,0:T(8,128)(2,1)}, bf16[8,128,128]{2,1,0:T(8,128)(2,1)}, u32[]{:S(2)}, u32[]{:S(2)}) collective-permute-start(bf16[8,128,128]{2,1,0:T(8,128)(2,1)} %get-tuple-element.97), channel_id=1, source_target_pairs={{16,0},{24,8},{0,16},{8,24},{17,1},{25,9},{1,17},{9,25},{18,2},{26... | collective-permute-start | bytes 786440 | tf_op jit(solution)/shard_map/ppermute | solution.py:22
  57.0 56.9 %collective-permute-done.16 = bf16[8,128,128]{2,1,0:T(8,128)(2,1)} collective-permute-done((bf16[8,128,128]{2,1,0:T(8,128)(2,1)S(1)}, bf16[8,128,128]{2,1,0:T(8,128)(2,1)}, u32[]{:S(2)}, u32[]{:S(2)}) %collective-permute-start.16) | collective-permute-done | bytes 262176 | tf_op jit(solution)/shard_map/ppermute | solution.py:22
  114.9 4.7 %collective-permute-done.17 = bf16[8,128,128]{2,1,0:T(8,128)(2,1)} collective-permute-done((bf16[8,128,128]{2,1,0:T(8,128)(2,1)}, bf16[8,128,128]{2,1,0:T(8,128)(2,1)}, u32[]{:S(2)}, u32[]{:S(2)}) %collective-permute-start.17) | collective-permute-done | bytes 262176 | tf_op jit(solution)/shard_map/ppermute | solution.py:22
  119.6 2.2 %collective-permute-start.7 = (bf16[8,128,128]{2,1,0:T(8,128)(2,1)}, bf16[8,128,128]{2,1,0:T(8,128)(2,1)S(1)}, u32[]{:S(2)}, u32[]{:S(2)}) collective-permute-start(bf16[8,128,128]{2,1,0:T(8,128)(2,1)} %get-tuple-element.98), channel_id=1, source_target_pairs={{8,0},{16,8},{24,16},{0,24},{9,1},{17,9},{25,17},{1,25},{10,2},{18... | collective-permute-start | bytes 786440 | tf_op jit(solution)/shard_map/ppermute | solution.py:22
  123.0 10.5 %collective-permute-done.18.refs_5_ = bf16[1,128,128]{2,1,0:T(8,128)(2,1)S(1)} collective-permute-done((bf16[1,128,128]{2,1,0:T(8,128)(2,1)S(1)}, bf16[1,128,128]{2,1,0:T(8,128)(2,1)S(1)}, u32[]{:S(2)}, u32[]{:S(2)}) %collective-permute-start.18) | collective-permute-done | bytes 32800 | tf_op jit(solution)/shard_map/ppermute | solution.py:22
  133.5 2.8 %collective-permute-done.20.refs_7_ = bf16[1,128,128]{2,1,0:T(8,128)(2,1)S(1)} collective-permute-done((bf16[1,128,128]{2,1,0:T(8,128)(2,1)S(1)}, bf16[1,128,128]{2,1,0:T(8,128)(2,1)S(1)}, u32[]{:S(2)}, u32[]{:S(2)}) %collective-permute-start.20) | collective-permute-done | bytes 32800 | tf_op jit(solution)/shard_map/ppermute | solution.py:22
  137.7 3.5 %collective-permute-start.21 = (bf16[4,128,128]{2,1,0:T(8,128)(2,1)S(1)}, bf16[4,128,128]{2,1,0:T(8,128)(2,1)S(1)}, u32[]{:S(2)}, u32[]{:S(2)}) collective-permute-start(bf16[4,128,128]{2,1,0:T(8,128)(2,1)S(1)} %get-tuple-element.119), channel_id=1, source_target_pairs={{7,0},{0,1},{1,2},{2,3},{3,4},{4,5},{5,6},{6,7},{15,8},{8,9},{9,10... | collective-permute-start | bytes 393224 | tf_op jit(solution)/shard_map/ppermute | solution.py:22
  143.2 2.0 %collective-permute-start.25 = (bf16[4,128,128]{2,1,0:T(8,128)(2,1)S(1)}, bf16[4,128,128]{2,1,0:T(8,128)(2,1)S(1)}, u32[]{:S(2)}, u32[]{:S(2)}) collective-permute-start(bf16[4,128,128]{2,1,0:T(8,128)(2,1)S(1)} %get-tuple-element.123), channel_id=1, source_target_pairs={{3,0},{4,1},{5,2},{6,3},{7,4},{0,5},{1,6},{2,7},{11,8},{12,9},{13,... | collective-permute-start | bytes 393224 | tf_op jit(solution)/shard_map/ppermute | solution.py:22
  149.4 4.1 %collective-permute-start.8 = (bf16[4,128,128]{2,1,0:T(8,128)(2,1)S(1)}, bf16[4,128,128]{2,1,0:T(8,128)(2,1)S(1)}, u32[]{:S(2)}, u32[]{:S(2)}) collective-permute-start(bf16[4,128,128]{2,1,0:T(8,128)(2,1)S(1)} %get-tuple-element.100), channel_id=1, source_target_pairs={{7,0},{0,1},{1,2},{2,3},{3,4},{4,5},{5,6},{6,7},{15,8},{8,9},{9,10... | collective-permute-start | bytes 393224 | tf_op jit(solution)/shard_map/ppermute | solution.py:22
  153.5 2.2 %collective-permute-start.9 = (bf16[4,128,128]{2,1,0:T(8,128)(2,1)S(1)}, bf16[4,128,128]{2,1,0:T(8,128)(2,1)S(1)}, u32[]{:S(2)}, u32[]{:S(2)}) collective-permute-start(bf16[4,128,128]{2,1,0:T(8,128)(2,1)S(1)} %get-tuple-element.101), channel_id=1, source_target_pairs={{6,0},{7,1},{0,2},{1,3},{2,4},{3,5},{4,6},{5,7},{14,8},{15,9},{8,1... | collective-permute-start | bytes 393224 | tf_op jit(solution)/shard_map/ppermute | solution.py:22
  156.9 2.0 %collective-permute-start.12 = (bf16[4,128,128]{2,1,0:T(8,128)(2,1)S(1)}, bf16[4,128,128]{2,1,0:T(8,128)(2,1)S(1)}, u32[]{:S(2)}, u32[]{:S(2)}) collective-permute-start(bf16[4,128,128]{2,1,0:T(8,128)(2,1)S(1)} %get-tuple-element.104), channel_id=1, source_target_pairs={{3,0},{4,1},{5,2},{6,3},{7,4},{0,5},{1,6},{2,7},{11,8},{12,9},{13,... | collective-permute-start | bytes 393224 | tf_op jit(solution)/shard_map/ppermute | solution.py:22
  159.5 3.3 %shard_map.77 = (bf16[32,128,512]{2,1,0:T(8,128)(2,1)}, f32[32,128,1024]{2,1,0:T(8,128)}) custom-call(s32[32,128]{1,0:T(8,128)S(1)} %shard_map.68.plan, bf16[4,128,128]{2,1,0:T(8,128)(2,1)S(1)} %get-tuple-element.118.refs_0_, bf16[4,128,128]{2,1,0:T(8,128)(2,1)S(1)} %collective-permute-done.21.refs_1_, ...), custom_call_target="tpu_custom_call" | custom-call | flops 1073741824 | bytes 6400000 | tf_op jit(solution)/shard_map/pallas_call | solution.py:427
  162.8 5.0 %collective-permute-done.11.refs_4_ = bf16[4,128,128]{2,1,0:T(8,128)(2,1)S(1)} collective-permute-done((bf16[4,128,128]{2,1,0:T(8,128)(2,1)S(1)}, bf16[4,128,128]{2,1,0:T(8,128)(2,1)S(1)}, u32[]{:S(2)}, u32[]{:S(2)}) %collective-permute-start.11) | collective-permute-done | bytes 131104 | tf_op jit(solution)/shard_map/ppermute | solution.py:22
  169.1 3.3 %shard_map.78 = (bf16[32,128,512]{2,1,0:T(8,128)(2,1)}, f32[32,128,1024]{2,1,0:T(8,128)}) custom-call(s32[32,128]{1,0:T(8,128)S(1)} %shard_map.68.plan, bf16[4,128,128]{2,1,0:T(8,128)(2,1)S(1)} %get-tuple-element.99.refs_0_, bf16[4,128,128]{2,1,0:T(8,128)(2,1)S(1)} %collective-permute-done.8.refs_1_, ...), custom_call_target="tpu_custom_call", output_to_operand_aliasing={{0}: (10, {}), {1}: (11, {})} | custom-call | flops 1073741824 | bytes 6400000 | tf_op jit(solution)/shard_map/pallas_call | solution.py:427
  172.4 5.0 %shard_map.79 = (bf16[32,128,512]{2,1,0:T(8,128)(2,1)}, f32[32,128,1024]{2,1,0:T(8,128)}) custom-call(s32[32,128]{1,0:T(8,128)S(1)} %shard_map.68.plan, bf16[4,8,2,128,128]{4,3,2,1,0:T(8,128)(2,1)S(1)} %bitcast.2, bf16[512,1024]{1,0:T(8,128)(2,1)S(1)} %copy-done.1, ...), custom_call_target="tpu_custom_call", output_to_operand_aliasing={{0}: (3, {}), {1}: (4, {})} | custom-call | flops 2147483648 | bytes 12800000 | tf_op jit(solution)/shard_map/pallas_call | solution.py:427
  (55 shorter events, 20.5 us)
Async XLA Ops:
  3.9 26.9 %collective-permute-start.3 = (bf16[2,2064,128]{2,1,0:T(8,128)(2,1)}, bf16[2,2064,128]{2,1,0:T(8,128)(2,1)}, u32[]{:S(2)}, u32[]{:S(2)}) collective-permute-start(bf16[2,2064,128]{2,1,0:T(8,128)(2,1)} %get-tuple-element.85), channel_id=1, source_target_pairs={{7,0},{0,1},{1,2},{2,3},{3,4},{4,5},{5,6},{6,7},{15,8},{8,9},{9,10... | collective-permute-start | bytes 3170312 | tf_op jit(solution)/shard_map/ppermute | solution.py:22
  5.7 25.0 %collective-permute-start.4 = (bf16[2,2048,128]{2,1,0:T(8,128)(2,1)}, bf16[2,2048,128]{2,1,0:T(8,128)(2,1)}, u32[]{:S(2)}, u32[]{:S(2)}) collective-permute-start(bf16[2,2048,128]{2,1,0:T(8,128)(2,1)} %get-tuple-element.86), channel_id=1, source_target_pairs={{1,0},{2,1},{3,2},{4,3},{5,4},{6,5},{7,6},{0,7},{9,8},{10,9},{11,1... | collective-permute-start | bytes 3145736 | tf_op jit(solution)/shard_map/ppermute | solution.py:22
  35.5 136.9 %all-to-all-start = ((bf16[64,128,128]{2,1,0:T(8,128)(2,1)}), bf16[64,128,128]{2,1,0:T(8,128)(2,1)S(1)}, u32[]{:S(2)}, u32[]{:S(2)}) async-start(bf16[64,128,128]{2,1,0:T(8,128)(2,1)} %copy-done), calls=%async_computation | async-start | bytes 4194304 | tf_op jit(solution)/shard_map/all_to_all | solution.py:502
  42.6 71.3 %collective-permute-start.16 = (bf16[8,128,128]{2,1,0:T(8,128)(2,1)S(1)}, bf16[8,128,128]{2,1,0:T(8,128)(2,1)}, u32[]{:S(2)}, u32[]{:S(2)}) collective-permute-start(bf16[8,128,128]{2,1,0:T(8,128)(2,1)S(1)} %shard_map.75), channel_id=1, source_target_pairs={{16,0},{24,8},{0,16},{8,24},{17,1},{25,9},{1,17},{9,25},{18,2},{26... | collective-permute-start | bytes 786440 | tf_op jit(solution)/shard_map/ppermute | solution.py:22
  46.2 68.7 %collective-permute-start.15 = (bf16[8,128,128]{2,1,0:T(8,128)(2,1)}, bf16[8,128,128]{2,1,0:T(8,128)(2,1)}, u32[]{:S(2)}, u32[]{:S(2)}) collective-permute-start(bf16[8,128,128]{2,1,0:T(8,128)(2,1)} %get-tuple-element.108), channel_id=1, source_target_pairs={{24,0},{0,8},{8,16},{16,24},{25,1},{1,9},{9,17},{17,25},{26,2},{2,... | collective-permute-start | bytes 786440 | tf_op jit(solution)/shard_map/ppermute | solution.py:22
  47.5 72.1 %collective-permute-start.17 = (bf16[8,128,128]{2,1,0:T(8,128)(2,1)}, bf16[8,128,128]{2,1,0:T(8,128)(2,1)}, u32[]{:S(2)}, u32[]{:S(2)}) collective-permute-start(bf16[8,128,128]{2,1,0:T(8,128)(2,1)} %get-tuple-element.109), channel_id=1, source_target_pairs={{8,0},{16,8},{24,16},{0,24},{9,1},{17,9},{25,17},{1,25},{10,2},{18... | collective-permute-start | bytes 786440 | tf_op jit(solution)/shard_map/ppermute | solution.py:22
  52.7 90.3 %collective-permute-start.5 = (bf16[8,128,128]{2,1,0:T(8,128)(2,1)}, bf16[8,128,128]{2,1,0:T(8,128)(2,1)S(1)}, u32[]{:S(2)}, u32[]{:S(2)}) collective-permute-start(bf16[8,128,128]{2,1,0:T(8,128)(2,1)} %get-tuple-element.96), channel_id=1, source_target_pairs={{24,0},{0,8},{8,16},{16,24},{25,1},{1,9},{9,17},{17,25},{26,2},{2,... | collective-permute-start | bytes 786440 | tf_op jit(solution)/shard_map/ppermute | solution.py:22
  53.7 89.2 %collective-permute-start.6 = (bf16[8,128,128]{2,1,0:T(8,128)(2,1)}, bf16[8,128,128]{2,1,0:T(8,128)(2,1)}, u32[]{:S(2)}, u32[]{:S(2)}) collective-permute-start(bf16[8,128,128]{2,1,0:T(8,128)(2,1)} %get-tuple-element.97), channel_id=1, source_target_pairs={{16,0},{24,8},{0,16},{8,24},{17,1},{25,9},{1,17},{9,25},{18,2},{26... | collective-permute-start | bytes 786440 | tf_op jit(solution)/shard_map/ppermute | solution.py:22
  119.6 23.5 %collective-permute-start.7 = (bf16[8,128,128]{2,1,0:T(8,128)(2,1)}, bf16[8,128,128]{2,1,0:T(8,128)(2,1)S(1)}, u32[]{:S(2)}, u32[]{:S(2)}) collective-permute-start(bf16[8,128,128]{2,1,0:T(8,128)(2,1)} %get-tuple-element.98), channel_id=1, source_target_pairs={{8,0},{16,8},{24,16},{0,24},{9,1},{17,9},{25,17},{1,25},{10,2},{18... | collective-permute-start | bytes 786440 | tf_op jit(solution)/shard_map/ppermute | solution.py:22
  121.8 11.7 %collective-permute-start.18 = (bf16[1,128,128]{2,1,0:T(8,128)(2,1)S(1)}, bf16[1,128,128]{2,1,0:T(8,128)(2,1)S(1)}, u32[]{:S(2)}, u32[]{:S(2)}) collective-permute-start(bf16[1,128,128]{2,1,0:T(8,128)(2,1)S(1)} %get-tuple-element.115), channel_id=1, source_target_pairs={{24,0},{0,8},{8,16},{16,24},{25,1},{1,9},{9,17},{17,25},{26,2},{2,... | collective-permute-start | bytes 98312 | tf_op jit(solution)/shard_map/ppermute | solution.py:22
  121.8 11.7 %collective-permute-start.19 = (bf16[1,128,128]{2,1,0:T(8,128)(2,1)S(1)}, bf16[1,128,128]{2,1,0:T(8,128)(2,1)S(1)}, u32[]{:S(2)}, u32[]{:S(2)}) collective-permute-start(bf16[1,128,128]{2,1,0:T(8,128)(2,1)S(1)} %get-tuple-element.116), channel_id=1, source_target_pairs={{16,0},{24,8},{0,16},{8,24},{17,1},{25,9},{1,17},{9,25},{18,2},{26... | collective-permute-start | bytes 98312 | tf_op jit(solution)/shard_map/ppermute | solution.py:22
  137.7 9.4 %collective-permute-start.21 = (bf16[4,128,128]{2,1,0:T(8,128)(2,1)S(1)}, bf16[4,128,128]{2,1,0:T(8,128)(2,1)S(1)}, u32[]{:S(2)}, u32[]{:S(2)}) collective-permute-start(bf16[4,128,128]{2,1,0:T(8,128)(2,1)S(1)} %get-tuple-element.119), channel_id=1, source_target_pairs={{7,0},{0,1},{1,2},{2,3},{3,4},{4,5},{5,6},{6,7},{15,8},{8,9},{9,10... | collective-permute-start | bytes 393224 | tf_op jit(solution)/shard_map/ppermute | solution.py:22
  141.2 7.2 %collective-permute-start.22 = (bf16[4,128,128]{2,1,0:T(8,128)(2,1)S(1)}, bf16[4,128,128]{2,1,0:T(8,128)(2,1)S(1)}, u32[]{:S(2)}, u32[]{:S(2)}) collective-permute-start(bf16[4,128,128]{2,1,0:T(8,128)(2,1)S(1)} %get-tuple-element.120), channel_id=1, source_target_pairs={{6,0},{7,1},{0,2},{1,3},{2,4},{3,5},{4,6},{5,7},{14,8},{15,9},{8,1... | collective-permute-start | bytes 393224 | tf_op jit(solution)/shard_map/ppermute | solution.py:22
  142.9 6.5 %collective-permute-start.23 = (bf16[4,128,128]{2,1,0:T(8,128)(2,1)S(1)}, bf16[4,128,128]{2,1,0:T(8,128)(2,1)S(1)}, u32[]{:S(2)}, u32[]{:S(2)}) collective-permute-start(bf16[4,128,128]{2,1,0:T(8,128)(2,1)S(1)} %get-tuple-element.121), channel_id=1, source_target_pairs={{5,0},{6,1},{7,2},{0,3},{1,4},{2,5},{3,6},{4,7},{13,8},{14,9},{15,... | collective-permute-start | bytes 393224 | tf_op jit(solution)/shard_map/ppermute | solution.py:22
  143.0 10.5 %collective-permute-start.24 = (bf16[4,128,128]{2,1,0:T(8,128)(2,1)S(1)}, bf16[4,128,128]{2,1,0:T(8,128)(2,1)S(1)}, u32[]{:S(2)}, u32[]{:S(2)}) collective-permute-start(bf16[4,128,128]{2,1,0:T(8,128)(2,1)S(1)} %get-tuple-element.122), channel_id=1, source_target_pairs={{4,0},{5,1},{6,2},{7,3},{0,4},{1,5},{2,6},{3,7},{12,8},{13,9},{14,... | collective-permute-start | bytes 393224 | tf_op jit(solution)/shard_map/ppermute | solution.py:22
  143.2 12.5 %collective-permute-start.25 = (bf16[4,128,128]{2,1,0:T(8,128)(2,1)S(1)}, bf16[4,128,128]{2,1,0:T(8,128)(2,1)S(1)}, u32[]{:S(2)}, u32[]{:S(2)}) collective-permute-start(bf16[4,128,128]{2,1,0:T(8,128)(2,1)S(1)} %get-tuple-element.123), channel_id=1, source_target_pairs={{3,0},{4,1},{5,2},{6,3},{7,4},{0,5},{1,6},{2,7},{11,8},{12,9},{13,... | collective-permute-start | bytes 393224 | tf_op jit(solution)/shard_map/ppermute | solution.py:22
  147.1 8.6 %collective-permute-start.26 = (bf16[4,128,128]{2,1,0:T(8,128)(2,1)S(1)}, bf16[4,128,128]{2,1,0:T(8,128)(2,1)S(1)}, u32[]{:S(2)}, u32[]{:S(2)}) collective-permute-start(bf16[4,128,128]{2,1,0:T(8,128)(2,1)S(1)} %get-tuple-element.124), channel_id=1, source_target_pairs={{2,0},{3,1},{4,2},{5,3},{6,4},{7,5},{0,6},{1,7},{10,8},{11,9},{12,... | collective-permute-start | bytes 393224 | tf_op jit(solution)/shard_map/ppermute | solution.py:22
  148.5 8.4 %collective-permute-start.27 = (bf16[4,128,128]{2,1,0:T(8,128)(2,1)S(1)}, bf16[4,128,128]{2,1,0:T(8,128)(2,1)S(1)}, u32[]{:S(2)}, u32[]{:S(2)}) collective-permute-start(bf16[4,128,128]{2,1,0:T(8,128)(2,1)S(1)} %get-tuple-element.125), channel_id=1, source_target_pairs={{1,0},{2,1},{3,2},{4,3},{5,4},{6,5},{7,6},{0,7},{9,8},{10,9},{11,1... | collective-permute-start | bytes 393224 | tf_op jit(solution)/shard_map/ppermute | solution.py:22
  149.4 9.5 %collective-permute-start.8 = (bf16[4,128,128]{2,1,0:T(8,128)(2,1)S(1)}, bf16[4,128,128]{2,1,0:T(8,128)(2,1)S(1)}, u32[]{:S(2)}, u32[]{:S(2)}) collective-permute-start(bf16[4,128,128]{2,1,0:T(8,128)(2,1)S(1)} %get-tuple-element.100), channel_id=1, source_target_pairs={{7,0},{0,1},{1,2},{2,3},{3,4},{4,5},{5,6},{6,7},{15,8},{8,9},{9,10... | collective-permute-start | bytes 393224 | tf_op jit(solution)/shard_map/ppermute | solution.py:22
  155.7 7.1 %collective-permute-start.10 = (bf16[4,128,128]{2,1,0:T(8,128)(2,1)S(1)}, bf16[4,128,128]{2,1,0:T(8,128)(2,1)S(1)}, u32[]{:S(2)}, u32[]{:S(2)}) collective-permute-start(bf16[4,128,128]{2,1,0:T(8,128)(2,1)S(1)} %get-tuple-element.102), channel_id=1, source_target_pairs={{5,0},{6,1},{7,2},{0,3},{1,4},{2,5},{3,6},{4,7},{13,8},{14,9},{15,... | collective-permute-start | bytes 393224 | tf_op jit(solution)/shard_map/ppermute | solution.py:22
  155.7 12.2 %collective-permute-start.11 = (bf16[4,128,128]{2,1,0:T(8,128)(2,1)S(1)}, bf16[4,128,128]{2,1,0:T(8,128)(2,1)S(1)}, u32[]{:S(2)}, u32[]{:S(2)}) collective-permute-start(bf16[4,128,128]{2,1,0:T(8,128)(2,1)S(1)} %get-tuple-element.103), channel_id=1, source_target_pairs={{4,0},{5,1},{6,2},{7,3},{0,4},{1,5},{2,6},{3,7},{12,8},{13,9},{14,... | collective-permute-start | bytes 393224 | tf_op jit(solution)/shard_map/ppermute | solution.py:22
  156.9 12.2 %collective-permute-start.12 = (bf16[4,128,128]{2,1,0:T(8,128)(2,1)S(1)}, bf16[4,128,128]{2,1,0:T(8,128)(2,1)S(1)}, u32[]{:S(2)}, u32[]{:S(2)}) collective-permute-start(bf16[4,128,128]{2,1,0:T(8,128)(2,1)S(1)} %get-tuple-element.104), channel_id=1, source_target_pairs={{3,0},{4,1},{5,2},{6,3},{7,4},{0,5},{1,6},{2,7},{11,8},{12,9},{13,... | collective-permute-start | bytes 393224 | tf_op jit(solution)/shard_map/ppermute | solution.py:22
  158.9 10.2 %collective-permute-start.13 = (bf16[4,128,128]{2,1,0:T(8,128)(2,1)S(1)}, bf16[4,128,128]{2,1,0:T(8,128)(2,1)S(1)}, u32[]{:S(2)}, u32[]{:S(2)}) collective-permute-start(bf16[4,128,128]{2,1,0:T(8,128)(2,1)S(1)} %get-tuple-element.105), channel_id=1, source_target_pairs={{2,0},{3,1},{4,2},{5,3},{6,4},{7,5},{0,6},{1,7},{10,8},{11,9},{12,... | collective-permute-start | bytes 393224 | tf_op jit(solution)/shard_map/ppermute | solution.py:22
  159.1 10.0 %collective-permute-start.14 = (bf16[4,128,128]{2,1,0:T(8,128)(2,1)S(1)}, bf16[4,128,128]{2,1,0:T(8,128)(2,1)S(1)}, u32[]{:S(2)}, u32[]{:S(2)}) collective-permute-start(bf16[4,128,128]{2,1,0:T(8,128)(2,1)S(1)} %get-tuple-element.106), channel_id=1, source_target_pairs={{1,0},{2,1},{3,2},{4,3},{5,4},{6,5},{7,6},{0,7},{9,8},{10,9},{11,1... | collective-permute-start | bytes 393224 | tf_op jit(solution)/shard_map/ppermute | solution.py:22
  (8 other events, 44.8 us)

commit v6 on v5

--- a/solution.py
+++ b/solution.py
@@ -480,22 +480,30 @@
     if ranks:
         apart = near_half(n_data)
         whole, first = layout.stage(0), {}
-        for shifts in (apart[:1], apart[1:] + [0]):
+        for shifts in (apart[:1], apart[1:]):
             first.update(zip(shifts, pack_all([whole[s] for s in shifts], 60)))
-        stages = {0: send_z(first)}
-        rest = [layout.late() + rest[0]] + rest[1:]
-    packed = pack_all([parts for group in rest for parts in group], 50)
+        late, one = layout.late(), rest[0]
+        sent = [late[s] for s in apart] + [one[s] for s in apart]
+        rest = [sent] + rest[1:-1] + [rest[-1] + [late[0], one[0]]]
+    own = [whole[0]] if ranks else []
+    packed = pack_all([parts for group in rest for parts in group] + own, 50)
     complete, at = [], 0
     for group in rest:
         complete.append(overlay_all(group, packed[at : at + len(group)]))
         at += len(group)
     if ranks:
-        late = send_z(complete[0][:n_data])
-        for rank in ranks[1:]:
-            stages[rank] = send_z(complete[0][n_data * rank :])
+        first[0] = packed[at]
+        stages = {0: send_z(first)}
+        count = len(apart)
+        late = send_z(dict(zip(apart + [0], complete[0][:count] + complete[-1][1:2])))
+        one = dict(zip(apart + [0], complete[0][count:] + complete[-1][2:3]))
+        stages[1] = send_z(one)
+        for rank in ranks[2:]:
+            stages[rank] = send_z(complete[rank - 1])
 
         def resend(early):
-            return send_z(overlay_all(layout.stage(0), [first[s] for s in every_z]))
+            again = overlay_all(layout.stage(0), [first[s] for s in every_z])
+            return send_z(again)
 
         crowded = plan[0, per_pair + 2] > LATE
         stages[0] = lax.cond(crowded, resend, lambda early: early, stages[0])

time: 178 us -> 178 us (level)
  transfers between devices with their start and end apart: 26 -> 26, of which waited for: 9 -> 10; matrix products, arithmetic and copies ran while one was open for 0% -> 0% of each run, Pallas kernels for 14% -> 15%
where the time goes in v6:
time: 178 us
  waiting for transfers between devices  101 us (57%)
  Pallas kernels  38.2 us (21%)
  starting transfers between devices  34.8 us (20%)
  local copies, waits for them, and re-layouts  2.08 us (1%)
    ppermute x25, waiting for transfers between devices, from_behind(): return lax.ppermute(block, axis, route)  101 us
    ppermute x25, starting transfers between devices, from_behind(): return lax.ppermute(block, axis, route)  29.7 us
    pallas_call x3, Pallas kernels, pack(): pl.pallas_call(functools.partial(pack_kernel, arrays), out_shape=[jax.Sha...  12.6 us
    pallas_call x3, Pallas kernels, store_ranks(): pl.pallas_call(functools.partial(store_kernel, layout, ranks, direct, cou...  11.7 us
    pallas_call x2, Pallas kernels, overlay(): pl.pallas_call(functools.partial(overlay_kernel, arrays, layout.n_tensor)...  6.87 us
    all_to_all x1, starting transfers between devices, shards(): lax.all_to_all(complete[-1][0], ('dp', 'tensor'), split_axis=0, concat_ax...  5.17 us
  transfers between devices with their start and end apart: 26, of which 10 were waited for; matrix products, arithmetic and copies ran while one was open for 0% of the time, Pallas kernels for 15%

profile of v6, /device:TPU:19, one launch (start us, length us, event | category | flops | bytes accessed | tf_op | source)
XLA Modules:
  0.0 177.8 jit_solution(10092720538300314333)
XLA Ops:
  0.6 3.2 %shard_map.70 = (bf16[2,2048,128]{2,1,0:T(8,128)(2,1)}, bf16[2,2064,128]{2,1,0:T(8,128)(2,1)}) custom-call(s32[2,9]{1,0:T(2,128)} %offsets.13, bf16[12288,128]{1,0:T(8,128)(2,1)} %embed.7, bf16[12288,128]{1,0:T(8,128)(2,1)} %head.7), custom_call_target="tpu_custom_call" | custom-call | tf_op jit(solution)/shard_map/pallas_call | solution.py:70
  3.9 1.8 %collective-permute-start.3 = (bf16[2,2064,128]{2,1,0:T(8,128)(2,1)}, bf16[2,2064,128]{2,1,0:T(8,128)(2,1)}, u32[]{:S(2)}, u32[]{:S(2)}) collective-permute-start(bf16[2,2064,128]{2,1,0:T(8,128)(2,1)} %get-tuple-element.88), channel_id=1, source_target_pairs={{7,0},{0,1},{1,2},{2,3},{3,4},{4,5},{5,6},{6,7},{15,8},{8,9},{9,10... | collective-permute-start | bytes 3170312 | tf_op jit(solution)/shard_map/ppermute | solution.py:22
  7.0 7.7 %shard_map.69 = (bf16[1,128,128]{2,1,0:T(8,128)(2,1)S(1)}, bf16[1,128,128]{2,1,0:T(8,128)(2,1)S(1)}, bf16[1,128,128]{2,1,0:T(8,128)(2,1)S(1)}, bf16[8,128,128]{2...) custom-call(s32[32,128]{1,0:T(8,128)S(1)} %shard_map.68.plan, ...), custom_call_target="tpu_custom_call" | custom-call | flops 3240000000 | bytes 7560000 | tf_op jit(solution)/shard_map/pallas_call | solution.py:262
  14.7 16.0 %collective-permute-done.4.refs_4_.refs_7_ = bf16[2,2048,128]{2,1,0:T(8,128)(2,1)} collective-permute-done((bf16[2,2048,128]{2,1,0:T(8,128)(2,1)}, bf16[2,2048,128]{2,1,0:T(8,128)(2,1)}, u32[]{:S(2)}, u32[]{:S(2)}) %collective-permute-start.4) | collective-permute-done | bytes 1048608 | tf_op jit(solution)/shard_map/ppermute | solution.py:22
  30.8 3.7 %shard_map.71 = (bf16[64,128,128]{2,1,0:T(8,128)(2,1)S(1)}, bf16[1,128,128]{2,1,0:T(8,128)(2,1)S(1)}, bf16[8,128,128]{2,1,0:T(8,128)(2,1)S(1)}) custom-call(s32[32,128]{1,0:T(8,128)S(1)} %shard_map.68.plan, s32[2,9]{1,0:T(2,128)S(1)} %copy-done.2, bf16[64,128,128]{2,1,0:T(8,128)(2,1)S(1)} %get-tuple-element.85.refs_0_, ...), custom_call_target="tpu_custom_call" | custom-call | flops 1000000000 | bytes 4000000 | tf_op jit(solution)/shard_map/pallas_call | solution.py:324
  35.8 5.2 %all-to-all-start = ((bf16[64,128,128]{2,1,0:T(8,128)(2,1)}), bf16[64,128,128]{2,1,0:T(8,128)(2,1)S(1)}, u32[]{:S(2)}, u32[]{:S(2)}) async-start(bf16[64,128,128]{2,1,0:T(8,128)(2,1)} %copy-done.1), calls=%async_computation | async-start | bytes 4194304 | tf_op jit(solution)/shard_map/all_to_all | solution.py:510
  41.0 1.9 %shard_map.75 = bf16[8,128,128]{2,1,0:T(8,128)(2,1)S(1)} custom-call(s32[32,128]{1,0:T(8,128)S(1)} %shard_map.68.plan, s32[2,9]{1,0:T(2,128)S(1)} %copy-done.2, bf16[12288,128]{1,0:T(8,128)(2,1)} %embed.7, bf16[12288,128]{1,0:T(8,128)(2,1)} %head.7), custom_call_target="tpu_custom_call" | custom-call | flops 240000000 | bytes 560000 | tf_op jit(solution)/shard_map/pallas_call | solution.py:262
  43.2 3.0 %shard_map.74 = (bf16[8,128,128]{2,1,0:T(8,128)(2,1)}, bf16[8,128,128]{2,1,0:T(8,128)(2,1)}) custom-call(s32[32,128]{1,0:T(8,128)S(1)} %shard_map.68.plan, s32[2,9]{1,0:T(2,128)S(1)} %copy-done.2, bf16[12288,128]{1,0:T(8,128)(2,1)} %embed.7, bf16[12288,128]{1,0:T(8,128)(2,1)} %head.7), custom_call_target="tpu_custom_call" | custom-call | flops 480000000 | bytes 1120000 | tf_op jit(solution)/shard_map/pallas_call | solution.py:262
  48.5 3.2 %shard_map.72 = (bf16[1,128,128]{2,1,0:T(8,128)(2,1)S(1)}, bf16[1,128,128]{2,1,0:T(8,128)(2,1)S(1)}, bf16[1,128,128]{2,1,0:T(8,128)(2,1)S(1)}, bf16[8,128,128]{2...) custom-call(s32[32,128]{1,0:T(8,128)S(1)} %shard_map.68.plan, s32[2,9]{1,0:T(2,128)S(1)} %copy-done.2, ...), custom_call_target="tpu_custom_call" | custom-call | flops 1000000000 | bytes 4000000 | tf_op jit(solution)/shard_map/pallas_call | solution.py:324
  52.7 2.1 %collective-permute-start.6 = (bf16[8,128,128]{2,1,0:T(8,128)(2,1)}, bf16[8,128,128]{2,1,0:T(8,128)(2,1)}, u32[]{:S(2)}, u32[]{:S(2)}) collective-permute-start(bf16[8,128,128]{2,1,0:T(8,128)(2,1)} %get-tuple-element.99), channel_id=1, source_target_pairs={{16,0},{24,8},{0,16},{8,24},{17,1},{25,9},{1,17},{9,25},{18,2},{26... | collective-permute-start | bytes 786440 | tf_op jit(solution)/shard_map/ppermute | solution.py:22
  56.2 58.0 %collective-permute-done.16 = bf16[8,128,128]{2,1,0:T(8,128)(2,1)} collective-permute-done((bf16[8,128,128]{2,1,0:T(8,128)(2,1)S(1)}, bf16[8,128,128]{2,1,0:T(8,128)(2,1)}, u32[]{:S(2)}, u32[]{:S(2)}) %collective-permute-start.16) | collective-permute-done | bytes 262176 | tf_op jit(solution)/shard_map/ppermute | solution.py:22
  115.3 4.7 %collective-permute-done.17 = bf16[8,128,128]{2,1,0:T(8,128)(2,1)} collective-permute-done((bf16[8,128,128]{2,1,0:T(8,128)(2,1)}, bf16[8,128,128]{2,1,0:T(8,128)(2,1)}, u32[]{:S(2)}, u32[]{:S(2)}) %collective-permute-start.17) | collective-permute-done | bytes 262176 | tf_op jit(solution)/shard_map/ppermute | solution.py:22
  119.9 2.2 %collective-permute-start.7 = (bf16[8,128,128]{2,1,0:T(8,128)(2,1)}, bf16[8,128,128]{2,1,0:T(8,128)(2,1)S(1)}, u32[]{:S(2)}, u32[]{:S(2)}) collective-permute-start(bf16[8,128,128]{2,1,0:T(8,128)(2,1)} %get-tuple-element.100), channel_id=1, source_target_pairs={{8,0},{16,8},{24,16},{0,24},{9,1},{17,9},{25,17},{1,25},{10,2},{18... | collective-permute-start | bytes 786440 | tf_op jit(solution)/shard_map/ppermute | solution.py:22
  123.3 10.5 %collective-permute-done.18.refs_5_ = bf16[1,128,128]{2,1,0:T(8,128)(2,1)S(1)} collective-permute-done((bf16[1,128,128]{2,1,0:T(8,128)(2,1)S(1)}, bf16[1,128,128]{2,1,0:T(8,128)(2,1)S(1)}, u32[]{:S(2)}, u32[]{:S(2)}) %collective-permute-start.18) | collective-permute-done | bytes 32800 | tf_op jit(solution)/shard_map/ppermute | solution.py:22
  133.8 2.8 %collective-permute-done.20.refs_7_ = bf16[1,128,128]{2,1,0:T(8,128)(2,1)S(1)} collective-permute-done((bf16[1,128,128]{2,1,0:T(8,128)(2,1)S(1)}, bf16[1,128,128]{2,1,0:T(8,128)(2,1)S(1)}, u32[]{:S(2)}, u32[]{:S(2)}) %collective-permute-start.20) | collective-permute-done | bytes 32800 | tf_op jit(solution)/shard_map/ppermute | solution.py:22
  138.1 3.5 %collective-permute-start.21 = (bf16[4,128,128]{2,1,0:T(8,128)(2,1)S(1)}, bf16[4,128,128]{2,1,0:T(8,128)(2,1)S(1)}, u32[]{:S(2)}, u32[]{:S(2)}) collective-permute-start(bf16[4,128,128]{2,1,0:T(8,128)(2,1)S(1)} %get-tuple-element.121), channel_id=1, source_target_pairs={{7,0},{0,1},{1,2},{2,3},{3,4},{4,5},{5,6},{6,7},{15,8},{8,9},{9,10... | collective-permute-start | bytes 393224 | tf_op jit(solution)/shard_map/ppermute | solution.py:22
  143.5 2.0 %collective-permute-start.25 = (bf16[4,128,128]{2,1,0:T(8,128)(2,1)S(1)}, bf16[4,128,128]{2,1,0:T(8,128)(2,1)S(1)}, u32[]{:S(2)}, u32[]{:S(2)}) collective-permute-start(bf16[4,128,128]{2,1,0:T(8,128)(2,1)S(1)} %get-tuple-element.125), channel_id=1, source_target_pairs={{3,0},{4,1},{5,2},{6,3},{7,4},{0,5},{1,6},{2,7},{11,8},{12,9},{13,... | collective-permute-start | bytes 393224 | tf_op jit(solution)/shard_map/ppermute | solution.py:22
  149.7 4.1 %collective-permute-start.8 = (bf16[4,128,128]{2,1,0:T(8,128)(2,1)S(1)}, bf16[4,128,128]{2,1,0:T(8,128)(2,1)S(1)}, u32[]{:S(2)}, u32[]{:S(2)}) collective-permute-start(bf16[4,128,128]{2,1,0:T(8,128)(2,1)S(1)} %get-tuple-element.102), channel_id=1, source_target_pairs={{7,0},{0,1},{1,2},{2,3},{3,4},{4,5},{5,6},{6,7},{15,8},{8,9},{9,10... | collective-permute-start | bytes 393224 | tf_op jit(solution)/shard_map/ppermute | solution.py:22
  153.8 2.2 %collective-permute-start.9 = (bf16[4,128,128]{2,1,0:T(8,128)(2,1)S(1)}, bf16[4,128,128]{2,1,0:T(8,128)(2,1)S(1)}, u32[]{:S(2)}, u32[]{:S(2)}) collective-permute-start(bf16[4,128,128]{2,1,0:T(8,128)(2,1)S(1)} %get-tuple-element.103), channel_id=1, source_target_pairs={{6,0},{7,1},{0,2},{1,3},{2,4},{3,5},{4,6},{5,7},{14,8},{15,9},{8,1... | collective-permute-start | bytes 393224 | tf_op jit(solution)/shard_map/ppermute | solution.py:22
  157.2 2.0 %collective-permute-start.12 = (bf16[4,128,128]{2,1,0:T(8,128)(2,1)S(1)}, bf16[4,128,128]{2,1,0:T(8,128)(2,1)S(1)}, u32[]{:S(2)}, u32[]{:S(2)}) collective-permute-start(bf16[4,128,128]{2,1,0:T(8,128)(2,1)S(1)} %get-tuple-element.106), channel_id=1, source_target_pairs={{3,0},{4,1},{5,2},{6,3},{7,4},{0,5},{1,6},{2,7},{11,8},{12,9},{13,... | collective-permute-start | bytes 393224 | tf_op jit(solution)/shard_map/ppermute | solution.py:22
  159.8 3.3 %shard_map.77 = (bf16[32,128,512]{2,1,0:T(8,128)(2,1)}, f32[32,128,1024]{2,1,0:T(8,128)}) custom-call(s32[32,128]{1,0:T(8,128)S(1)} %shard_map.68.plan, bf16[4,128,128]{2,1,0:T(8,128)(2,1)S(1)} %get-tuple-element.120.refs_0_, bf16[4,128,128]{2,1,0:T(8,128)(2,1)S(1)} %collective-permute-done.21.refs_1_, ...), custom_call_target="tpu_custom_call" | custom-call | flops 1073741824 | bytes 6400000 | tf_op jit(solution)/shard_map/pallas_call | solution.py:427
  163.1 5.0 %collective-permute-done.11.refs_4_ = bf16[4,128,128]{2,1,0:T(8,128)(2,1)S(1)} collective-permute-done((bf16[4,128,128]{2,1,0:T(8,128)(2,1)S(1)}, bf16[4,128,128]{2,1,0:T(8,128)(2,1)S(1)}, u32[]{:S(2)}, u32[]{:S(2)}) %collective-permute-start.11) | collective-permute-done | bytes 131104 | tf_op jit(solution)/shard_map/ppermute | solution.py:22
  169.4 3.3 %shard_map.78 = (bf16[32,128,512]{2,1,0:T(8,128)(2,1)}, f32[32,128,1024]{2,1,0:T(8,128)}) custom-call(s32[32,128]{1,0:T(8,128)S(1)} %shard_map.68.plan, bf16[4,128,128]{2,1,0:T(8,128)(2,1)S(1)} %get-tuple-element.101.refs_0_, bf16[4,128,128]{2,1,0:T(8,128)(2,1)S(1)} %collective-permute-done.8.refs_1_, ...), custom_call_target="tpu_custom_call", output_to_operand_aliasing={{0}: (10, {}), {1}: (11, {})} | custom-call | flops 1073741824 | bytes 6400000 | tf_op jit(solution)/shard_map/pallas_call | solution.py:427
  172.8 5.0 %shard_map.79 = (bf16[32,128,512]{2,1,0:T(8,128)(2,1)}, f32[32,128,1024]{2,1,0:T(8,128)}) custom-call(s32[32,128]{1,0:T(8,128)S(1)} %shard_map.68.plan, bf16[4,8,2,128,128]{4,3,2,1,0:T(8,128)(2,1)S(1)} %bitcast.2, bf16[512,1024]{1,0:T(8,128)(2,1)S(1)} %copy-done, ...), custom_call_target="tpu_custom_call", output_to_operand_aliasing={{0}: (3, {}), {1}: (4, {})} | custom-call | flops 2147483648 | bytes 12800000 | tf_op jit(solution)/shard_map/pallas_call | solution.py:427
  (51 shorter events, 19.8 us)
Async XLA Ops:
  3.9 26.9 %collective-permute-start.3 = (bf16[2,2064,128]{2,1,0:T(8,128)(2,1)}, bf16[2,2064,128]{2,1,0:T(8,128)(2,1)}, u32[]{:S(2)}, u32[]{:S(2)}) collective-permute-start(bf16[2,2064,128]{2,1,0:T(8,128)(2,1)} %get-tuple-element.88), channel_id=1, source_target_pairs={{7,0},{0,1},{1,2},{2,3},{3,4},{4,5},{5,6},{6,7},{15,8},{8,9},{9,10... | collective-permute-start | bytes 3170312 | tf_op jit(solution)/shard_map/ppermute | solution.py:22
  5.7 25.0 %collective-permute-start.4 = (bf16[2,2048,128]{2,1,0:T(8,128)(2,1)}, bf16[2,2048,128]{2,1,0:T(8,128)(2,1)}, u32[]{:S(2)}, u32[]{:S(2)}) collective-permute-start(bf16[2,2048,128]{2,1,0:T(8,128)(2,1)} %get-tuple-element.89), channel_id=1, source_target_pairs={{1,0},{2,1},{3,2},{4,3},{5,4},{6,5},{7,6},{0,7},{9,8},{10,9},{11,1... | collective-permute-start | bytes 3145736 | tf_op jit(solution)/shard_map/ppermute | solution.py:22
  35.8 136.9 %all-to-all-start = ((bf16[64,128,128]{2,1,0:T(8,128)(2,1)}), bf16[64,128,128]{2,1,0:T(8,128)(2,1)S(1)}, u32[]{:S(2)}, u32[]{:S(2)}) async-start(bf16[64,128,128]{2,1,0:T(8,128)(2,1)} %copy-done.1), calls=%async_computation | async-start | bytes 4194304 | tf_op jit(solution)/shard_map/all_to_all | solution.py:510
  42.9 71.3 %collective-permute-start.16 = (bf16[8,128,128]{2,1,0:T(8,128)(2,1)S(1)}, bf16[8,128,128]{2,1,0:T(8,128)(2,1)}, u32[]{:S(2)}, u32[]{:S(2)}) collective-permute-start(bf16[8,128,128]{2,1,0:T(8,128)(2,1)S(1)} %shard_map.75), channel_id=1, source_target_pairs={{16,0},{24,8},{0,16},{8,24},{17,1},{25,9},{1,17},{9,25},{18,2},{26... | collective-permute-start | bytes 786440 | tf_op jit(solution)/shard_map/ppermute | solution.py:22
  46.2 69.1 %collective-permute-start.15 = (bf16[8,128,128]{2,1,0:T(8,128)(2,1)}, bf16[8,128,128]{2,1,0:T(8,128)(2,1)}, u32[]{:S(2)}, u32[]{:S(2)}) collective-permute-start(bf16[8,128,128]{2,1,0:T(8,128)(2,1)} %get-tuple-element.110), channel_id=1, source_target_pairs={{24,0},{0,8},{8,16},{16,24},{25,1},{1,9},{9,17},{17,25},{26,2},{2,... | collective-permute-start | bytes 786440 | tf_op jit(solution)/shard_map/ppermute | solution.py:22
  47.5 72.5 %collective-permute-start.17 = (bf16[8,128,128]{2,1,0:T(8,128)(2,1)}, bf16[8,128,128]{2,1,0:T(8,128)(2,1)}, u32[]{:S(2)}, u32[]{:S(2)}) collective-permute-start(bf16[8,128,128]{2,1,0:T(8,128)(2,1)} %get-tuple-element.111), channel_id=1, source_target_pairs={{8,0},{16,8},{24,16},{0,24},{9,1},{17,9},{25,17},{1,25},{10,2},{18... | collective-permute-start | bytes 786440 | tf_op jit(solution)/shard_map/ppermute | solution.py:22
  51.7 91.6 %collective-permute-start.5 = (bf16[8,128,128]{2,1,0:T(8,128)(2,1)}, bf16[8,128,128]{2,1,0:T(8,128)(2,1)}, u32[]{:S(2)}, u32[]{:S(2)}) collective-permute-start(bf16[8,128,128]{2,1,0:T(8,128)(2,1)} %get-tuple-element.98), channel_id=1, source_target_pairs={{24,0},{0,8},{8,16},{16,24},{25,1},{1,9},{9,17},{17,25},{26,2},{2,... | collective-permute-start | bytes 786440 | tf_op jit(solution)/shard_map/ppermute | solution.py:22
  52.7 90.5 %collective-permute-start.6 = (bf16[8,128,128]{2,1,0:T(8,128)(2,1)}, bf16[8,128,128]{2,1,0:T(8,128)(2,1)}, u32[]{:S(2)}, u32[]{:S(2)}) collective-permute-start(bf16[8,128,128]{2,1,0:T(8,128)(2,1)} %get-tuple-element.99), channel_id=1, source_target_pairs={{16,0},{24,8},{0,16},{8,24},{17,1},{25,9},{1,17},{9,25},{18,2},{26... | collective-permute-start | bytes 786440 | tf_op jit(solution)/shard_map/ppermute | solution.py:22
  119.9 23.5 %collective-permute-start.7 = (bf16[8,128,128]{2,1,0:T(8,128)(2,1)}, bf16[8,128,128]{2,1,0:T(8,128)(2,1)S(1)}, u32[]{:S(2)}, u32[]{:S(2)}) collective-permute-start(bf16[8,128,128]{2,1,0:T(8,128)(2,1)} %get-tuple-element.100), channel_id=1, source_target_pairs={{8,0},{16,8},{24,16},{0,24},{9,1},{17,9},{25,17},{1,25},{10,2},{18... | collective-permute-start | bytes 786440 | tf_op jit(solution)/shard_map/ppermute | solution.py:22
  122.1 11.7 %collective-permute-start.18 = (bf16[1,128,128]{2,1,0:T(8,128)(2,1)S(1)}, bf16[1,128,128]{2,1,0:T(8,128)(2,1)S(1)}, u32[]{:S(2)}, u32[]{:S(2)}) collective-permute-start(bf16[1,128,128]{2,1,0:T(8,128)(2,1)S(1)} %get-tuple-element.117), channel_id=1, source_target_pairs={{24,0},{0,8},{8,16},{16,24},{25,1},{1,9},{9,17},{17,25},{26,2},{2,... | collective-permute-start | bytes 98312 | tf_op jit(solution)/shard_map/ppermute | solution.py:22
  122.2 11.7 %collective-permute-start.19 = (bf16[1,128,128]{2,1,0:T(8,128)(2,1)S(1)}, bf16[1,128,128]{2,1,0:T(8,128)(2,1)S(1)}, u32[]{:S(2)}, u32[]{:S(2)}) collective-permute-start(bf16[1,128,128]{2,1,0:T(8,128)(2,1)S(1)} %get-tuple-element.118), channel_id=1, source_target_pairs={{16,0},{24,8},{0,16},{8,24},{17,1},{25,9},{1,17},{9,25},{18,2},{26... | collective-permute-start | bytes 98312 | tf_op jit(solution)/shard_map/ppermute | solution.py:22
  138.1 8.5 %collective-permute-start.21 = (bf16[4,128,128]{2,1,0:T(8,128)(2,1)S(1)}, bf16[4,128,128]{2,1,0:T(8,128)(2,1)S(1)}, u32[]{:S(2)}, u32[]{:S(2)}) collective-permute-start(bf16[4,128,128]{2,1,0:T(8,128)(2,1)S(1)} %get-tuple-element.121), channel_id=1, source_target_pairs={{7,0},{0,1},{1,2},{2,3},{3,4},{4,5},{5,6},{6,7},{15,8},{8,9},{9,10... | collective-permute-start | bytes 393224 | tf_op jit(solution)/shard_map/ppermute | solution.py:22
  141.6 6.9 %collective-permute-start.22 = (bf16[4,128,128]{2,1,0:T(8,128)(2,1)S(1)}, bf16[4,128,128]{2,1,0:T(8,128)(2,1)S(1)}, u32[]{:S(2)}, u32[]{:S(2)}) collective-permute-start(bf16[4,128,128]{2,1,0:T(8,128)(2,1)S(1)} %get-tuple-element.122), channel_id=1, source_target_pairs={{6,0},{7,1},{0,2},{1,3},{2,4},{3,5},{4,6},{5,7},{14,8},{15,9},{8,1... | collective-permute-start | bytes 393224 | tf_op jit(solution)/shard_map/ppermute | solution.py:22
  143.3 6.5 %collective-permute-start.23 = (bf16[4,128,128]{2,1,0:T(8,128)(2,1)S(1)}, bf16[4,128,128]{2,1,0:T(8,128)(2,1)S(1)}, u32[]{:S(2)}, u32[]{:S(2)}) collective-permute-start(bf16[4,128,128]{2,1,0:T(8,128)(2,1)S(1)} %get-tuple-element.123), channel_id=1, source_target_pairs={{5,0},{6,1},{7,2},{0,3},{1,4},{2,5},{3,6},{4,7},{13,8},{14,9},{15,... | collective-permute-start | bytes 393224 | tf_op jit(solution)/shard_map/ppermute | solution.py:22
  143.3 10.5 %collective-permute-start.24 = (bf16[4,128,128]{2,1,0:T(8,128)(2,1)S(1)}, bf16[4,128,128]{2,1,0:T(8,128)(2,1)S(1)}, u32[]{:S(2)}, u32[]{:S(2)}) collective-permute-start(bf16[4,128,128]{2,1,0:T(8,128)(2,1)S(1)} %get-tuple-element.124), channel_id=1, source_target_pairs={{4,0},{5,1},{6,2},{7,3},{0,4},{1,5},{2,6},{3,7},{12,8},{13,9},{14,... | collective-permute-start | bytes 393224 | tf_op jit(solution)/shard_map/ppermute | solution.py:22
  143.5 12.5 %collective-permute-start.25 = (bf16[4,128,128]{2,1,0:T(8,128)(2,1)S(1)}, bf16[4,128,128]{2,1,0:T(8,128)(2,1)S(1)}, u32[]{:S(2)}, u32[]{:S(2)}) collective-permute-start(bf16[4,128,128]{2,1,0:T(8,128)(2,1)S(1)} %get-tuple-element.125), channel_id=1, source_target_pairs={{3,0},{4,1},{5,2},{6,3},{7,4},{0,5},{1,6},{2,7},{11,8},{12,9},{13,... | collective-permute-start | bytes 393224 | tf_op jit(solution)/shard_map/ppermute | solution.py:22
  146.6 9.5 %collective-permute-start.26 = (bf16[4,128,128]{2,1,0:T(8,128)(2,1)S(1)}, bf16[4,128,128]{2,1,0:T(8,128)(2,1)S(1)}, u32[]{:S(2)}, u32[]{:S(2)}) collective-permute-start(bf16[4,128,128]{2,1,0:T(8,128)(2,1)S(1)} %get-tuple-element.126), channel_id=1, source_target_pairs={{2,0},{3,1},{4,2},{5,3},{6,4},{7,5},{0,6},{1,7},{10,8},{11,9},{12,... | collective-permute-start | bytes 393224 | tf_op jit(solution)/shard_map/ppermute | solution.py:22
  148.4 8.8 %collective-permute-start.27 = (bf16[4,128,128]{2,1,0:T(8,128)(2,1)S(1)}, bf16[4,128,128]{2,1,0:T(8,128)(2,1)S(1)}, u32[]{:S(2)}, u32[]{:S(2)}) collective-permute-start(bf16[4,128,128]{2,1,0:T(8,128)(2,1)S(1)} %get-tuple-element.127), channel_id=1, source_target_pairs={{1,0},{2,1},{3,2},{4,3},{5,4},{6,5},{7,6},{0,7},{9,8},{10,9},{11,1... | collective-permute-start | bytes 393224 | tf_op jit(solution)/shard_map/ppermute | solution.py:22
  149.7 9.5 %collective-permute-start.8 = (bf16[4,128,128]{2,1,0:T(8,128)(2,1)S(1)}, bf16[4,128,128]{2,1,0:T(8,128)(2,1)S(1)}, u32[]{:S(2)}, u32[]{:S(2)}) collective-permute-start(bf16[4,128,128]{2,1,0:T(8,128)(2,1)S(1)} %get-tuple-element.102), channel_id=1, source_target_pairs={{7,0},{0,1},{1,2},{2,3},{3,4},{4,5},{5,6},{6,7},{15,8},{8,9},{9,10... | collective-permute-start | bytes 393224 | tf_op jit(solution)/shard_map/ppermute | solution.py:22
  156.0 7.1 %collective-permute-start.10 = (bf16[4,128,128]{2,1,0:T(8,128)(2,1)S(1)}, bf16[4,128,128]{2,1,0:T(8,128)(2,1)S(1)}, u32[]{:S(2)}, u32[]{:S(2)}) collective-permute-start(bf16[4,128,128]{2,1,0:T(8,128)(2,1)S(1)} %get-tuple-element.104), channel_id=1, source_target_pairs={{5,0},{6,1},{7,2},{0,3},{1,4},{2,5},{3,6},{4,7},{13,8},{14,9},{15,... | collective-permute-start | bytes 393224 | tf_op jit(solution)/shard_map/ppermute | solution.py:22
  156.0 12.2 %collective-permute-start.11 = (bf16[4,128,128]{2,1,0:T(8,128)(2,1)S(1)}, bf16[4,128,128]{2,1,0:T(8,128)(2,1)S(1)}, u32[]{:S(2)}, u32[]{:S(2)}) collective-permute-start(bf16[4,128,128]{2,1,0:T(8,128)(2,1)S(1)} %get-tuple-element.105), channel_id=1, source_target_pairs={{4,0},{5,1},{6,2},{7,3},{0,4},{1,5},{2,6},{3,7},{12,8},{13,9},{14,... | collective-permute-start | bytes 393224 | tf_op jit(solution)/shard_map/ppermute | solution.py:22
  157.2 12.2 %collective-permute-start.12 = (bf16[4,128,128]{2,1,0:T(8,128)(2,1)S(1)}, bf16[4,128,128]{2,1,0:T(8,128)(2,1)S(1)}, u32[]{:S(2)}, u32[]{:S(2)}) collective-permute-start(bf16[4,128,128]{2,1,0:T(8,128)(2,1)S(1)} %get-tuple-element.106), channel_id=1, source_target_pairs={{3,0},{4,1},{5,2},{6,3},{7,4},{0,5},{1,6},{2,7},{11,8},{12,9},{13,... | collective-permute-start | bytes 393224 | tf_op jit(solution)/shard_map/ppermute | solution.py:22
  159.3 10.2 %collective-permute-start.13 = (bf16[4,128,128]{2,1,0:T(8,128)(2,1)S(1)}, bf16[4,128,128]{2,1,0:T(8,128)(2,1)S(1)}, u32[]{:S(2)}, u32[]{:S(2)}) collective-permute-start(bf16[4,128,128]{2,1,0:T(8,128)(2,1)S(1)} %get-tuple-element.107), channel_id=1, source_target_pairs={{2,0},{3,1},{4,2},{5,3},{6,4},{7,5},{0,6},{1,7},{10,8},{11,9},{12,... | collective-permute-start | bytes 393224 | tf_op jit(solution)/shard_map/ppermute | solution.py:22
  159.4 10.0 %collective-permute-start.14 = (bf16[4,128,128]{2,1,0:T(8,128)(2,1)S(1)}, bf16[4,128,128]{2,1,0:T(8,128)(2,1)S(1)}, u32[]{:S(2)}, u32[]{:S(2)}) collective-permute-start(bf16[4,128,128]{2,1,0:T(8,128)(2,1)S(1)} %get-tuple-element.108), channel_id=1, source_target_pairs={{1,0},{2,1},{3,2},{4,3},{5,4},{6,5},{7,6},{0,7},{9,8},{10,9},{11,1... | collective-permute-start | bytes 393224 | tf_op jit(solution)/shard_map/ppermute | solution.py:22
  (6 other events, 43.2 us)
